TPU v7x, 8 devices: a whole 2x2x1 slice. The times are simulated.
8 devices in a mesh: fsdp: 2 (over z, y), model: 4 (over x, core).
Axes of the slice: x: 2, y: 2, z: 1, core: 2. Of those that a mesh axis runs over, the one named last changes fastest.
Arguments:
- x_in: bfloat16 [16, 1024, 2048], P('fsdp', 'model')
- gain_attn: float32 [2, 2048], replicated
- gain_mlp: float32 [2, 2048], replicated
- rope_cos: float32 [1024, 32], replicated
- rope_sin: float32 [1024, 32], replicated
- w_q: bfloat16 [2, 2048, 2048], P(None, 'fsdp', 'model')
- w_k: bfloat16 [2, 2048, 512], P(None, 'fsdp', 'model')
- w_v: bfloat16 [2, 2048, 512], P(None, 'fsdp', 'model')
- w_o: bfloat16 [2, 2048, 2048], P(None, 'model', 'fsdp')
- w_gate: bfloat16 [2, 2048, 8192], P(None, 'fsdp', 'model')
- w_up: bfloat16 [2, 2048, 8192], P(None, 'fsdp', 'model')
- w_down: bfloat16 [2, 8192, 2048], P(None, 'model', 'fsdp')
Outputs:
- output: bfloat16 [16, 1024, 2048], P('fsdp', 'model')
All inputs are finite; a program needn't handle non-finite values.
Results may differ from a plain program's by a relative error of at most 0.02.
Values are sent between devices in bfloat16 or wider.
A program may use at most 1 GiB of HBM per device.

v0:
```python
import jax
import jax.numpy as jnp
from jax import lax
from jax.sharding import PartitionSpec as P

EPS = 1e-5


def rms_norm(seq_rows, gain_vec):
    rows_f = seq_rows.astype(jnp.float32)
    mean_sq = jnp.mean(rows_f * rows_f, axis=-1, keepdims=True)
    return (rows_f * lax.rsqrt(mean_sq + EPS) * gain_vec).astype(jnp.bfloat16)


def rotate(head_vals, cos_b, sin_b):
    half_dim = head_vals.shape[-1] // 2
    heads_f = head_vals.astype(jnp.float32)
    first_half = heads_f[..., :half_dim]
    second_half = heads_f[..., half_dim:]
    return jnp.concatenate([first_half * cos_b - second_half * sin_b, second_half * cos_b + first_half * sin_b], axis=-1).astype(jnp.bfloat16)


def attend(q_proj, k_proj, v_proj, rope_cos, rope_sin, kv_count):
    batch_rows, seq_len, q_width = q_proj.shape
    head_dim = 2 * rope_cos.shape[1]
    group_size = q_width // (head_dim * kv_count)
    q_rot = rotate(q_proj.reshape(batch_rows, seq_len, kv_count, group_size, head_dim), rope_cos[None, :, None, None, :], rope_sin[None, :, None, None, :])
    k_rot = rotate(k_proj.reshape(batch_rows, seq_len, kv_count, head_dim), rope_cos[None, :, None, :], rope_sin[None, :, None, :])
    v_heads = v_proj.reshape(batch_rows, seq_len, kv_count, head_dim)
    scores = jnp.einsum('bqkgd,bskd->bkgqs', q_rot, k_rot, preferred_element_type=jnp.float32) * head_dim ** -0.5
    positions = jnp.arange(seq_len)
    causal = positions[:, None] >= positions[None, :]
    scores = jnp.where(causal, scores, -jnp.inf)
    attn_probs = jax.nn.softmax(scores, axis=-1).astype(jnp.bfloat16)
    attn_out = jnp.einsum('bkgqs,bskd->bqkgd', attn_probs, v_heads, preferred_element_type=jnp.float32).astype(jnp.bfloat16)
    return attn_out.reshape(batch_rows, seq_len, q_width)


def solution(mesh):
    act_spec = P('fsdp', 'model', None)
    col_spec = P(None, 'fsdp', 'model')
    row_spec = P(None, 'model', 'fsdp')

    def device_step(x_in, gain_attn, gain_mlp, rope_cos, rope_sin, w_q, w_k, w_v, w_o, w_gate, w_up, w_down):
        head_dim = 2 * rope_cos.shape[1]
        kv_local = w_k.shape[-1] // head_dim
        residual = x_in
        for layer_idx in range(w_q.shape[0]):
            wq_full = lax.all_gather(w_q[layer_idx], 'fsdp', axis=0, tiled=True)
            wk_full = lax.all_gather(w_k[layer_idx], 'fsdp', axis=0, tiled=True)
            wv_full = lax.all_gather(w_v[layer_idx], 'fsdp', axis=0, tiled=True)
            wo_full = lax.all_gather(w_o[layer_idx], 'fsdp', axis=1, tiled=True)
            normed = rms_norm(residual, gain_attn[layer_idx])
            normed_all = lax.all_gather(normed, 'model', axis=1, tiled=True)
            q_proj = jnp.einsum('bsd,dn->bsn', normed_all, wq_full, preferred_element_type=jnp.float32).astype(jnp.bfloat16)
            k_proj = jnp.einsum('bsd,dn->bsn', normed_all, wk_full, preferred_element_type=jnp.float32).astype(jnp.bfloat16)
            v_proj = jnp.einsum('bsd,dn->bsn', normed_all, wv_full, preferred_element_type=jnp.float32).astype(jnp.bfloat16)
            attn_out = attend(q_proj, k_proj, v_proj, rope_cos, rope_sin, kv_local)
            attn_part = jnp.einsum('bsn,nd->bsd', attn_out, wo_full, preferred_element_type=jnp.float32)
            attn_sum = lax.psum_scatter(attn_part, 'model', scatter_dimension=1, tiled=True)
            mid_rows = (residual.astype(jnp.float32) + attn_sum).astype(jnp.bfloat16)
            wg_full = lax.all_gather(w_gate[layer_idx], 'fsdp', axis=0, tiled=True)
            wu_full = lax.all_gather(w_up[layer_idx], 'fsdp', axis=0, tiled=True)
            wd_full = lax.all_gather(w_down[layer_idx], 'fsdp', axis=1, tiled=True)
            normed_mlp = rms_norm(mid_rows, gain_mlp[layer_idx])
            mlp_in = lax.all_gather(normed_mlp, 'model', axis=1, tiled=True)
            gate_acc = jnp.einsum('bsd,df->bsf', mlp_in, wg_full, preferred_element_type=jnp.float32)
            up_acc = jnp.einsum('bsd,df->bsf', mlp_in, wu_full, preferred_element_type=jnp.float32)
            hidden = (jax.nn.silu(gate_acc) * up_acc).astype(jnp.bfloat16)
            mlp_part = jnp.einsum('bsf,fd->bsd', hidden, wd_full, preferred_element_type=jnp.float32)
            mlp_sum = lax.psum_scatter(mlp_part, 'model', scatter_dimension=1, tiled=True)
            residual = (mid_rows.astype(jnp.float32) + mlp_sum).astype(jnp.bfloat16)
        return residual

    return jax.shard_map(device_step, mesh=mesh, in_specs=(act_spec, P(), P(), P(), P(), col_spec, col_spec, col_spec, row_spec, col_spec, col_spec, row_spec), out_specs=act_spec, check_vma=False)
```

profile of v0, /device:TPU:0, one launch (start us, length us, event | category | flops | bytes accessed | tf_op | source)
XLA Modules:
  0.0 4071.9 jit_solution(12010449651998476064)
XLA Ops:
  57.9 192.4 %all-gather.29.cloned.1.call-done = bf16[8,1024,2048]{2,1,0:T(8,128)(2,1)} async-done(((bf16[8,256,2048]{2,1,0:T(8,128)(2,1)}), bf16[8,1024,2048]{2,1,0:T(8,128)(2,1)}) %all-gather.29.cloned.1.call-update) | async-done | bytes 33554448 | tf_op jit(solution)/shard_map/all_gather | solution.py:54
  250.3 26.4 convolution_convert_fusion.1
  288.0 21.6 convolution_convert_fusion.4
  320.4 110.2 %fusion.86 = (f32[8,2,4,1024]{3,2,1,0:T(4,128)S(1)}, f32[8,2,4,1024,1024]{3,4,2,1,0:T(8,128)}) fusion(pred[1024,1024]{0,1:T(8,128)(4,1)S(1)} %iota_compare_fusion, bf16[8,1024,2,4,32]{1,4,3,2,0:T(8,128)(2,1)} %get-tuple-element.14, bf16[8,1024,2,4,32]{1,4,3,2,0:T(8,128)(2,1)} %get-tuple-element.13, bf16[8,1024,2,32]{1,3,2,0:T(8,128)(2,1)S(1)} %get-tuple-element.24, ...), kind=kOutput, calls=%fused_computation.118 | convolution fusion | flops 8879342592 | bytes 280231936 | tf_op jit(solution)/shard_map/sub | solution.py:34
  430.6 21.7 convolution_convert_fusion.5
  452.3 83.1 %fusion.47 = bf16[8,2,64,4,1024]{4,2,3,1,0:T(8,128)(2,1)} fusion(bf16[8,1024,2,64,1]{1,3,4,2,0:T(8,128)(2,1)S(1)} %bitcast.167, f32[8,2,4,1024,1024]{3,4,2,1,0:T(8,128)} %get-tuple-element.38, f32[8,2,4,1024]{3,2,1,0:T(4,128)S(1)} %get-tuple-element.37), kind=kOutput, calls=%fused_computation.69 | convolution fusion | flops 8728346624 | bytes 279183360 | tf_op jit(solution)/shard_map/bkgqs,bskd->bqkgd/dot_general | solution.py:35
  535.4 29.7 fusion.53
  571.9 433.9 %reduce-scatter.5.cloned.1.call-done = f32[8,256,2048]{2,1,0:T(8,128)} async-done(((f32[8,1024,2048]{2,1,0:T(8,128)}), f32[8,256,2048]{2,1,0:T(8,128)}) %reduce-scatter.5.cloned.1.call-update) | async-done | bytes 16777232 | tf_op jit(solution)/shard_map/reduce_scatter | solution.py:60
  1038.7 70.7 %all-gather.43.cloned.1.call-done = bf16[1,2048,2048]{2,1,0:T(8,128)(2,1)} async-done(((bf16[1,1024,2048]{2,1,0:T(8,128)(2,1)}), bf16[1,2048,2048]{2,1,0:T(8,128)(2,1)}) %all-gather.43.cloned.1.call-update) | async-done | bytes 8388624 | tf_op jit(solution)/shard_map/all_gather | solution.py:63
  1109.5 200.8 %all-gather.31.cloned.1.call-done = bf16[8,1024,2048]{2,1,0:T(8,128)(2,1)} async-done(((bf16[8,256,2048]{2,1,0:T(8,128)(2,1)}), bf16[8,1024,2048]{2,1,0:T(8,128)(2,1)}) %all-gather.31.cloned.1.call-update) | async-done | bytes 33554448 | tf_op jit(solution)/shard_map/all_gather | solution.py:66
  1310.2 78.7 %fusion.42 = f32[8,1024,2048]{2,1,0:T(8,128)} fusion(bf16[8,1024,2048]{2,1,0:T(8,128)(2,1)} %all-gather.31.cloned.1.call-done, bf16[1,2048,2048]{2,1,0:T(8,128)(2,1)} %all-gather.43.cloned.1.call-done), kind=kOutput, calls=%fused_computation.61 | convolution fusion | flops 68719476736 | bytes 109051904 | tf_op jit(solution)/shard_map/bsd,df->bsf/dot_general | solution.py:68
  1389.0 25.1 all-gather.41.cloned.1.call-done
  1414.1 85.5 %multiply_convert_fusion.1.clone.2 = bf16[8,1024,2048]{2,1,0:T(8,128)(2,1)} fusion(f32[8,1024,2048]{2,1,0:T(8,128)} %fusion.42, bf16[8,1024,2048]{2,1,0:T(8,128)(2,1)} %all-gather.31.cloned.1.call-done, bf16[1,2048,2048]{2,1,0:T(8,128)(2,1)} %all-gather.41.cloned.1.call-done), kind=kOutput, calls=%fused_computation.19.clone.clone.clone | convolution fusion | flops 68820140032 | bytes 142606336 | tf_op jit(solution)/shard_map/bsd,df->bsf/dot_general | solution.py:67
  1499.6 18.3 all-gather.45.cloned.1.call-done
  1517.9 78.7 %fusion.13 = f32[8,1024,2048]{2,1,0:T(8,128)} fusion(bf16[1,2048,2048]{2,1,0:T(8,128)(2,1)} %all-gather.45.cloned.1.call-done, bf16[8,1024,2048]{2,1,0:T(8,128)(2,1)} %multiply_convert_fusion.1.clone.2), kind=kOutput, calls=%fused_computation.21 | convolution fusion | flops 68719476736 | bytes 109051904 | tf_op jit(solution)/shard_map/bsf,fd->bsd/dot_general | solution.py:70
  1599.2 438.1 %reduce-scatter.7.cloned.1.call-done = f32[8,256,2048]{2,1,0:T(8,128)} async-done(((f32[8,1024,2048]{2,1,0:T(8,128)}), f32[8,256,2048]{2,1,0:T(8,128)}) %reduce-scatter.7.cloned.1.call-update) | async-done | bytes 16777232 | tf_op jit(solution)/shard_map/reduce_scatter | solution.py:71
  2081.9 193.4 %all-gather.33.cloned.1.call-done = bf16[8,1024,2048]{2,1,0:T(8,128)(2,1)} async-done(((bf16[8,256,2048]{2,1,0:T(8,128)(2,1)}), bf16[8,1024,2048]{2,1,0:T(8,128)(2,1)}) %all-gather.33.cloned.1.call-update) | async-done | bytes 33554448 | tf_op jit(solution)/shard_map/all_gather | solution.py:54
  2275.4 26.4 convolution_convert_fusion
  2323.0 21.6 convolution_convert_fusion.2
  2345.8 100.1 %fusion.87 = (f32[8,2,4,1024]{3,2,1,0:T(4,128)S(1)}, f32[8,2,4,1024,1024]{3,4,2,1,0:T(8,128)}) fusion(pred[1024,1024]{0,1:T(8,128)(4,1)S(1)} %copy-done.7, bf16[8,1024,2,4,32]{1,4,3,2,0:T(8,128)(2,1)} %get-tuple-element.12, bf16[8,1024,2,4,32]{1,4,3,2,0:T(8,128)(2,1)} %get-tuple-element.11, bf16[8,1024,2,32]{1,3,2,0:T(8,128)(2,1)S(1)} %get-tuple-element.22, ...), kind=kOutput, calls=%fused_computation.119 | convolution fusion | flops 8879342592 | bytes 280231936 | tf_op jit(solution)/shard_map/sub | solution.py:34
  2446.0 21.7 convolution_convert_fusion.3
  2467.6 83.1 %fusion.46 = bf16[8,2,64,4,1024]{4,2,3,1,0:T(8,128)(2,1)} fusion(bf16[8,1024,2,64,1]{1,3,4,2,0:T(8,128)(2,1)S(1)} %bitcast.168, f32[8,2,4,1024,1024]{3,4,2,1,0:T(8,128)} %get-tuple-element.40, f32[8,2,4,1024]{3,2,1,0:T(4,128)S(1)} %get-tuple-element.39), kind=kOutput, calls=%fused_computation.68 | convolution fusion | flops 8728346624 | bytes 279183360 | tf_op jit(solution)/shard_map/bkgqs,bskd->bqkgd/dot_general | solution.py:35
  2550.8 29.7 fusion.50
  2581.1 440.1 %reduce-scatter.9.cloned.1.call-done = f32[8,256,2048]{2,1,0:T(8,128)} async-done(((f32[8,1024,2048]{2,1,0:T(8,128)}), f32[8,256,2048]{2,1,0:T(8,128)}) %reduce-scatter.9.cloned.1.call-update) | async-done | bytes 16777232 | tf_op jit(solution)/shard_map/reduce_scatter | solution.py:60
  3043.0 81.8 %all-gather.53.cloned.1.call-done = bf16[1,2048,2048]{2,1,0:T(8,128)(2,1)} async-done(((bf16[1,1024,2048]{2,1,0:T(8,128)(2,1)}), bf16[1,2048,2048]{2,1,0:T(8,128)(2,1)}) %all-gather.53.cloned.1.call-update) | async-done | bytes 8388624 | tf_op jit(solution)/shard_map/all_gather | solution.py:63
  3124.9 200.8 %all-gather.35.cloned.1.call-done = bf16[8,1024,2048]{2,1,0:T(8,128)(2,1)} async-done(((bf16[8,256,2048]{2,1,0:T(8,128)(2,1)}), bf16[8,1024,2048]{2,1,0:T(8,128)(2,1)}) %all-gather.35.cloned.1.call-update) | async-done | bytes 33554448 | tf_op jit(solution)/shard_map/all_gather | solution.py:66
  3325.6 78.7 %fusion.37 = f32[8,1024,2048]{2,1,0:T(8,128)} fusion(bf16[8,1024,2048]{2,1,0:T(8,128)(2,1)} %all-gather.35.cloned.1.call-done, bf16[1,2048,2048]{2,1,0:T(8,128)(2,1)} %all-gather.53.cloned.1.call-done), kind=kOutput, calls=%fused_computation.57 | convolution fusion | flops 68719476736 | bytes 109051904 | tf_op jit(solution)/shard_map/bsd,df->bsf/dot_general | solution.py:68
  3404.4 24.9 all-gather.51.cloned.1.call-done
  3429.3 85.4 %multiply_convert_fusion.clone.4 = bf16[8,1024,2048]{2,1,0:T(8,128)(2,1)} fusion(f32[8,1024,2048]{2,1,0:T(8,128)} %fusion.37, bf16[8,1024,2048]{2,1,0:T(8,128)(2,1)} %all-gather.35.cloned.1.call-done, bf16[1,2048,2048]{2,1,0:T(8,128)(2,1)} %all-gather.51.cloned.1.call-done), kind=kOutput, calls=%fused_computation.18.clone.clone.clone.1 | convolution fusion | flops 68820140032 | bytes 142606336 | tf_op jit(solution)/shard_map/bsd,df->bsf/dot_general | solution.py:67
  3514.7 18.3 all-gather.55.cloned.1.call-done
  3533.0 78.8 %fusion.12 = f32[8,1024,2048]{2,1,0:T(8,128)} fusion(bf16[1,2048,2048]{2,1,0:T(8,128)(2,1)} %all-gather.55.cloned.1.call-done, bf16[8,1024,2048]{2,1,0:T(8,128)(2,1)} %multiply_convert_fusion.clone.4), kind=kOutput, calls=%fused_computation.20 | convolution fusion | flops 68719476736 | bytes 109051904 | tf_op jit(solution)/shard_map/bsf,fd->bsd/dot_general | solution.py:70
  3611.8 440.7 %reduce-scatter.11.cloned.1.call-done = f32[8,256,2048]{2,1,0:T(8,128)} async-done(((f32[8,1024,2048]{2,1,0:T(8,128)}), f32[8,256,2048]{2,1,0:T(8,128)}) %reduce-scatter.11.cloned.1.call-update) | async-done | bytes 16777232 | tf_op jit(solution)/shard_map/reduce_scatter | solution.py:71
  (109 shorter events, 217.0 us)
Async XLA Ops:
  6.5 9.2 copy-start.12
  6.5 51.4 %all-gather.37.cloned.1.call-start = ((), (), s32[]{:S(2)}) async-start(), calls=%async_computation.12 | async-start | bytes 3145728 | tf_op jit(solution)/shard_map/all_gather | solution.py:49
  10.6 239.7 %all-gather.29.cloned.1.call-start = ((), (), s32[]{:S(2)}) async-start(), calls=%async_computation.4 | async-start | bytes 41943040 | tf_op jit(solution)/shard_map/all_gather | solution.py:54
  25.1 1.6 copy-start.5
  25.2 510.2 %all-gather.39.cloned.1.call-start = ((), (), s32[]{:S(2)}) async-start(), calls=%async_computation.13 | async-start | bytes 3145728 | tf_op jit(solution)/shard_map/all_gather | solution.py:52
  28.3 977.5 %reduce-scatter.5.cloned.1.call-start = ((), (), s32[]{:S(2)}) async-start(), calls=%async_computation.5 | async-start | bytes 83886080 | tf_op jit(solution)/shard_map/reduce_scatter | solution.py:60
  28.7 291.7 %copy-start.6 = (pred[1024,1024]{0,1:T(8,128)(4,1)}, pred[1024,1024]{0,1:T(8,128)(4,1)S(1)}, u32[]{:S(2)}) copy-start(pred[1024,1024]{0,1:T(8,128)(4,1)S(1)} %iota_compare_fusion) | copy-start | bytes 3145732
  288.0 22.1 copy-start.1
  288.0 22.1 copy-start.3
  565.1 6.2 copy-start.13
  565.1 544.4 %all-gather.43.cloned.1.call-start = ((), (), s32[]{:S(2)}) async-start(), calls=%async_computation.15 | async-start | bytes 12582912 | tf_op jit(solution)/shard_map/all_gather | solution.py:63
  571.2 739.0 %all-gather.31.cloned.1.call-start = ((), (), s32[]{:S(2)}) async-start(), calls=%async_computation.6 | async-start | bytes 41943040 | tf_op jit(solution)/shard_map/all_gather | solution.py:66
  1026.4 387.6 %all-gather.41.cloned.1.call-start = ((), (), s32[]{:S(2)}) async-start(), calls=%async_computation.14 | async-start | bytes 12582912 | tf_op jit(solution)/shard_map/all_gather | solution.py:62
  1032.7 485.2 %all-gather.45.cloned.1.call-start = ((), (), s32[]{:S(2)}) async-start(), calls=%async_computation.16 | async-start | bytes 12582912 | tf_op jit(solution)/shard_map/all_gather | solution.py:64
  1038.7 998.6 %reduce-scatter.7.cloned.1.call-start = ((), (), s32[]{:S(2)}) async-start(), calls=%async_computation.7 | async-start | bytes 83886080 | tf_op jit(solution)/shard_map/reduce_scatter | solution.py:71
  1596.5 1.2 copy-start
  1596.5 485.4 %all-gather.47.cloned.1.call-start = ((), (), s32[]{:S(2)}) async-start(), calls=%async_computation.17 | async-start | bytes 3145728 | tf_op jit(solution)/shard_map/all_gather | solution.py:49
  1599.2 450.1 %copy-start.11 = (f32[1,2048]{1,0:T(1,128)S(1)}, f32[1,2048]{1,0:T(1,128)}, u32[]{:S(2)}) copy-start(f32[1,2048]{1,0:T(1,128)} %get-tuple-element.35) | copy-start | bytes 24580
  1599.2 676.2 %all-gather.33.cloned.1.call-start = ((), (), s32[]{:S(2)}) async-start(), calls=%async_computation.8 | async-start | bytes 41943040 | tf_op jit(solution)/shard_map/all_gather | solution.py:54
  2057.9 1.0 copy-start.8
  2057.9 16.0 copy-start.9
  2058.0 492.8 %all-gather.49.cloned.1.call-start = ((), (), s32[]{:S(2)}) async-start(), calls=%async_computation.18 | async-start | bytes 3145728 | tf_op jit(solution)/shard_map/all_gather | solution.py:52
  2058.5 962.7 %reduce-scatter.9.cloned.1.call-start = ((), (), s32[]{:S(2)}) async-start(), calls=%async_computation.9 | async-start | bytes 83886080 | tf_op jit(solution)/shard_map/reduce_scatter | solution.py:60
  2301.8 11.4 copy-start.2
  2301.8 11.4 copy-start.4
  2344.6 1.2 copy-start.7
  2580.5 544.4 %all-gather.53.cloned.1.call-start = ((), (), s32[]{:S(2)}) async-start(), calls=%async_computation.20 | async-start | bytes 12582912 | tf_op jit(solution)/shard_map/all_gather | solution.py:63
  2581.0 452.2 %copy-start.10 = (f32[1,2048]{1,0:T(1,128)S(1)}, f32[1,2048]{1,0:T(1,128)}, u32[]{:S(2)}) copy-start(f32[1,2048]{1,0:T(1,128)} %get-tuple-element.33) | copy-start | bytes 24580
  2581.1 744.6 %all-gather.35.cloned.1.call-start = ((), (), s32[]{:S(2)}) async-start(), calls=%async_computation.10 | async-start | bytes 41943040 | tf_op jit(solution)/shard_map/all_gather | solution.py:66
  3041.8 387.5 %all-gather.51.cloned.1.call-start = ((), (), s32[]{:S(2)}) async-start(), calls=%async_computation.19 | async-start | bytes 12582912 | tf_op jit(solution)/shard_map/all_gather | solution.py:62
  3042.4 490.6 %all-gather.55.cloned.1.call-start = ((), (), s32[]{:S(2)}) async-start(), calls=%async_computation.21 | async-start | bytes 12582912 | tf_op jit(solution)/shard_map/all_gather | solution.py:64
  3043.0 1009.6 %reduce-scatter.11.cloned.1.call-start = ((), (), s32[]{:S(2)}) async-start(), calls=%async_computation.11 | async-start | bytes 83886080 | tf_op jit(solution)/shard_map/reduce_scatter | solution.py:71
Sparse Core Ops, SparseCore 0:
  10.7 38.5 all-gather.36
  50.9 199.3 all-gather.28
  251.8 30.1 all-gather.38
  565.2 440.5 reduce-scatter.4
  1007.2 102.2 all-gather.42
  1110.9 199.3 all-gather.30
  1311.7 102.2 all-gather.40
  1415.6 102.2 all-gather.44
  1596.7 440.5 reduce-scatter.6
  2038.6 35.7 all-gather.46
  2076.0 199.3 all-gather.32
  2276.7 30.1 all-gather.48
  2580.6 440.5 reduce-scatter.8
  3022.6 102.2 all-gather.52
  3126.3 199.3 all-gather.34
  3327.0 102.2 all-gather.50
  3430.7 102.2 all-gather.54
  3611.9 440.5 reduce-scatter.10
where the time goes:
time: 4080 us; the launch traced here: 4070 us
  waiting for transfers between devices  2780 us (68%)
  matrix products  1060 us (26%)
  other arithmetic  132 us (3%)
  blocking collectives  47.7 us (1%)
    reduce_scatter x2, waiting for transfers between devices, device_step(): lax.psum_scatter(mlp_part, 'model', scatter_dimension=1, tiled=True)  879 us
    reduce_scatter x2, waiting for transfers between devices, device_step(): lax.psum_scatter(attn_part, 'model', scatter_dimension=1, tiled=True)  874 us
    all_gather x2, waiting for transfers between devices, device_step(): mlp_in = lax.all_gather(normed_mlp, 'model', axis=1, tiled=True)  402 us
    all_gather x2, waiting for transfers between devices, device_step(): normed_all = lax.all_gather(normed, 'model', axis=1, tiled=True)  386 us
    sub x2, matrix products, attend(): attn_probs = jax.nn.softmax(scores, axis=-1).astype(jnp.bfloat16)  210 us
    dot_general x2, matrix products, device_step(): jnp.einsum('bsd,df->bsf', mlp_in, wg_full, preferred_element_type=jnp.flo...  171 us
    dot_general x2, matrix products, attend(): jnp.einsum('bkgqs,bskd->bqkgd', attn_probs, v_heads, preferred_element_ty...  166 us
    dot_general x2, matrix products, device_step(): jnp.einsum('bsd,df->bsf', mlp_in, wu_full, preferred_element_type=jnp.flo...  157 us
  transfers between devices with their start and end apart: 18, of which 14 were waited for; matrix products, arithmetic and copies ran while one was open for 24% of the time, Pallas kernels for 0%

commit v1 on v0

v1 whole, which is shorter than its diff:
```python
import functools
import math

import jax
import jax.numpy as jnp
from jax import lax
from jax.experimental import pallas as pl
from jax.experimental.pallas import tpu as pltpu
from jax.sharding import PartitionSpec as P


EPS = 1e-5
VMEM = 60 * 1024 * 1024
F32 = jnp.float32
BF16 = jnp.bfloat16


def dot(a, b):
    return jnp.dot(a, b, preferred_element_type=F32)


def params():
    return pltpu.CompilerParams(dimension_semantics=("arbitrary",), vmem_limit_bytes=VMEM)


def normalise(x_ref, gain_ref, h_ref, chunk):
    def step(i, carry):
        rows = pl.ds(pl.multiple_of(i * chunk, chunk), chunk)
        x = x_ref[rows, :].astype(F32)
        mean_sq = jnp.mean(x * x, axis=-1, keepdims=True)
        h_ref[rows, :] = (x * lax.rsqrt(mean_sq + EPS) * gain_ref[...]).astype(BF16)
        return carry

    lax.fori_loop(0, x_ref.shape[0] // chunk, step, 0)


def rotate(x, cos, sin):
    lane = lax.broadcasted_iota(jnp.int32, x.shape, 1)
    swapped = jnp.where(lane % 64 < 32, pltpu.roll(x, 96, 1), pltpu.roll(x, 32, 1))
    return x * cos + swapped * sin


def qkv_kernel(x_ref, gain_ref, cos_ref, sin_ref, w_ref, q_ref, k_ref, v_ref, h_ref):
    @pl.when(pl.program_id(0) == 0)
    def _():
        normalise(x_ref, gain_ref, h_ref, 128)

    w = w_ref[...].reshape(w_ref.shape[0] * w_ref.shape[2], w_ref.shape[3])
    q_width, k_width = q_ref.shape[1], k_ref.shape[1]
    positions = 256
    rows_step = 2 * positions

    def step(i, carry):
        rows = pl.ds(pl.multiple_of(i * rows_step, rows_step), rows_step)
        out = dot(h_ref[rows, :], w).astype(BF16)
        table = pl.ds(pl.multiple_of(i * positions, positions), positions)
        cos, sin = cos_ref[table, :], sin_ref[table, :]
        cos, sin = jnp.concatenate([cos, cos], axis=0), jnp.concatenate([sin, sin], axis=0)
        for c in range(0, q_width, 128):
            q_ref[rows, c:c + 128] = rotate(out[:, c:c + 128].astype(F32), cos, sin).astype(BF16)
        for c in range(0, k_width, 128):
            k_ref[rows, c:c + 128] = rotate(out[:, q_width + c:q_width + c + 128].astype(F32), cos, sin).astype(BF16)
        v_ref[rows, :] = out[:, q_width + k_width:]
        return carry

    lax.fori_loop(0, h_ref.shape[0] // rows_step, step, 0)


def project_qkv(x, gain, cos, sin, w):
    tokens, width = x.shape
    q_width, k_width = 512, 128
    blocks = w.shape[1]
    flops = 2 * tokens * width * blocks * w.shape[3]
    return pl.pallas_call(
        qkv_kernel,
        grid=(blocks,),
        in_specs=[
            pl.BlockSpec((tokens, width), lambda m: (0, 0)),
            pl.BlockSpec((1, width), lambda m: (0, 0)),
            pl.BlockSpec(cos.shape, lambda m: (0, 0)),
            pl.BlockSpec(sin.shape, lambda m: (0, 0)),
            pl.BlockSpec((w.shape[0], 1, w.shape[2], w.shape[3]), lambda m: (0, m, 0, 0)),
        ],
        out_specs=[
            pl.BlockSpec((tokens, q_width), lambda m: (0, m)),
            pl.BlockSpec((tokens, k_width), lambda m: (0, m)),
            pl.BlockSpec((tokens, k_width), lambda m: (0, m)),
        ],
        out_shape=[
            jax.ShapeDtypeStruct((tokens, blocks * q_width), BF16),
            jax.ShapeDtypeStruct((tokens, blocks * k_width), BF16),
            jax.ShapeDtypeStruct((tokens, blocks * k_width), BF16),
        ],
        scratch_shapes=[pltpu.VMEM((tokens, width), BF16)],
        compiler_params=params(),
        cost_estimate=pl.CostEstimate(flops=flops, bytes_accessed=4 * tokens * width + 2 * w.size, transcendentals=0),
        name="qkv",
    )(x, gain, cos, sin, w)


def attention_kernel(q_ref, k_ref, v_ref, o_ref, qs, ks, vs, os):
    chunks, _, chunk, q_width = q_ref.shape
    seq = chunks * chunk
    heads, kv_heads = q_width // 64, k_ref.shape[3] // 64
    for j in range(heads):
        qs[j] = q_ref[:, 0, :, 64 * j:64 * j + 64].reshape(seq, 64)
    for g in range(kv_heads):
        ks[g] = k_ref[:, 0, :, 64 * g:64 * g + 64].reshape(seq, 64)
        vs[g] = v_ref[:, 0, :, 64 * g:64 * g + 64].reshape(seq, 64)
    scale = 64 ** -0.5 * math.log2(math.e)
    row = lax.broadcasted_iota(jnp.int32, (chunk, chunk), 0)
    col = lax.broadcasted_iota(jnp.int32, (chunk, chunk), 1)
    causal = row >= col

    def score(q, k):
        return lax.dot_general(q, k, (((1,), (1,)), ((), ())), preferred_element_type=F32)

    def head(j, carry):
        g = j // (heads // kv_heads)
        for b in range(chunks):
            here = slice(b * chunk, (b + 1) * chunk)
            q = qs[j, here, :]
            diag = jnp.where(causal, score(q, ks[g, here, :]), -jnp.inf)
            top = jnp.max(diag, axis=1, keepdims=True)
            if b:
                past = score(q, ks[g, :b * chunk, :])
                top = jnp.maximum(top, jnp.max(past, axis=1, keepdims=True))
            diag = jnp.exp2((diag - top) * scale)
            total = jnp.sum(diag, axis=1, keepdims=True)
            if b:
                past = jnp.exp2((past - top) * scale)
                total = total + jnp.sum(past, axis=1, keepdims=True)
            inverse = 1.0 / total
            out = dot((diag * inverse).astype(BF16), vs[g, here, :])
            if b:
                out = out + dot((past * inverse).astype(BF16), vs[g, :b * chunk, :])
            os[j, here, :] = out.astype(BF16)
        return carry

    lax.fori_loop(0, heads, head, 0)
    for j in range(heads):
        o_ref[:, 0, :, 64 * j:64 * j + 64] = os[j].reshape(chunks, chunk, 64)


def attend(q, k, v, chunks, seqs):
    tokens = q.shape[0]
    chunk = tokens // (chunks * seqs)
    q4, k4, v4 = (a.reshape(chunks, seqs, chunk, a.shape[1]) for a in (q, k, v))
    seq = chunks * chunk
    blocks = k.shape[1] // 128
    q_width = q.shape[1] // blocks
    heads = q.shape[1] // 64
    out = pl.pallas_call(
        attention_kernel,
        grid=(seqs * blocks,),
        in_specs=[
            pl.BlockSpec((chunks, 1, chunk, q_width), lambda i: (0, i // blocks, 0, i % blocks)),
            pl.BlockSpec((chunks, 1, chunk, 128), lambda i: (0, i // blocks, 0, i % blocks)),
            pl.BlockSpec((chunks, 1, chunk, 128), lambda i: (0, i // blocks, 0, i % blocks)),
        ],
        out_specs=pl.BlockSpec((chunks, 1, chunk, q_width), lambda i: (0, i // blocks, 0, i % blocks)),
        out_shape=jax.ShapeDtypeStruct(q4.shape, BF16),
        scratch_shapes=[
            pltpu.VMEM((q_width // 64, seq, 64), BF16),
            pltpu.VMEM((2, seq, 64), BF16),
            pltpu.VMEM((2, seq, 64), BF16),
            pltpu.VMEM((q_width // 64, seq, 64), BF16),
        ],
        compiler_params=params(),
        cost_estimate=pl.CostEstimate(flops=16 * seqs * heads * seq * seq * 64, bytes_accessed=5 * q.size, transcendentals=seqs * heads * seq * seq),
        name="attention",
    )(q4, k4, v4)
    return out.reshape(q.shape)


def add_matmul_kernel(a_ref, w_ref, r_ref, o_ref, *, chunk):
    w = w_ref[0]
    for r in range(0, a_ref.shape[0], chunk):
        acc = dot(a_ref[r:r + chunk, :], w)
        o_ref[r:r + chunk, :] = (r_ref[r:r + chunk, :].astype(F32) + acc).astype(BF16)


def add_matmul(a, w, resid, part, block, rows):
    tokens, depth = a.shape
    halves, _, cols = w.shape
    per = cols // block
    full = resid.shape[1] // halves // block

    def resid_cols(i):
        y, j = (i // per) % halves, i % per
        return y * full + part * per + j

    steps = halves * per
    return pl.pallas_call(
        functools.partial(add_matmul_kernel, chunk=min(512, rows)),
        grid=(tokens // rows * steps,),
        in_specs=[
            pl.BlockSpec((rows, depth), lambda i: (i // steps, 0)),
            pl.BlockSpec((1, depth, block), lambda i: ((i // per) % halves, 0, i % per)),
            pl.BlockSpec((rows, block), lambda i: (i // steps, resid_cols(i))),
        ],
        out_specs=pl.BlockSpec((rows, block), lambda i: (i // steps, i % steps)),
        out_shape=jax.ShapeDtypeStruct((tokens, halves * cols), BF16),
        compiler_params=params(),
        cost_estimate=pl.CostEstimate(flops=2 * tokens * depth * halves * cols, bytes_accessed=2 * (a.size + w.size), transcendentals=0),
    )(a, w, resid)


def gate_up_kernel(x_ref, gain_ref, wg_ref, wu_ref, z_ref, h_ref, *, chunk):
    @pl.when(pl.program_id(0) == 0)
    def _():
        normalise(x_ref, gain_ref, h_ref, 128)

    depth = wg_ref.shape[0] * wg_ref.shape[2]
    wg = wg_ref[...].reshape(depth, wg_ref.shape[3])
    wu = wu_ref[...].reshape(depth, wu_ref.shape[3])
    for r in range(0, h_ref.shape[0], chunk):
        h = h_ref[r:r + chunk, :]
        gate = dot(h, wg)
        up = dot(h, wu)
        z_ref[r:r + chunk, :] = (gate * jax.nn.sigmoid(gate) * up).astype(BF16)


def gate_up(x, gain, wg, wu):
    tokens, width = x.shape
    ys, blocks, rows, hidden = wg.shape
    block = 512
    per = hidden // block
    w_spec = pl.BlockSpec((ys, 1, rows, block), lambda i: (0, i // per, 0, i % per))
    return pl.pallas_call(
        functools.partial(gate_up_kernel, chunk=512),
        grid=(blocks * per,),
        in_specs=[
            pl.BlockSpec((tokens, width), lambda i: (0, 0)),
            pl.BlockSpec((1, width), lambda i: (0, 0)),
            w_spec,
            w_spec,
        ],
        out_specs=pl.BlockSpec((tokens, block), lambda i: (0, i)),
        out_shape=jax.ShapeDtypeStruct((tokens, blocks * hidden), BF16),
        scratch_shapes=[pltpu.VMEM((tokens, width), BF16)],
        compiler_params=params(),
        cost_estimate=pl.CostEstimate(flops=4 * tokens * width * blocks * hidden, bytes_accessed=2 * (x.size + 2 * wg.size), transcendentals=tokens * blocks * hidden),
    )(x, gain, wg, wu)


def down_kernel(za_ref, zb_ref, w_ref, r_ref, o_ref, *, chunk):
    blocks, _, hidden, cols = w_ref.shape[1:]
    wa = w_ref[0, :, 0].reshape(blocks * hidden, cols)
    wb = w_ref[0, :, 1].reshape(blocks * hidden, cols)
    for r in range(0, za_ref.shape[0], chunk):
        acc = dot(za_ref[r:r + chunk, :], wa) + dot(zb_ref[r:r + chunk, :], wb)
        o_ref[r:r + chunk, :] = (r_ref[r:r + chunk, :].astype(F32) + acc).astype(BF16)


def down(za, zb, w, resid, part, block):
    tokens, depth = za.shape
    ys, blocks, rows_w, cols = w.shape
    w = w.reshape(ys, blocks, 2, rows_w // 2, cols)
    per = cols // block
    full = resid.shape[1] // ys // block
    steps = ys * per
    rows = 1024

    def resid_cols(i):
        return (i // per) % ys * full + part * per + i % per

    return pl.pallas_call(
        functools.partial(down_kernel, chunk=512),
        grid=(tokens // rows * steps,),
        in_specs=[
            pl.BlockSpec((rows, depth), lambda i: (i // steps, 0)),
            pl.BlockSpec((rows, depth), lambda i: (i // steps, 0)),
            pl.BlockSpec((1, blocks, 2, rows_w // 2, block), lambda i: ((i // per) % ys, 0, 0, 0, i % per)),
            pl.BlockSpec((rows, block), lambda i: (i // steps, resid_cols(i))),
        ],
        out_specs=pl.BlockSpec((rows, block), lambda i: (i // steps, i % steps)),
        out_shape=jax.ShapeDtypeStruct((tokens, ys * cols), BF16),
        compiler_params=params(),
        cost_estimate=pl.CostEstimate(flops=4 * tokens * depth * ys * cols, bytes_accessed=2 * (2 * za.size + w.size), transcendentals=0),
    )(za, zb, w, resid)


def solution(mesh):
    act_spec = P('fsdp', 'model', None)
    col_spec = P(None, 'fsdp', 'model')
    row_spec = P(None, 'model', 'fsdp')
    ys, ms = mesh.shape['fsdp'], mesh.shape['model']
    tail_parts = 4

    def gather(block):
        full = lax.all_gather(block, ('fsdp', 'model'), axis=0, tiled=False)
        return full.reshape((ys, ms) + block.shape)

    def exchange(tokens):
        return lax.all_to_all(tokens, 'model', split_axis=0, concat_axis=0, tiled=True)

    def device_step(x_in, gain_attn, gain_mlp, rope_cos, rope_sin, w_q, w_k, w_v, w_o, w_gate, w_up, w_down):
        layers = w_q.shape[0]
        half = w_gate.shape[2] // 2
        seqs = x_in.shape[0] // ms
        x = exchange(x_in)
        gathered = []
        for l in range(layers):
            block = jnp.concatenate([w_q[l], w_k[l], w_v[l]], axis=1)
            wqkv = gather(block)
            wo = gather(w_o[l])
            wgs, wus = [], []
            for h in range(2):
                gate, up = (w[l, :, h * half:(h + 1) * half] for w in (w_gate, w_up))
                wgs.append(gather(gate))
                wus.append(gather(up))
            parts = tail_parts if l == layers - 1 else 1
            cols = w_down.shape[2] // parts
            wds = []
            for c in range(parts):
                block = w_down[l, :, c * cols:(c + 1) * cols]
                wds.append(gather(block))
            gathered.append((wqkv, wo, wgs, wus, wds))

        chunk_shape = x.shape[:2]
        x = x.reshape(-1, x.shape[2])
        cos = jnp.tile(rope_cos, (1, 4))
        sin = jnp.tile(jnp.concatenate([-rope_sin, rope_sin], axis=1), (1, 2))
        for l in range(layers):
            wqkv, wo, wgs, wus, wds = gathered[l]
            q, k, v = project_qkv(x, gain_attn[l][None], cos, sin, wqkv)
            o = attend(q, k, v, ms, seqs)
            m = add_matmul(o, wo.reshape(ys, -1, wo.shape[3]), x, 0, 512, x.shape[0])
            za, zb = (gate_up(m, gain_mlp[l][None], wg, wu) for wg, wu in zip(wgs, wus))
            outs = [down(za, zb, wd, m, c, 256) for c, wd in enumerate(wds)]
            if l < layers - 1:
                x = outs[0]
        cols = outs[0].shape[1] // ys
        outs = [exchange(out.reshape(chunk_shape + (out.shape[1],))) for out in outs]
        return jnp.concatenate([out[:, :, y * cols:(y + 1) * cols] for y in range(ys) for out in outs], axis=2)

    return jax.shard_map(device_step, mesh=mesh, in_specs=(act_spec, P(), P(), P(), P(), col_spec, col_spec, col_spec, row_spec, col_spec, col_spec, row_spec), out_specs=act_spec, check_vma=False)
```

time: 4080 us -> 1480 us (0.36)
  waiting for transfers between devices: 2780 us -> 425 us
  matrix products: 1060 us -> 0 us
  Pallas kernels: 0 us -> 967 us
  other arithmetic: 132 us -> 2.58 us
  blocking collectives: 47.7 us -> 0 us
    reduce_scatter x4 -> x0, waiting for transfers between devices: 1750 us -> none  [the longest x2 879 us: device_step(): lax.psum_scatter(mlp_part, 'model', scatter_dimension=1, tiled=True)]
    pallas_call x0 -> x15, Pallas kernels: none -> 967 us  [the longest x4 324 us: gate_up(): pl.pallas_call(functools.partial(gate_up_kernel, chunk=512), grid=(blocks...]
    dot_general x16 -> x0, matrix products: 851 us -> none  [the longest x2 171 us: device_step(): jnp.einsum('bsd,df->bsf', mlp_in, wg_full, preferred_element_type=jnp.flo...]
    all_gather x14 -> x17, waiting for transfers between devices: 1030 us -> 237 us  [gather(): full = lax.all_gather(block, ('fsdp', 'model'), axis=0, tiled=False)]
    sub x2 -> x0, matrix products: 210 us -> none  [attend(): attn_probs = jax.nn.softmax(scores, axis=-1).astype(jnp.bfloat16)]
    all_to_all x0 -> x5, waiting for transfers between devices: none -> 182 us  [exchange(): lax.all_to_all(tokens, 'model', split_axis=0, concat_axis=0, tiled=True)]
    convert_element_type x9 -> x0, other arithmetic: 70.2 us -> none  [the longest x4 34.6 us: rms_norm(): return (rows_f * lax.rsqrt(mean_sq + EPS) * gain_vec).astype(jnp.bfloat16)]
    all_gather x4 -> x0, blocking collectives: 47.7 us -> none  [the longest x2 31.4 us: device_step(): wv_full = lax.all_gather(w_v[layer_idx], 'fsdp', axis=0, tiled=True)]
  transfers between devices with their start and end apart: 18 -> 22, of which waited for: 14 -> 8; matrix products, arithmetic and copies ran while one was open for 24% -> 2% of each run, Pallas kernels for 0% -> 65%
where the time goes in v1:
time: 1480 us
  Pallas kernels  967 us (65%)
  waiting for transfers between devices  425 us (29%)
  local copies, waits for them, and re-layouts  46.9 us (3%)
  starting transfers between devices  23.9 us (2%)
    pallas_call x4, Pallas kernels, gate_up(): pl.pallas_call(functools.partial(gate_up_kernel, chunk=512), grid=(blocks...  324 us
    pallas_call x2, Pallas kernels, attend(): pl.pallas_call(attention_kernel, grid=(seqs * blocks,), in_specs=[pl.Bloc...  304 us
    all_gather x17, waiting for transfers between devices, gather(): full = lax.all_gather(block, ('fsdp', 'model'), axis=0, tiled=False)  237 us
    pallas_call x5, Pallas kernels, down(): pl.pallas_call(functools.partial(down_kernel, chunk=512), grid=(tokens //...  203 us
    all_to_all x5, waiting for transfers between devices, exchange(): lax.all_to_all(tokens, 'model', split_axis=0, concat_axis=0, tiled=True)  182 us
    pallas_call x2, Pallas kernels, project_qkv(): pl.pallas_call(qkv_kernel, grid=(blocks,), in_specs=[pl.BlockSpec((tokens...  85.9 us
    pallas_call x2, Pallas kernels, add_matmul(): pl.pallas_call(functools.partial(add_matmul_kernel, chunk=min(512, rows))...  50.3 us
  transfers between devices with their start and end apart: 22, of which 8 were waited for; matrix products, arithmetic and copies ran while one was open for 2% of the time, Pallas kernels for 65%

profile of v1, /device:TPU:0, one launch (start us, length us, event | category | flops | bytes accessed | tf_op | source)
XLA Modules:
  0.0 1479.0 jit_solution(432288945399263977)
XLA Ops:
  12.1 6.1 fusion.2
  18.3 7.8 fusion.1
  27.3 4.6 slice.111
  37.6 4.3 fusion
  43.2 5.8 all-to-all-start
  53.1 150.7 %all-to-all-done = bf16[8,256,2048]{2,1,0:T(8,128)(2,1)} async-done(((bf16[8,256,2048]{2,1,0:T(8,128)(2,1)}), bf16[8,256,2048]{2,1,0:T(8,128)(2,1)}, u32[]{:S(2)}, u32[]{:S(2)}) %all-to-all-start) | async-done | bytes 8388640 | tf_op jit(solution)/shard_map/all_to_all | solution.py:296
  203.7 43.1 %qkv.2 = (bf16[2048,2048]{1,0:T(8,128)(2,1)}, bf16[2048,512]{1,0:T(8,128)(2,1)}, bf16[2048,512]{1,0:T(8,128)(2,1)}) custom-call(bf16[2048,2048]{1,0:T(8,128)(2,1)} %bitcast.x_ref.r_ref, f32[1,2048]{1,0:T(1,128)} %get-tuple-element.40.gain_ref, f32[1024,128]{1,0:T(8,128)} %copy.19.cos_ref, f32[1024,128]{1,0:T(8,128)} %copy.20.sin_ref, ...), custom_call_target="tpu_custom_call" | custom-call | flops 25769803776 | bytes 29360128 | tf_op jit(solution)/shard_map/qkv/pallas_call | solution.py:74
  246.8 151.5 %attention.2 = bf16[4,2,256,2048]{3,2,1,0:T(8,128)(2,1)} custom-call(bf16[4,2,256,2048]{3,2,1,0:T(8,128)(2,1)} %bitcast.70, bf16[4,2,256,512]{3,2,1,0:T(8,128)(2,1)} %bitcast.73, bf16[4,2,256,512]{3,2,1,0:T(8,128)(2,1)} %bitcast.74), custom_call_target="tpu_custom_call" | custom-call | flops 68719476736 | bytes 20971520 | tf_op jit(solution)/shard_map/attention/pallas_call | solution.py:153
  398.3 26.2 %shard_map.118.x_ref.r_ref = bf16[2048,2048]{1,0:T(8,128)(2,1)} custom-call(bf16[2048,2048]{1,0:T(8,128)(2,1)} %bitcast.67, bf16[2,2048,1024]{2,1,0:T(8,128)(2,1)} %bitcast.61, bf16[2048,2048]{1,0:T(8,128)(2,1)} %bitcast.x_ref.r_ref), custom_call_target="tpu_custom_call" | custom-call | flops 17179869184 | bytes 16777216 | tf_op jit(solution)/shard_map/pallas_call | solution.py:194
  424.5 81.0 %shard_map.119.za_ref = bf16[2048,4096]{1,0:T(8,128)(2,1)} custom-call(bf16[2048,2048]{1,0:T(8,128)(2,1)} %shard_map.118.x_ref.r_ref, f32[1,2048]{1,0:T(1,128)} %get-tuple-element.38.gain_ref, bf16[2,4,1024,1024]{3,2,1,0:T(8,128)(2,1)} %bitcast.51, bf16[2,4,1024,1024]{3,2,1,0:T(8,128)(2,1)} %bitcast.52), custom_call_target="tpu_custom_call" | custom-call | flops 68719476736 | bytes 41943040 | tf_op jit(solution)/shard_map/pallas_call | solution.py:230
  505.5 28.1 %all-gather.28.cloned.1.call-done = bf16[8,1024,1024]{2,1,0:T(8,128)(2,1)} async-done(((bf16[1,1024,1024]{2,1,0:T(8,128)(2,1)}), bf16[8,1024,1024]{2,1,0:T(8,128)(2,1)}) %all-gather.28.cloned.1.call-update) | async-done | bytes 16777232 | tf_op jit(solution)/shard_map/all_gather | solution.py:292
  533.6 81.2 %shard_map.120.zb_ref = bf16[2048,4096]{1,0:T(8,128)(2,1)} custom-call(bf16[2048,2048]{1,0:T(8,128)(2,1)} %shard_map.118.x_ref.r_ref, f32[1,2048]{1,0:T(1,128)} %get-tuple-element.38.gain_ref, bf16[2,4,1024,1024]{3,2,1,0:T(8,128)(2,1)} %bitcast.53, bf16[2,4,1024,1024]{3,2,1,0:T(8,128)(2,1)} %bitcast.54), custom_call_target="tpu_custom_call" | custom-call | flops 68719476736 | bytes 41943040 | tf_op jit(solution)/shard_map/pallas_call | solution.py:230
  614.8 75.7 %all-gather.30.cloned.1.call-done = bf16[8,2048,1024]{2,1,0:T(8,128)(2,1)} async-done(((bf16[1,2048,1024]{2,1,0:T(8,128)(2,1)}), bf16[8,2048,1024]{2,1,0:T(8,128)(2,1)}) %all-gather.30.cloned.1.call-update) | async-done | bytes 33554448 | tf_op jit(solution)/shard_map/all_gather | solution.py:292
  690.6 84.6 %shard_map.121.x_ref.r_ref = bf16[2048,2048]{1,0:T(8,128)(2,1)} custom-call(bf16[2048,4096]{1,0:T(8,128)(2,1)} %shard_map.119.za_ref, bf16[2048,4096]{1,0:T(8,128)(2,1)} %shard_map.120.zb_ref, bf16[2,4,2,1024,1024]{4,3,2,1,0:T(8,128)(2,1)} %bitcast.50, bf16[2048,2048]{1,0:T(8,128)(2,1)} %shard_map.118.x_ref.r_ref), custom_call_target="tpu_custom_call" | custom-call | flops 68719476736 | bytes 67108864 | tf_op jit(solution)/shard_map/pallas_call | solution.py:268
  775.2 42.9 %qkv.3 = (bf16[2048,2048]{1,0:T(8,128)(2,1)}, bf16[2048,512]{1,0:T(8,128)(2,1)}, bf16[2048,512]{1,0:T(8,128)(2,1)}) custom-call(bf16[2048,2048]{1,0:T(8,128)(2,1)} %shard_map.121.x_ref.r_ref, f32[1,2048]{1,0:T(1,128)} %get-tuple-element.39.gain_ref, f32[1024,128]{1,0:T(8,128)} %copy.19.cos_ref, f32[1024,128]{1,0:T(8,128)} %copy.20.sin_ref, ...), custom_call_target="tpu_custom_call" | custom-call | flops 25769803776 | bytes 29360128 | tf_op jit(solution)/shard_map/qkv/pallas_call | solution.py:74
  818.0 152.0 %attention.3 = bf16[4,2,256,2048]{3,2,1,0:T(8,128)(2,1)} custom-call(bf16[4,2,256,2048]{3,2,1,0:T(8,128)(2,1)} %bitcast.69, bf16[4,2,256,512]{3,2,1,0:T(8,128)(2,1)} %bitcast.71, bf16[4,2,256,512]{3,2,1,0:T(8,128)(2,1)} %bitcast.72), custom_call_target="tpu_custom_call" | custom-call | flops 68719476736 | bytes 20971520 | tf_op jit(solution)/shard_map/attention/pallas_call | solution.py:153
  970.0 24.2 %shard_map.122.x_ref.r_ref = bf16[2048,2048]{1,0:T(8,128)(2,1)} custom-call(bf16[2048,2048]{1,0:T(8,128)(2,1)} %bitcast.68, bf16[2,2048,1024]{2,1,0:T(8,128)(2,1)} %bitcast.62, bf16[2048,2048]{1,0:T(8,128)(2,1)} %shard_map.121.x_ref.r_ref), custom_call_target="tpu_custom_call" | custom-call | flops 17179869184 | bytes 16777216 | tf_op jit(solution)/shard_map/pallas_call | solution.py:194
  994.2 80.8 %shard_map.124.zb_ref = bf16[2048,4096]{1,0:T(8,128)(2,1)} custom-call(bf16[2048,2048]{1,0:T(8,128)(2,1)} %shard_map.122.x_ref.r_ref, f32[1,2048]{1,0:T(1,128)} %get-tuple-element.37.gain_ref, bf16[2,4,1024,1024]{3,2,1,0:T(8,128)(2,1)} %bitcast.55, bf16[2,4,1024,1024]{3,2,1,0:T(8,128)(2,1)} %bitcast.56), custom_call_target="tpu_custom_call" | custom-call | flops 68719476736 | bytes 41943040 | tf_op jit(solution)/shard_map/pallas_call | solution.py:230
  1075.0 78.2 %all-gather.36.cloned.1.call-done = bf16[8,1024,1024]{2,1,0:T(8,128)(2,1)} async-done(((bf16[1,1024,1024]{2,1,0:T(8,128)(2,1)}), bf16[8,1024,1024]{2,1,0:T(8,128)(2,1)}) %all-gather.36.cloned.1.call-update) | async-done | bytes 16777232 | tf_op jit(solution)/shard_map/all_gather | solution.py:292
  1153.2 81.0 %shard_map.123.za_ref = bf16[2048,4096]{1,0:T(8,128)(2,1)} custom-call(bf16[2048,2048]{1,0:T(8,128)(2,1)} %shard_map.122.x_ref.r_ref, f32[1,2048]{1,0:T(1,128)} %get-tuple-element.37.gain_ref, bf16[2,4,1024,1024]{3,2,1,0:T(8,128)(2,1)} %bitcast.57, bf16[2,4,1024,1024]{3,2,1,0:T(8,128)(2,1)} %bitcast.58), custom_call_target="tpu_custom_call" | custom-call | flops 68719476736 | bytes 41943040 | tf_op jit(solution)/shard_map/pallas_call | solution.py:230
  1234.2 29.4 %shard_map.127 = bf16[2048,512]{1,0:T(8,128)(2,1)} custom-call(bf16[2048,4096]{1,0:T(8,128)(2,1)} %shard_map.123.za_ref, bf16[2048,4096]{1,0:T(8,128)(2,1)} %shard_map.124.zb_ref, bf16[2,4,2,1024,256]{4,3,2,1,0:T(8,128)(2,1)} %bitcast.66, bf16[2048,2048]{1,0:T(8,128)(2,1)} %shard_map.122.x_ref.r_ref), custom_call_target="tpu_custom_call" | custom-call | flops 17179869184 | bytes 41943040 | tf_op jit(solution)/shard_map/pallas_call | solution.py:268
  1263.6 3.9 all-to-all-start.3
  1267.5 30.7 %shard_map.126 = bf16[2048,512]{1,0:T(8,128)(2,1)} custom-call(bf16[2048,4096]{1,0:T(8,128)(2,1)} %shard_map.123.za_ref, bf16[2048,4096]{1,0:T(8,128)(2,1)} %shard_map.124.zb_ref, bf16[2,4,2,1024,256]{4,3,2,1,0:T(8,128)(2,1)} %bitcast.65, bf16[2048,2048]{1,0:T(8,128)(2,1)} %shard_map.122.x_ref.r_ref), custom_call_target="tpu_custom_call" | custom-call | flops 17179869184 | bytes 41943040 | tf_op jit(solution)/shard_map/pallas_call | solution.py:268
  1298.2 11.5 all-to-all-done.3
  1309.7 4.5 all-to-all-start.2
  1314.2 8.9 all-gather.42.cloned.1.call-done
  1323.1 29.4 %shard_map.125 = bf16[2048,512]{1,0:T(8,128)(2,1)} custom-call(bf16[2048,4096]{1,0:T(8,128)(2,1)} %shard_map.123.za_ref, bf16[2048,4096]{1,0:T(8,128)(2,1)} %shard_map.124.zb_ref, bf16[2,4,2,1024,256]{4,3,2,1,0:T(8,128)(2,1)} %bitcast.63, bf16[2048,2048]{1,0:T(8,128)(2,1)} %shard_map.122.x_ref.r_ref), custom_call_target="tpu_custom_call" | custom-call | flops 17179869184 | bytes 41943040 | tf_op jit(solution)/shard_map/pallas_call | solution.py:268
  1352.6 4.5 all-to-all-start.1
  1357.1 45.6 %all-gather.48.cloned.1.call-done = bf16[8,2048,256]{2,1,0:T(8,128)(2,1)} async-done(((bf16[1,2048,256]{2,1,0:T(8,128)(2,1)}), bf16[8,2048,256]{2,1,0:T(8,128)(2,1)}) %all-gather.48.cloned.1.call-update) | async-done | bytes 8388624 | tf_op jit(solution)/shard_map/all_gather | solution.py:292
  1402.6 29.3 %shard_map.128 = bf16[2048,512]{1,0:T(8,128)(2,1)} custom-call(bf16[2048,4096]{1,0:T(8,128)(2,1)} %shard_map.123.za_ref, bf16[2048,4096]{1,0:T(8,128)(2,1)} %shard_map.124.zb_ref, bf16[2,4,2,1024,256]{4,3,2,1,0:T(8,128)(2,1)} %bitcast.64, bf16[2048,2048]{1,0:T(8,128)(2,1)} %shard_map.122.x_ref.r_ref), custom_call_target="tpu_custom_call" | custom-call | flops 17179869184 | bytes 41943040 | tf_op jit(solution)/shard_map/pallas_call | solution.py:268
  1432.0 4.4 all-to-all-start.4
  1442.0 20.2 %all-to-all-done.4 = bf16[8,256,512]{2,1,0:T(8,128)(2,1)} async-done(((bf16[8,256,512]{2,1,0:T(8,128)(2,1)}), bf16[8,256,512]{2,1,0:T(8,128)(2,1)}, u32[]{:S(2)}, u32[]{:S(2)}) %all-to-all-start.4) | async-done | bytes 2097184 | tf_op jit(solution)/shard_map/all_to_all | solution.py:296
  (85 shorter events, 33.2 us)
Async XLA Ops:
  6.5 197.2 %all-gather.50.cloned.1.call-start = ((), (), s32[]{:S(2)}) async-start(), calls=%async_computation.20 | async-start | bytes 14155776 | tf_op jit(solution)/shard_map/all_gather | solution.py:292
  6.5 1.8 copy-start.3
  6.5 1.8 copy-start.4
  8.4 2.1 copy-start
  10.5 387.8 %all-gather.20.cloned.1.call-start = ((), (), s32[]{:S(2)}) async-start(), calls=%async_computation.5 | async-start | bytes 9437184 | tf_op jit(solution)/shard_map/all_gather | solution.py:292
  12.1 412.4 %all-gather.22.cloned.1.call-start = ((), (), s32[]{:S(2)}) async-start(), calls=%async_computation.6 | async-start | bytes 18874368 | tf_op jit(solution)/shard_map/all_gather | solution.py:292
  18.2 406.2 %all-gather.24.cloned.1.call-start = ((), (), s32[]{:S(2)}) async-start(), calls=%async_computation.7 | async-start | bytes 18874368 | tf_op jit(solution)/shard_map/all_gather | solution.py:292
  26.1 479.4 %all-gather.26.cloned.1.call-start = ((), (), s32[]{:S(2)}) async-start(), calls=%async_computation.8 | async-start | bytes 18874368 | tf_op jit(solution)/shard_map/all_gather | solution.py:292
  26.7 506.9 %all-gather.28.cloned.1.call-start = ((), (), s32[]{:S(2)}) async-start(), calls=%async_computation.9 | async-start | bytes 18874368 | tf_op jit(solution)/shard_map/all_gather | solution.py:292
  27.3 663.3 %all-gather.30.cloned.1.call-start = ((), (), s32[]{:S(2)}) async-start(), calls=%async_computation.10 | async-start | bytes 37748736 | tf_op jit(solution)/shard_map/all_gather | solution.py:292
  32.0 0.9 copy-start.1
  32.0 743.2 %all-gather.52.cloned.1.call-start = ((), (), s32[]{:S(2)}) async-start(), calls=%async_computation.21 | async-start | bytes 14155776 | tf_op jit(solution)/shard_map/all_gather | solution.py:292
  34.2 935.8 %all-gather.32.cloned.1.call-start = ((), (), s32[]{:S(2)}) async-start(), calls=%async_computation.11 | async-start | bytes 9437184 | tf_op jit(solution)/shard_map/all_gather | solution.py:292
  34.9 959.3 %all-gather.38.cloned.1.call-start = ((), (), s32[]{:S(2)}) async-start(), calls=%async_computation.14 | async-start | bytes 18874368 | tf_op jit(solution)/shard_map/all_gather | solution.py:292
  35.5 958.7 %all-gather.40.cloned.1.call-start = ((), (), s32[]{:S(2)}) async-start(), calls=%async_computation.15 | async-start | bytes 18874368 | tf_op jit(solution)/shard_map/all_gather | solution.py:292
  36.3 1038.8 %all-gather.34.cloned.1.call-start = ((), (), s32[]{:S(2)}) async-start(), calls=%async_computation.12 | async-start | bytes 18874368 | tf_op jit(solution)/shard_map/all_gather | solution.py:292
  36.8 1116.4 %all-gather.36.cloned.1.call-start = ((), (), s32[]{:S(2)}) async-start(), calls=%async_computation.13 | async-start | bytes 18874368 | tf_op jit(solution)/shard_map/all_gather | solution.py:292
  37.6 1196.7 %all-gather.46.cloned.1.call-start = ((), (), s32[]{:S(2)}) async-start(), calls=%async_computation.18 | async-start | bytes 9437184 | tf_op jit(solution)/shard_map/all_gather | solution.py:292
  42.0 1225.5 %all-gather.44.cloned.1.call-start = ((), (), s32[]{:S(2)}) async-start(), calls=%async_computation.17 | async-start | bytes 9437184 | tf_op jit(solution)/shard_map/all_gather | solution.py:292
  42.6 1280.6 %all-gather.42.cloned.1.call-start = ((), (), s32[]{:S(2)}) async-start(), calls=%async_computation.16 | async-start | bytes 9437184 | tf_op jit(solution)/shard_map/all_gather | solution.py:292
  43.2 6.4 copy-start.2
  43.2 7.6 copy-start.5
  43.2 160.5 %all-to-all-start = ((bf16[8,256,2048]{2,1,0:T(8,128)(2,1)}), bf16[8,256,2048]{2,1,0:T(8,128)(2,1)}, u32[]{:S(2)}, u32[]{:S(2)}) async-start(bf16[8,256,2048]{2,1,0:T(8,128)(2,1)} %param.12), calls=%async_computation | async-start | bytes 16777216 | tf_op jit(solution)/shard_map/all_to_all | solution.py:296
  49.0 2.8 copy-start.6
  49.0 3.4 copy-start.7
  49.0 1353.6 %all-gather.48.cloned.1.call-start = ((), (), s32[]{:S(2)}) async-start(), calls=%async_computation.19 | async-start | bytes 9437184 | tf_op jit(solution)/shard_map/all_gather | solution.py:292
  1263.6 46.1 %all-to-all-start.3 = ((bf16[8,256,512]{2,1,0:T(8,128)(2,1)}), bf16[8,256,512]{2,1,0:T(8,128)(2,1)S(1)}, u32[]{:S(2)}, u32[]{:S(2)}) async-start(bf16[8,256,512]{2,1,0:T(8,128)(2,1)} %bitcast.48), calls=%async_computation.3 | async-start | bytes 4194304 | tf_op jit(solution)/shard_map/all_to_all | solution.py:296
  1309.7 42.9 %all-to-all-start.2 = ((bf16[8,256,512]{2,1,0:T(8,128)(2,1)}), bf16[8,256,512]{2,1,0:T(8,128)(2,1)}, u32[]{:S(2)}, u32[]{:S(2)}) async-start(bf16[8,256,512]{2,1,0:T(8,128)(2,1)} %bitcast.47), calls=%async_computation.2 | async-start | bytes 4194304 | tf_op jit(solution)/shard_map/all_to_all | solution.py:296
  1352.6 79.4 %all-to-all-start.1 = ((bf16[8,256,512]{2,1,0:T(8,128)(2,1)}), bf16[8,256,512]{2,1,0:T(8,128)(2,1)}, u32[]{:S(2)}, u32[]{:S(2)}) async-start(bf16[8,256,512]{2,1,0:T(8,128)(2,1)} %bitcast.45), calls=%async_computation.1 | async-start | bytes 4194304 | tf_op jit(solution)/shard_map/all_to_all | solution.py:296
  1432.0 30.2 %all-to-all-start.4 = ((bf16[8,256,512]{2,1,0:T(8,128)(2,1)}), bf16[8,256,512]{2,1,0:T(8,128)(2,1)}, u32[]{:S(2)}, u32[]{:S(2)}) async-start(bf16[8,256,512]{2,1,0:T(8,128)(2,1)} %bitcast.46), calls=%async_computation.4 | async-start | bytes 4194304 | tf_op jit(solution)/shard_map/all_to_all | solution.py:296
Sparse Core Ops, SparseCore 0:
  10.6 94.1 all-gather.49
  106.6 81.4 all-gather.19
  189.9 85.9 all-gather.21
  277.6 84.1 all-gather.23
  363.5 84.1 all-gather.25
  449.4 84.1 all-gather.27
  535.4 155.0 all-gather.29
  692.4 66.4 all-gather.51
  760.7 48.6 all-gather.31
  811.1 84.1 all-gather.37
  897.1 84.1 all-gather.39
  983.0 84.1 all-gather.33
  1069.0 84.1 all-gather.35
  1154.9 48.6 all-gather.45
  1205.3 48.6 all-gather.43
  1255.7 67.4 all-gather.41
  1324.8 77.7 all-gather.47

commit v2 on v1

v2 whole, which is shorter than its diff:
```python
import functools
import math

import jax
import jax.numpy as jnp
from jax import lax
from jax.experimental import pallas as pl
from jax.experimental.pallas import tpu as pltpu
from jax.sharding import PartitionSpec as P


EPS = 1e-5
VMEM = 60 * 1024 * 1024
F32 = jnp.float32
BF16 = jnp.bfloat16


def dot(a, b):
    return jnp.dot(a, b, preferred_element_type=F32)


def params():
    return pltpu.CompilerParams(dimension_semantics=("arbitrary",), vmem_limit_bytes=VMEM)


def normalise(x_ref, gain_ref, h_ref, chunk):
    def step(i, carry):
        rows = pl.ds(pl.multiple_of(i * chunk, chunk), chunk)
        x = x_ref[rows, :].astype(F32)
        mean_sq = jnp.mean(x * x, axis=-1, keepdims=True)
        h_ref[rows, :] = (x * lax.rsqrt(mean_sq + EPS) * gain_ref[...]).astype(BF16)
        return carry

    lax.fori_loop(0, x_ref.shape[0] // chunk, step, 0)


def rotate(x, cos, sin):
    lane = lax.broadcasted_iota(jnp.int32, x.shape, 1)
    swapped = jnp.where(lane % 64 < 32, pltpu.roll(x, 96, 1), pltpu.roll(x, 32, 1))
    return x * cos + swapped * sin


def qkv_kernel(x_ref, gain_ref, cos_ref, sin_ref, w_ref, q_ref, k_ref, v_ref, h_ref):
    @pl.when(pl.program_id(0) == 0)
    def _():
        normalise(x_ref, gain_ref, h_ref, 128)

    w = w_ref[...].reshape(w_ref.shape[0] * w_ref.shape[2], w_ref.shape[3])
    q_width, k_width = q_ref.shape[1], k_ref.shape[1]
    positions = 256
    rows_step = 2 * positions

    def step(i, carry):
        rows = pl.ds(pl.multiple_of(i * rows_step, rows_step), rows_step)
        out = dot(h_ref[rows, :], w).astype(BF16)
        table = pl.ds(pl.multiple_of(i * positions, positions), positions)
        cos, sin = cos_ref[table, :], sin_ref[table, :]
        cos, sin = jnp.concatenate([cos, cos], axis=0), jnp.concatenate([sin, sin], axis=0)
        for c in range(0, q_width, 128):
            q_ref[rows, c:c + 128] = rotate(out[:, c:c + 128].astype(F32), cos, sin).astype(BF16)
        for c in range(0, k_width, 128):
            k_ref[rows, c:c + 128] = rotate(out[:, q_width + c:q_width + c + 128].astype(F32), cos, sin).astype(BF16)
        v_ref[rows, :] = out[:, q_width + k_width:]
        return carry

    lax.fori_loop(0, h_ref.shape[0] // rows_step, step, 0)


def project_qkv(x, gain, cos, sin, w):
    tokens, width = x.shape
    q_width, k_width = 512, 128
    blocks = w.shape[1]
    flops = 2 * tokens * width * blocks * w.shape[3]
    return pl.pallas_call(
        qkv_kernel,
        grid=(blocks,),
        in_specs=[
            pl.BlockSpec((tokens, width), lambda m: (0, 0)),
            pl.BlockSpec((1, width), lambda m: (0, 0)),
            pl.BlockSpec(cos.shape, lambda m: (0, 0)),
            pl.BlockSpec(sin.shape, lambda m: (0, 0)),
            pl.BlockSpec((w.shape[0], 1, w.shape[2], w.shape[3]), lambda m: (0, m, 0, 0)),
        ],
        out_specs=[
            pl.BlockSpec((tokens, q_width), lambda m: (0, m)),
            pl.BlockSpec((tokens, k_width), lambda m: (0, m)),
            pl.BlockSpec((tokens, k_width), lambda m: (0, m)),
        ],
        out_shape=[
            jax.ShapeDtypeStruct((tokens, blocks * q_width), BF16),
            jax.ShapeDtypeStruct((tokens, blocks * k_width), BF16),
            jax.ShapeDtypeStruct((tokens, blocks * k_width), BF16),
        ],
        scratch_shapes=[pltpu.VMEM((tokens, width), BF16)],
        compiler_params=params(),
        cost_estimate=pl.CostEstimate(flops=flops, bytes_accessed=4 * tokens * width + 2 * w.size, transcendentals=0),
        name="qkv",
    )(x, gain, cos, sin, w)


def attention_kernel(q_ref, k_ref, v_ref, o_ref, qs, ks, vs, os):
    chunks, _, chunk, q_width = q_ref.shape
    seq = chunks * chunk
    heads, kv_heads = q_width // 64, k_ref.shape[3] // 64
    for j in range(heads):
        qs[j] = q_ref[:, 0, :, 64 * j:64 * j + 64].reshape(seq, 64)
    for c in range(chunks):
        keys = k_ref[c, 0].astype(F32).T.astype(BF16)
        for g in range(kv_heads):
            ks[g, :, c * chunk:(c + 1) * chunk] = keys[64 * g:64 * g + 64, :]
    for g in range(kv_heads):
        vs[g] = v_ref[:, 0, :, 64 * g:64 * g + 64].reshape(seq, 64)
    scale = 64 ** -0.5 * math.log2(math.e)
    row = lax.broadcasted_iota(jnp.int32, (chunk, chunk), 0)
    col = lax.broadcasted_iota(jnp.int32, (chunk, chunk), 1)
    causal = row >= col

    def head(j, carry):
        g = j // (heads // kv_heads)
        for b in range(chunks):
            q = qs[j, b * chunk:(b + 1) * chunk, :]
            parts = [dot(q, ks[g, :, c * chunk:(c + 1) * chunk]) for c in range(b + 1)]
            parts[b] = jnp.where(causal, parts[b], -jnp.inf)
            top = jnp.max(functools.reduce(jnp.maximum, parts), axis=1, keepdims=True)
            parts = [jnp.exp2((part - top) * scale) for part in parts]
            inverse = 1.0 / jnp.sum(functools.reduce(jnp.add, parts), axis=1, keepdims=True)
            probs = jnp.concatenate([(part * inverse).astype(BF16) for part in parts], axis=1)
            os[j, b * chunk:(b + 1) * chunk, :] = dot(probs, vs[g, :(b + 1) * chunk, :]).astype(BF16)
        return carry

    lax.fori_loop(0, heads, head, 0)
    for j in range(heads):
        o_ref[:, 0, :, 64 * j:64 * j + 64] = os[j].reshape(chunks, chunk, 64)


def attend(q, k, v, chunks, seqs):
    tokens = q.shape[0]
    chunk = tokens // (chunks * seqs)
    q4, k4, v4 = (a.reshape(chunks, seqs, chunk, a.shape[1]) for a in (q, k, v))
    seq = chunks * chunk
    blocks = k.shape[1] // 128
    q_width = q.shape[1] // blocks
    heads = q.shape[1] // 64
    out = pl.pallas_call(
        attention_kernel,
        grid=(seqs * blocks,),
        in_specs=[
            pl.BlockSpec((chunks, 1, chunk, q_width), lambda i: (0, i // blocks, 0, i % blocks)),
            pl.BlockSpec((chunks, 1, chunk, 128), lambda i: (0, i // blocks, 0, i % blocks)),
            pl.BlockSpec((chunks, 1, chunk, 128), lambda i: (0, i // blocks, 0, i % blocks)),
        ],
        out_specs=pl.BlockSpec((chunks, 1, chunk, q_width), lambda i: (0, i // blocks, 0, i % blocks)),
        out_shape=jax.ShapeDtypeStruct(q4.shape, BF16),
        scratch_shapes=[
            pltpu.VMEM((q_width // 64, seq, 64), BF16),
            pltpu.VMEM((2, 64, seq), BF16),
            pltpu.VMEM((2, seq, 64), BF16),
            pltpu.VMEM((q_width // 64, seq, 64), BF16),
        ],
        compiler_params=params(),
        cost_estimate=pl.CostEstimate(flops=16 * seqs * heads * seq * seq * 64, bytes_accessed=5 * q.size, transcendentals=seqs * heads * seq * seq),
        name="attention",
    )(q4, k4, v4)
    return out.reshape(q.shape)


def out_proj_kernel(a_ref, w_ref, r_ref, o_ref, *, chunk):
    w = w_ref[0].reshape(a_ref.shape[1], w_ref.shape[3])
    for r in range(0, a_ref.shape[0], chunk):
        acc = dot(a_ref[r:r + chunk, :], w)
        o_ref[r:r + chunk, :] = (r_ref[r:r + chunk, :].astype(F32) + acc).astype(BF16)


def out_proj(a, w, row_block, resid):
    tokens, depth = a.shape
    ys, ms, _, cols = w.shape
    block = 512
    per = cols // block
    return pl.pallas_call(
        functools.partial(out_proj_kernel, chunk=512),
        grid=(ys * per,),
        in_specs=[
            pl.BlockSpec((tokens, depth), lambda i: (0, 0)),
            pl.BlockSpec((1, ms, depth // ms, block), lambda i: (i // per, 0, row_block, i % per)),
            pl.BlockSpec((tokens, block), lambda i: (0, i)),
        ],
        out_specs=pl.BlockSpec((tokens, block), lambda i: (0, i)),
        out_shape=jax.ShapeDtypeStruct((tokens, ys * cols), BF16),
        compiler_params=params(),
        cost_estimate=pl.CostEstimate(flops=2 * tokens * depth * ys * cols, bytes_accessed=6 * a.size + 2 * depth * ys * cols, transcendentals=0),
        name="out_proj",
    )(a, w, resid)


def gate_up_kernel(x_ref, gain_ref, wg_ref, wu_ref, z_ref, h_ref, *, chunk):
    @pl.when(pl.program_id(0) == 0)
    def _():
        normalise(x_ref, gain_ref, h_ref, 128)

    depth = wg_ref.shape[0] * wg_ref.shape[2]
    wg = wg_ref[...].reshape(depth, wg_ref.shape[3])
    wu = wu_ref[...].reshape(depth, wu_ref.shape[3])
    for r in range(0, h_ref.shape[0], chunk):
        h = h_ref[r:r + chunk, :]
        gate = dot(h, wg)
        up = dot(h, wu)
        z_ref[r:r + chunk, :] = (gate * jax.nn.sigmoid(gate) * up).astype(BF16)


def gate_up(x, gain, w, hidden):
    tokens, width = x.shape
    ys, ms = w.shape[:2]
    rows = width // ys
    block = 512
    per = hidden // block
    return pl.pallas_call(
        functools.partial(gate_up_kernel, chunk=512),
        grid=(ms * per,),
        in_specs=[
            pl.BlockSpec((tokens, width), lambda i: (0, 0)),
            pl.BlockSpec((1, width), lambda i: (0, 0)),
            pl.BlockSpec((ys, 1, rows, block), lambda i: (0, i // per, 0, i % per)),
            pl.BlockSpec((ys, 1, rows, block), lambda i: (0, i // per, 1, i % per)),
        ],
        out_specs=pl.BlockSpec((tokens, block), lambda i: (0, i)),
        out_shape=jax.ShapeDtypeStruct((tokens, ms * hidden), BF16),
        scratch_shapes=[pltpu.VMEM((tokens, width), BF16)],
        compiler_params=params(),
        cost_estimate=pl.CostEstimate(flops=4 * tokens * width * ms * hidden, bytes_accessed=2 * x.size + 4 * width * ms * hidden, transcendentals=tokens * ms * hidden),
    )(x, gain, w, w)


def down_kernel(place_ref, *refs, count, chunk):
    za, zb, ws = refs[:count], refs[count:2 * count], refs[2 * count:3 * count]
    r_ref, o_ref = refs[3 * count], refs[-1]
    half = za[0].shape[1]
    w = jnp.concatenate([w[h * half:(h + 1) * half, :] for h in range(2) for w in ws], axis=0)
    for r in range(0, r_ref.shape[0], chunk):
        z = jnp.concatenate([z[r:r + chunk, :] for z in za + zb], axis=1)
        o_ref[r:r + chunk, :] = (r_ref[r:r + chunk, :].astype(F32) + dot(z, w)).astype(BF16)


def down(place, za, zb, ws, resid, other, onto=None):
    tokens, width = resid.shape
    count = len(ws)
    half = za.shape[1] // count
    cols = ws[0].shape[1]
    block, rows = 256, 1024
    per = cols // block

    def columns(i, place):
        return (i // per, (place[1] ^ other) * per + i % per)

    z_specs = [pl.BlockSpec((rows, half), lambda i, place, k=k: (i // per, place[0] ^ k)) for k in range(count)]
    in_specs = z_specs + z_specs
    in_specs += [pl.BlockSpec((2 * half, block), lambda i, place: (0, i % per))] * count
    in_specs += [pl.BlockSpec((rows, block), columns)]
    operands = [za] * count + [zb] * count + list(ws) + [resid]
    aliases = {}
    if onto is not None:
        in_specs.append(pl.BlockSpec(memory_space=pl.ANY))
        aliases = {1 + len(operands): 0}
        operands.append(onto)
    return pl.pallas_call(
        functools.partial(down_kernel, count=count, chunk=512),
        grid_spec=pltpu.PrefetchScalarGridSpec(
            num_scalar_prefetch=1,
            grid=(tokens // rows * per,),
            in_specs=in_specs,
            out_specs=pl.BlockSpec((rows, block), columns),
        ),
        out_shape=jax.ShapeDtypeStruct((tokens, width), BF16),
        input_output_aliases=aliases,
        compiler_params=params(),
        cost_estimate=pl.CostEstimate(flops=4 * tokens * za.shape[1] * cols, bytes_accessed=4 * za.size + 4 * za.shape[1] * cols, transcendentals=0),
        name="down_other" if other else "down_own",
    )(place, *operands)


def solution(mesh):
    act_spec = P('fsdp', 'model', None)
    col_spec = P(None, 'fsdp', 'model')
    row_spec = P(None, 'model', 'fsdp')
    ys, ms = mesh.shape['fsdp'], mesh.shape['model']

    def gather(block):
        full = lax.all_gather(block, ('fsdp', 'model'), axis=0, tiled=False)
        return full.reshape((ys, ms) + block.shape)

    def exchange(tokens):
        return lax.all_to_all(tokens, 'model', split_axis=0, concat_axis=0, tiled=True)

    def swap(block, axis, bit):
        return lax.ppermute(block, axis, [(i, i ^ bit) for i in range(mesh.shape[axis])])

    def spread(block):
        across = swap(block, 'model', 2)
        over, over_across = swap(block, 'fsdp', 1), swap(across, 'fsdp', 1)
        partners = [swap(b, 'model', 1) for b in (block, across, over, over_across)]
        return (block, partners[0], across, partners[1]), (over, partners[2], over_across, partners[3])

    def device_step(x_in, gain_attn, gain_mlp, rope_cos, rope_sin, w_q, w_k, w_v, w_o, w_gate, w_up, w_down):
        layers = w_q.shape[0]
        half = w_gate.shape[2] // 2
        place = jnp.stack([lax.axis_index('model'), lax.axis_index('fsdp')]).astype(jnp.int32)
        seqs = x_in.shape[0] // ms
        x = exchange(x_in)
        gathered = []
        for l in range(layers):
            block = jnp.concatenate([w_q[l], w_k[l], w_v[l]], axis=1)
            wqkv = gather(block)
            block = jnp.concatenate([w_gate[l, :, :half], w_up[l, :, :half], w_o[l]], axis=0)
            wgua = gather(block)
            block = jnp.concatenate([w_gate[l, :, half:], w_up[l, :, half:]], axis=0)
            wgub = gather(block)
            block = w_down[l]
            gathered.append((wqkv, wgua, wgub, spread(block)))

        chunk_shape = x.shape[:2]
        x = x.reshape(-1, x.shape[2])
        cos = jnp.tile(rope_cos, (1, 4))
        sin = jnp.tile(jnp.concatenate([-rope_sin, rope_sin], axis=1), (1, 2))
        wo_block = 2 * w_gate.shape[1] // w_o.shape[1]
        for l in range(layers):
            wqkv, wgua, wgub, (own, other) = gathered[l]
            q, k, v = project_qkv(x, gain_attn[l][None], cos, sin, wqkv)
            o = attend(q, k, v, ms, seqs)
            m = out_proj(o, wgua, wo_block, x)
            if l == layers - 1:
                m = exchange(m.reshape(chunk_shape + m.shape[1:])).reshape(m.shape)
            za = gate_up(m, gain_mlp[l][None], wgua, half)
            zb = gate_up(m, gain_mlp[l][None], wgub, half)
            x = down(place, za, zb, own, m, 0)
            x = down(place, za, zb, other, m, 1, x)
        return x.reshape(x_in.shape)

    return jax.shard_map(device_step, mesh=mesh, in_specs=(act_spec, P(), P(), P(), P(), col_spec, col_spec, col_spec, row_spec, col_spec, col_spec, row_spec), out_specs=act_spec, check_vma=False)
```

time: 1480 us -> 1570 us (1.061)
  waiting for transfers between devices: 425 us -> 503 us
  other arithmetic: 2.58 us -> 30 us
  local copies, waits for them, and re-layouts: 46.9 us -> 24.4 us
    ppermute x0 -> x14, waiting for transfers between devices: none -> 503 us  [swap(): lax.ppermute(block, axis, [(i, i ^ bit) for i in range(mesh.shape[axis])])]
    all_gather x17 -> x6, waiting for transfers between devices: 237 us -> 0.04 us  [gather(): full = lax.all_gather(block, ('fsdp', 'model'), axis=0, tiled=False)]
    all_to_all x5 -> x2, waiting for transfers between devices: 182 us -> 0.01 us  [exchange(): lax.all_to_all(tokens, 'model', split_axis=0, concat_axis=0, tiled=True)]
    concatenate x0 -> x4, other arithmetic: none -> 25.8 us  [the longest x2 16.9 us: device_step(): jnp.concatenate([w_gate[l, :, :half], w_up[l, :, :half], w_o[l]], axis=0)]
    slice x6 -> x1, local copies, waits for them, and re-layouts: 25 us -> 0.61 us  [device_step(): za = gate_up(m, gain_mlp[l][None], wgua, half)]
    squeeze x0 -> x3, local copies, waits for them, and re-layouts: none -> 18.4 us  [the longest x1 11.1 us: device_step(): block = jnp.concatenate([w_gate[l, :, half:], w_up[l, :, half:]], axis=0)]
    pallas_call x11 -> x10, Pallas kernels: 578 us -> 575 us  [the longest x4 325 us: gate_up(): pl.pallas_call(functools.partial(gate_up_kernel, chunk=512), grid=(ms * p...]
  transfers between devices with their start and end apart: 22 -> 22, of which waited for: 8 -> 4; matrix products, arithmetic and copies ran while one was open for 2% -> 3% of each run, Pallas kernels for 65% -> 59%
where the time goes in v2:
time: 1570 us; the launch traced here: 1560 us
  Pallas kernels  968 us (62%)
  waiting for transfers between devices  503 us (32%)
  other arithmetic  30 us (2%)
  local copies, waits for them, and re-layouts  24.4 us (2%)
  starting transfers between devices  22.4 us (1%)
    ppermute x14, waiting for transfers between devices, swap(): lax.ppermute(block, axis, [(i, i ^ bit) for i in range(mesh.shape[axis])])  503 us
    pallas_call x4, Pallas kernels, gate_up(): pl.pallas_call(functools.partial(gate_up_kernel, chunk=512), grid=(ms * p...  325 us
    pallas_call x2, Pallas kernels, attend(): pl.pallas_call(attention_kernel, grid=(seqs * blocks,), in_specs=[pl.Bloc...  306 us
    pallas_call x4, Pallas kernels, down(): pl.pallas_call(functools.partial(down_kernel, count=count, chunk=512), gr...  202 us
    pallas_call x2, Pallas kernels, project_qkv(): pl.pallas_call(qkv_kernel, grid=(blocks,), in_specs=[pl.BlockSpec((tokens...  86.4 us
    pallas_call x2, Pallas kernels, out_proj(): pl.pallas_call(functools.partial(out_proj_kernel, chunk=512), grid=(ys *...  48.3 us
  transfers between devices with their start and end apart: 22, of which 4 were waited for; matrix products, arithmetic and copies ran while one was open for 3% of the time, Pallas kernels for 59%

profile of v2, /device:TPU:0, one launch (start us, length us, event | category | flops | bytes accessed | tf_op | source)
XLA Modules:
  0.0 1561.6 jit_solution(5839981389301657069)
XLA Ops:
  6.5 1.8 slice_bitcast_fusion.11
  11.7 11.1 slice_bitcast_fusion.2
  22.8 11.2 pad_maximum_fusion
  34.0 4.8 pad_maximum_fusion.2
  38.9 2.2 pad_maximum_fusion.5
  41.2 5.7 pad_maximum_fusion.1
  47.0 6.1 slice_bitcast_fusion
  53.1 3.3 collective-permute-start.2
  56.4 5.6 all-to-all-start
  62.3 4.1 pad_maximum_fusion.3
  66.5 1.4 collective-permute-start
  67.9 153.2 %collective-permute-done.2.refs_10_ = bf16[2048,1024]{1,0:T(8,128)(2,1)} collective-permute-done((bf16[2048,1024]{1,0:T(8,128)(2,1)}, bf16[2048,1024]{1,0:T(8,128)(2,1)}, u32[]{:S(2)}, u32[]{:S(2)}) %collective-permute-start.2) | collective-permute-done | bytes 4194336 | tf_op jit(solution)/shard_map/ppermute | solution.py:294
  221.1 1.6 collective-permute-start.3
  227.7 168.9 %collective-permute-done.3.refs_10_ = bf16[2048,1024]{1,0:T(8,128)(2,1)} collective-permute-done((bf16[2048,1024]{1,0:T(8,128)(2,1)}, bf16[2048,1024]{1,0:T(8,128)(2,1)}, u32[]{:S(2)}, u32[]{:S(2)}) %collective-permute-start.3) | collective-permute-done | bytes 4194336 | tf_op jit(solution)/shard_map/ppermute | solution.py:294
  396.7 43.4 %qkv.2 = (bf16[2048,2048]{1,0:T(8,128)(2,1)}, bf16[2048,512]{1,0:T(8,128)(2,1)}, bf16[2048,512]{1,0:T(8,128)(2,1)}) custom-call(bf16[2048,2048]{1,0:T(8,128)(2,1)} %bitcast.2.x_ref.r_ref, f32[1,2048]{1,0:T(1,128)} %get-tuple-element.38.gain_ref, f32[1024,128]{1,0:T(8,128)} %copy.17.cos_ref, f32[1024,128]{1,0:T(8,128)} %copy.18.sin_ref, ...), custom_call_target="tpu_custom_call" | custom-call | flops 25769803776 | bytes 29360128 | tf_op jit(solution)/shard_map/qkv/pallas_call | solution.py:74
  440.1 152.9 %attention.2 = bf16[4,2,256,2048]{3,2,1,0:T(8,128)(2,1)} custom-call(bf16[4,2,256,2048]{3,2,1,0:T(8,128)(2,1)} %bitcast.76, bf16[4,2,256,512]{3,2,1,0:T(8,128)(2,1)} %bitcast.79, bf16[4,2,256,512]{3,2,1,0:T(8,128)(2,1)} %bitcast.80), custom_call_target="tpu_custom_call" | custom-call | flops 68719476736 | bytes 20971520 | tf_op jit(solution)/shard_map/attention/pallas_call | solution.py:144
  593.0 24.1 %out_proj.2.x_ref.refs_12_ = bf16[2048,2048]{1,0:T(8,128)(2,1)} custom-call(bf16[2048,2048]{1,0:T(8,128)(2,1)} %bitcast.65, bf16[2,4,2560,1024]{3,2,1,0:T(8,128)(2,1)} %bitcast.61, bf16[2048,2048]{1,0:T(8,128)(2,1)} %bitcast.2.x_ref.r_ref), custom_call_target="tpu_custom_call" | custom-call | flops 17179869184 | bytes 33554432 | tf_op jit(solution)/shard_map/out_proj/pallas_call | solution.py:179
  617.2 81.1 %shard_map.118.refs_0_.refs_1_.refs_2_.refs_3_ = bf16[2048,4096]{1,0:T(8,128)(2,1)} custom-call(bf16[2048,2048]{1,0:T(8,128)(2,1)} %out_proj.2.x_ref.refs_12_, f32[1,2048]{1,0:T(1,128)} %get-tuple-element.36.gain_ref, bf16[2,4,2560,1024]{3,2,1,0:T(8,128)(2,1)} %bitcast.62, bf16[2,4,2560,1024]{3,2,1,0:T(8,128)(2,1)} %bitcast.63), custom_call_target="tpu_custom_call" | custom-call | flops 68719476736 | bytes 41943040 | tf_op jit(solution)/shard_map/pallas_call | solution.py:216
  698.2 81.6 %shard_map.119.refs_4_.refs_5_.refs_6_.refs_7_ = bf16[2048,4096]{1,0:T(8,128)(2,1)} custom-call(bf16[2048,2048]{1,0:T(8,128)(2,1)} %out_proj.2.x_ref.refs_12_, f32[1,2048]{1,0:T(1,128)} %get-tuple-element.36.gain_ref, bf16[2,4,2048,1024]{3,2,1,0:T(8,128)(2,1)} %bitcast.71, bf16[2,4,2048,1024]{3,2,1,0:T(8,128)(2,1)} %bitcast.72), custom_call_target="tpu_custom_call" | custom-call | flops 68719476736 | bytes 41943040 | tf_op jit(solution)/shard_map/pallas_call | solution.py:216
  779.8 54.7 %down_own.2.refs_13_ = bf16[2048,2048]{1,0:T(8,128)(2,1)} custom-call(s32[2]{0:T(128)} %pad_add_fusion.place_ref, bf16[2048,4096]{1,0:T(8,128)(2,1)} %shard_map.118.refs_0_.refs_1_.refs_2_.refs_3_, bf16[2048,4096]{1,0:T(8,128)(2,1)} %shard_map.118.refs_0_.refs_1_.refs_2_.refs_3_, bf16[2048,4096]{1,0:T(8,128)(2,1)} %shard_map.118.refs_0_.refs_1_.refs_2_.refs_3_, ...), custom_call_target="tpu_custom_call" | custom-call | flops 34359738368 | bytes 50331648 | tf_op jit(solution)/shard_map/down_own/pallas_call | solution.py:264
  834.5 49.4 %down_other.2.x_ref.r_ref = bf16[2048,2048]{1,0:T(8,128)(2,1)} custom-call(s32[2]{0:T(128)} %pad_add_fusion.place_ref, bf16[2048,4096]{1,0:T(8,128)(2,1)} %shard_map.118.refs_0_.refs_1_.refs_2_.refs_3_, bf16[2048,4096]{1,0:T(8,128)(2,1)} %shard_map.118.refs_0_.refs_1_.refs_2_.refs_3_, ...), custom_call_target="tpu_custom_call", output_to_operand_aliasing={{}: (14, {})} | custom-call | flops 34359738368 | bytes 50331648 | tf_op jit(solution)/shard_map/down_other/pallas_call | solution.py:264
  883.9 43.1 %qkv.3 = (bf16[2048,2048]{1,0:T(8,128)(2,1)}, bf16[2048,512]{1,0:T(8,128)(2,1)}, bf16[2048,512]{1,0:T(8,128)(2,1)}) custom-call(bf16[2048,2048]{1,0:T(8,128)(2,1)} %down_other.2.x_ref.r_ref, f32[1,2048]{1,0:T(1,128)} %get-tuple-element.37.gain_ref, f32[1024,128]{1,0:T(8,128)} %copy.17.cos_ref, f32[1024,128]{1,0:T(8,128)} %copy.18.sin_ref, ...), custom_call_target="tpu_custom_call" | custom-call | flops 25769803776 | bytes 29360128 | tf_op jit(solution)/shard_map/qkv/pallas_call | solution.py:74
  927.0 153.3 %attention.3 = bf16[4,2,256,2048]{3,2,1,0:T(8,128)(2,1)} custom-call(bf16[4,2,256,2048]{3,2,1,0:T(8,128)(2,1)} %bitcast.75, bf16[4,2,256,512]{3,2,1,0:T(8,128)(2,1)} %bitcast.77, bf16[4,2,256,512]{3,2,1,0:T(8,128)(2,1)} %bitcast.78), custom_call_target="tpu_custom_call" | custom-call | flops 68719476736 | bytes 20971520 | tf_op jit(solution)/shard_map/attention/pallas_call | solution.py:144
  1080.3 24.1 %out_proj.3 = bf16[2048,2048]{1,0:T(8,128)(2,1)} custom-call(bf16[2048,2048]{1,0:T(8,128)(2,1)} %bitcast.66, bf16[2,4,2560,1024]{3,2,1,0:T(8,128)(2,1)} %bitcast.58, bf16[2048,2048]{1,0:T(8,128)(2,1)} %down_other.2.x_ref.r_ref), custom_call_target="tpu_custom_call" | custom-call | flops 17179869184 | bytes 33554432 | tf_op jit(solution)/shard_map/out_proj/pallas_call | solution.py:179
  1104.5 5.8 all-to-all-start.1
  1110.3 2.6 collective-permute-start.7
  1113.5 91.2 %collective-permute-done.7.refs_8_ = bf16[2048,1024]{1,0:T(8,128)(2,1)} collective-permute-done((bf16[2048,1024]{1,0:T(8,128)(2,1)}, bf16[2048,1024]{1,0:T(8,128)(2,1)}, u32[]{:S(2)}, u32[]{:S(2)}) %collective-permute-start.7) | collective-permute-done | bytes 4194336 | tf_op jit(solution)/shard_map/ppermute | solution.py:294
  1204.7 89.7 %collective-permute-done.10.refs_10_ = bf16[2048,1024]{1,0:T(8,128)(2,1)} collective-permute-done((bf16[2048,1024]{1,0:T(8,128)(2,1)}, bf16[2048,1024]{1,0:T(8,128)(2,1)}, u32[]{:S(2)}, u32[]{:S(2)}) %collective-permute-start.10) | collective-permute-done | bytes 4194336 | tf_op jit(solution)/shard_map/ppermute | solution.py:294
  1294.4 80.9 %shard_map.120.refs_0_.refs_1_.refs_2_.refs_3_ = bf16[2048,4096]{1,0:T(8,128)(2,1)} custom-call(bf16[2048,2048]{1,0:T(8,128)(2,1)} %bitcast.34.x_ref.refs_12_, f32[1,2048]{1,0:T(1,128)} %get-tuple-element.35.gain_ref, bf16[2,4,2560,1024]{3,2,1,0:T(8,128)(2,1)} %bitcast.59, bf16[2,4,2560,1024]{3,2,1,0:T(8,128)(2,1)} %bitcast.60), custom_call_target="tpu_custom_call" | custom-call | flops 68719476736 | bytes 41943040 | tf_op jit(solution)/shard_map/pallas_call | solution.py:216
  1375.3 81.2 %shard_map.121.refs_4_.refs_5_.refs_6_.refs_7_ = bf16[2048,4096]{1,0:T(8,128)(2,1)} custom-call(bf16[2048,2048]{1,0:T(8,128)(2,1)} %bitcast.34.x_ref.refs_12_, f32[1,2048]{1,0:T(1,128)} %get-tuple-element.35.gain_ref, bf16[2,4,2048,1024]{3,2,1,0:T(8,128)(2,1)} %bitcast.69, bf16[2,4,2048,1024]{3,2,1,0:T(8,128)(2,1)} %bitcast.70), custom_call_target="tpu_custom_call" | custom-call | flops 68719476736 | bytes 41943040 | tf_op jit(solution)/shard_map/pallas_call | solution.py:216
  1456.4 48.8 %down_own.3.refs_13_ = bf16[2048,2048]{1,0:T(8,128)(2,1)} custom-call(s32[2]{0:T(128)} %pad_add_fusion.place_ref, bf16[2048,4096]{1,0:T(8,128)(2,1)} %shard_map.120.refs_0_.refs_1_.refs_2_.refs_3_, bf16[2048,4096]{1,0:T(8,128)(2,1)} %shard_map.120.refs_0_.refs_1_.refs_2_.refs_3_, bf16[2048,4096]{1,0:T(8,128)(2,1)} %shard_map.120.refs_0_.refs_1_.refs_2_.refs_3_, ...), custom_call_target="tpu_custom_call" | custom-call | flops 34359738368 | bytes 50331648 | tf_op jit(solution)/shard_map/down_own/pallas_call | solution.py:264
  1505.2 49.0 %down_other.3 = bf16[2048,2048]{1,0:T(8,128)(2,1)} custom-call(s32[2]{0:T(128)} %pad_add_fusion.place_ref, bf16[2048,4096]{1,0:T(8,128)(2,1)} %shard_map.120.refs_0_.refs_1_.refs_2_.refs_3_, bf16[2048,4096]{1,0:T(8,128)(2,1)} %shard_map.120.refs_0_.refs_1_.refs_2_.refs_3_, ...), custom_call_target="tpu_custom_call", output_to_operand_aliasing={{}: (14, {})} | custom-call | flops 34359738368 | bytes 50331648 | tf_op jit(solution)/shard_map/down_other/pallas_call | solution.py:264
  (68 shorter events, 9.5 us)
Async XLA Ops:
  6.5 390.2 %all-gather.13.cloned.1.call-start = ((), (), s32[]{:S(2)}) async-start(), calls=%async_computation.2 | async-start | bytes 14155776 | tf_op jit(solution)/shard_map/all_gather | solution.py:287
  6.5 1.8 copy-start.3
  6.5 1.8 copy-start.4
  8.4 2.2 copy-start.1
  10.5 582.5 %all-gather.15.cloned.1.call-start = ((), (), s32[]{:S(2)}) async-start(), calls=%async_computation.3 | async-start | bytes 47185920 | tf_op jit(solution)/shard_map/all_gather | solution.py:287
  34.0 664.2 %all-gather.17.cloned.1.call-start = ((), (), s32[]{:S(2)}) async-start(), calls=%async_computation.4 | async-start | bytes 37748736 | tf_op jit(solution)/shard_map/all_gather | solution.py:287
  38.9 845.0 %all-gather.19.cloned.1.call-start = ((), (), s32[]{:S(2)}) async-start(), calls=%async_computation.5 | async-start | bytes 14155776 | tf_op jit(solution)/shard_map/all_gather | solution.py:287
  41.2 1039.1 %all-gather.21.cloned.1.call-start = ((), (), s32[]{:S(2)}) async-start(), calls=%async_computation.6 | async-start | bytes 47185920 | tf_op jit(solution)/shard_map/all_gather | solution.py:287
  53.1 9.2 copy-start
  53.1 168.0 %collective-permute-start.2 = (bf16[2048,1024]{1,0:T(8,128)(2,1)}, bf16[2048,1024]{1,0:T(8,128)(2,1)}, u32[]{:S(2)}, u32[]{:S(2)}) collective-permute-start(bf16[2048,1024]{1,0:T(8,128)(2,1)} %get-tuple-element.18.refs_8_), channel_id=1, source_target_pairs={{0,2},{1,3},{2,0},{3,1},{4,6},{5,7},{6,4},{7,5}} | collective-permute-start | bytes 12582920 | tf_op jit(solution)/shard_map/ppermute | solution.py:294
  56.4 340.3 %all-to-all-start = ((bf16[8,256,2048]{2,1,0:T(8,128)(2,1)}), bf16[8,256,2048]{2,1,0:T(8,128)(2,1)}, u32[]{:S(2)}, u32[]{:S(2)}) async-start(bf16[8,256,2048]{2,1,0:T(8,128)(2,1)} %param.12), calls=%async_computation | async-start | bytes 16777216 | tf_op jit(solution)/shard_map/all_to_all | solution.py:291
  62.1 1313.2 %all-gather.23.cloned.1.call-start = ((), (), s32[]{:S(2)}) async-start(), calls=%async_computation.7 | async-start | bytes 37748736 | tf_op jit(solution)/shard_map/all_gather | solution.py:287
  66.4 156.8 %copy-start.5 = (f32[1024,32]{0,1:T(8,128)S(1)}, f32[1024,32]{0,1:T(8,128)}, u32[]{:S(2)}) copy-start(f32[1024,32]{0,1:T(8,128)} %param.15) | copy-start | bytes 393220
  66.4 157.8 %copy-start.2 = (f32[1024,32]{0,1:T(8,128)S(1)}, f32[1024,32]{0,1:T(8,128)}, u32[]{:S(2)}) copy-start(f32[1024,32]{0,1:T(8,128)} %param.16) | copy-start | bytes 393220
  66.4 159.5 %copy-start.6 = (f32[2,2048]{1,0:T(2,128)S(1)}, f32[2,2048]{1,0:T(2,128)}, u32[]{:S(2)}) copy-start(f32[2,2048]{1,0:T(2,128)} %param.13) | copy-start | bytes 49156
  66.5 160.2 %copy-start.7 = (f32[2,2048]{1,0:T(2,128)S(1)}, f32[2,2048]{1,0:T(2,128)}, u32[]{:S(2)}) copy-start(f32[2,2048]{1,0:T(2,128)} %param.14) | copy-start | bytes 49156
  66.5 161.0 %collective-permute-start = (bf16[2048,1024]{1,0:T(8,128)(2,1)}, bf16[2048,1024]{1,0:T(8,128)(2,1)}, u32[]{:S(2)}, u32[]{:S(2)}) collective-permute-start(bf16[2048,1024]{1,0:T(8,128)(2,1)} %get-tuple-element.18.refs_8_), channel_id=1, source_target_pairs={{0,4},{4,0},{1,5},{5,1},{2,6},{6,2},{3,7},{7,3}} | collective-permute-start | bytes 12582920 | tf_op jit(solution)/shard_map/ppermute | solution.py:294
  221.1 175.6 %collective-permute-start.3 = (bf16[2048,1024]{1,0:T(8,128)(2,1)}, bf16[2048,1024]{1,0:T(8,128)(2,1)}, u32[]{:S(2)}, u32[]{:S(2)}) collective-permute-start(bf16[2048,1024]{1,0:T(8,128)(2,1)} %collective-permute-done.2.refs_10_), channel_id=1, source_target_pairs={{0,4},{4,0},{1,5},{5,1},{2,6},{6,2},{3,7},{7,3}} | collective-permute-start | bytes 12582920 | tf_op jit(solution)/shard_map/ppermute | solution.py:294
  222.7 557.1 %collective-permute-start.5 = (bf16[2048,1024]{1,0:T(8,128)(2,1)}, bf16[2048,1024]{1,0:T(8,128)(2,1)}, u32[]{:S(2)}, u32[]{:S(2)}) collective-permute-start(bf16[2048,1024]{1,0:T(8,128)(2,1)} %get-tuple-element.18.refs_8_), channel_id=1, source_target_pairs={{0,1},{1,0},{2,3},{3,2},{4,5},{5,4},{6,7},{7,6}} | collective-permute-start | bytes 12582920 | tf_op jit(solution)/shard_map/ppermute | solution.py:294
  222.7 890.2 %collective-permute-start.9 = (bf16[2048,1024]{1,0:T(8,128)(2,1)}, bf16[2048,1024]{1,0:T(8,128)(2,1)}, u32[]{:S(2)}, u32[]{:S(2)}) collective-permute-start(bf16[2048,1024]{1,0:T(8,128)(2,1)} %get-tuple-element.17.refs_8_), channel_id=1, source_target_pairs={{0,2},{1,3},{2,0},{3,1},{4,6},{5,7},{6,4},{7,5}} | collective-permute-start | bytes 12582920 | tf_op jit(solution)/shard_map/ppermute | solution.py:294
  227.2 552.6 %collective-permute-start.6 = (bf16[2048,1024]{1,0:T(8,128)(2,1)}, bf16[2048,1024]{1,0:T(8,128)(2,1)}, u32[]{:S(2)}, u32[]{:S(2)}) collective-permute-start(bf16[2048,1024]{1,0:T(8,128)(2,1)} %collective-permute-done.2.refs_10_), channel_id=1, source_target_pairs={{0,1},{1,0},{2,3},{3,2},{4,5},{5,4},{6,7},{7,6}} | collective-permute-start | bytes 12582920 | tf_op jit(solution)/shard_map/ppermute | solution.py:294
  227.5 607.0 %collective-permute-start.1 = (bf16[2048,1024]{1,0:T(8,128)(2,1)}, bf16[2048,1024]{1,0:T(8,128)(2,1)}, u32[]{:S(2)}, u32[]{:S(2)}) collective-permute-start(bf16[2048,1024]{1,0:T(8,128)(2,1)} %collective-permute-done.refs_8_), channel_id=1, source_target_pairs={{0,1},{1,0},{2,3},{3,2},{4,5},{5,4},{6,7},{7,6}} | collective-permute-start | bytes 12582920 | tf_op jit(solution)/shard_map/ppermute | solution.py:294
  396.7 437.8 %collective-permute-start.4 = (bf16[2048,1024]{1,0:T(8,128)(2,1)}, bf16[2048,1024]{1,0:T(8,128)(2,1)}, u32[]{:S(2)}, u32[]{:S(2)}) collective-permute-start(bf16[2048,1024]{1,0:T(8,128)(2,1)} %collective-permute-done.3.refs_10_), channel_id=1, source_target_pairs={{0,1},{1,0},{2,3},{3,2},{4,5},{5,4},{6,7},{7,6}} | collective-permute-start | bytes 12582920 | tf_op jit(solution)/shard_map/ppermute | solution.py:294
  1104.5 189.9 %all-to-all-start.1 = ((bf16[8,256,2048]{2,1,0:T(8,128)(2,1)}), bf16[8,256,2048]{2,1,0:T(8,128)(2,1)}, u32[]{:S(2)}, u32[]{:S(2)}) async-start(bf16[8,256,2048]{2,1,0:T(8,128)(2,1)} %bitcast.64), calls=%async_computation.1 | async-start | bytes 16777216 | tf_op jit(solution)/shard_map/all_to_all | solution.py:291
  1110.3 94.3 %collective-permute-start.7 = (bf16[2048,1024]{1,0:T(8,128)(2,1)}, bf16[2048,1024]{1,0:T(8,128)(2,1)}, u32[]{:S(2)}, u32[]{:S(2)}) collective-permute-start(bf16[2048,1024]{1,0:T(8,128)(2,1)} %get-tuple-element.17.refs_8_), channel_id=1, source_target_pairs={{0,4},{4,0},{1,5},{5,1},{2,6},{6,2},{3,7},{7,3}} | collective-permute-start | bytes 12582920 | tf_op jit(solution)/shard_map/ppermute | solution.py:294
  1112.9 181.4 %collective-permute-start.10 = (bf16[2048,1024]{1,0:T(8,128)(2,1)}, bf16[2048,1024]{1,0:T(8,128)(2,1)}, u32[]{:S(2)}, u32[]{:S(2)}) collective-permute-start(bf16[2048,1024]{1,0:T(8,128)(2,1)} %collective-permute-done.9.refs_10_), channel_id=1, source_target_pairs={{0,4},{4,0},{1,5},{5,1},{2,6},{6,2},{3,7},{7,3}} | collective-permute-start | bytes 12582920 | tf_op jit(solution)/shard_map/ppermute | solution.py:294
  1113.0 343.5 %collective-permute-start.12 = (bf16[2048,1024]{1,0:T(8,128)(2,1)}, bf16[2048,1024]{1,0:T(8,128)(2,1)}, u32[]{:S(2)}, u32[]{:S(2)}) collective-permute-start(bf16[2048,1024]{1,0:T(8,128)(2,1)} %get-tuple-element.17.refs_8_), channel_id=1, source_target_pairs={{0,1},{1,0},{2,3},{3,2},{4,5},{5,4},{6,7},{7,6}} | collective-permute-start | bytes 12582920 | tf_op jit(solution)/shard_map/ppermute | solution.py:294
  1113.2 343.3 %collective-permute-start.13 = (bf16[2048,1024]{1,0:T(8,128)(2,1)}, bf16[2048,1024]{1,0:T(8,128)(2,1)}, u32[]{:S(2)}, u32[]{:S(2)}) collective-permute-start(bf16[2048,1024]{1,0:T(8,128)(2,1)} %collective-permute-done.9.refs_10_), channel_id=1, source_target_pairs={{0,1},{1,0},{2,3},{3,2},{4,5},{5,4},{6,7},{7,6}} | collective-permute-start | bytes 12582920 | tf_op jit(solution)/shard_map/ppermute | solution.py:294
  1204.7 300.6 %collective-permute-start.8 = (bf16[2048,1024]{1,0:T(8,128)(2,1)}, bf16[2048,1024]{1,0:T(8,128)(2,1)}, u32[]{:S(2)}, u32[]{:S(2)}) collective-permute-start(bf16[2048,1024]{1,0:T(8,128)(2,1)} %collective-permute-done.7.refs_8_), channel_id=1, source_target_pairs={{0,1},{1,0},{2,3},{3,2},{4,5},{5,4},{6,7},{7,6}} | collective-permute-start | bytes 12582920 | tf_op jit(solution)/shard_map/ppermute | solution.py:294
  1294.3 210.9 %collective-permute-start.11 = (bf16[2048,1024]{1,0:T(8,128)(2,1)}, bf16[2048,1024]{1,0:T(8,128)(2,1)}, u32[]{:S(2)}, u32[]{:S(2)}) collective-permute-start(bf16[2048,1024]{1,0:T(8,128)(2,1)} %collective-permute-done.10.refs_10_), channel_id=1, source_target_pairs={{0,1},{1,0},{2,3},{3,2},{4,5},{5,4},{6,7},{7,6}} | collective-permute-start | bytes 12582920 | tf_op jit(solution)/shard_map/ppermute | solution.py:294
Sparse Core Ops, SparseCore 0:
  10.6 88.9 all-gather.12
  101.4 357.4 all-gather.14
  460.7 198.3 all-gather.16
  660.8 66.4 all-gather.18
  728.9 191.4 all-gather.20
  922.1 155.2 all-gather.22

commit v3 on v2

v3 whole, which is shorter than its diff:
```python
import functools
import math

import jax
import jax.numpy as jnp
from jax import lax
from jax.experimental import pallas as pl
from jax.experimental.pallas import tpu as pltpu
from jax.sharding import PartitionSpec as P


EPS = 1e-5
VMEM = 60 * 1024 * 1024
F32 = jnp.float32
BF16 = jnp.bfloat16


def dot(a, b):
    return jnp.dot(a, b, preferred_element_type=F32)


def params():
    return pltpu.CompilerParams(dimension_semantics=("arbitrary",), vmem_limit_bytes=VMEM)


def normalise(x_ref, gain_ref, h_ref, chunk):
    def step(i, carry):
        rows = pl.ds(pl.multiple_of(i * chunk, chunk), chunk)
        x = x_ref[rows, :].astype(F32)
        mean_sq = jnp.mean(x * x, axis=-1, keepdims=True)
        h_ref[rows, :] = (x * lax.rsqrt(mean_sq + EPS) * gain_ref[...]).astype(BF16)
        return carry

    lax.fori_loop(0, x_ref.shape[0] // chunk, step, 0)


def rotate(x, cos, sin):
    lane = lax.broadcasted_iota(jnp.int32, x.shape, 1)
    swapped = jnp.where(lane % 64 < 32, pltpu.roll(x, 96, 1), pltpu.roll(x, 32, 1))
    return x * cos + swapped * sin


def qkv_kernel(x_ref, gain_ref, cos_ref, sin_ref, w_ref, q_ref, k_ref, v_ref, h_ref):
    @pl.when(pl.program_id(0) == 0)
    def _():
        normalise(x_ref, gain_ref, h_ref, 128)

    w = w_ref[...].reshape(w_ref.shape[0] * w_ref.shape[2], w_ref.shape[3])
    q_width, k_width = q_ref.shape[1], k_ref.shape[1]
    positions = 256
    step = 2 * positions
    for r in range(0, h_ref.shape[0], step):
        rows = slice(r, r + step)
        out = dot(h_ref[rows, :], w).astype(BF16)
        table = slice(r // 2, r // 2 + positions)
        cos, sin = cos_ref[table, :], sin_ref[table, :]
        cos, sin = jnp.concatenate([cos, cos], axis=0), jnp.concatenate([sin, sin], axis=0)
        for c in range(0, q_width, 128):
            q_ref[rows, c:c + 128] = rotate(out[:, c:c + 128].astype(F32), cos, sin).astype(BF16)
        for c in range(0, k_width, 128):
            k_ref[rows, c:c + 128] = rotate(out[:, q_width + c:q_width + c + 128].astype(F32), cos, sin).astype(BF16)
        v_ref[rows, :] = out[:, q_width + k_width:]


def project_qkv(x, gain, cos, sin, w):
    tokens, width = x.shape
    q_width, k_width = 512, 128
    blocks = w.shape[1]
    flops = 2 * tokens * width * blocks * w.shape[3]
    return pl.pallas_call(
        qkv_kernel,
        grid=(blocks,),
        in_specs=[
            pl.BlockSpec((tokens, width), lambda m: (0, 0)),
            pl.BlockSpec((1, width), lambda m: (0, 0)),
            pl.BlockSpec(cos.shape, lambda m: (0, 0)),
            pl.BlockSpec(sin.shape, lambda m: (0, 0)),
            pl.BlockSpec((w.shape[0], 1, w.shape[2], w.shape[3]), lambda m: (0, m, 0, 0)),
        ],
        out_specs=[
            pl.BlockSpec((tokens, q_width), lambda m: (0, m)),
            pl.BlockSpec((tokens, k_width), lambda m: (0, m)),
            pl.BlockSpec((tokens, k_width), lambda m: (0, m)),
        ],
        out_shape=[
            jax.ShapeDtypeStruct((tokens, blocks * q_width), BF16),
            jax.ShapeDtypeStruct((tokens, blocks * k_width), BF16),
            jax.ShapeDtypeStruct((tokens, blocks * k_width), BF16),
        ],
        scratch_shapes=[pltpu.VMEM((tokens, width), BF16)],
        compiler_params=params(),
        cost_estimate=pl.CostEstimate(flops=flops, bytes_accessed=4 * tokens * width + 2 * w.size, transcendentals=0),
        name="qkv",
    )(x, gain, cos, sin, w)


def attention_kernel(q_ref, k_ref, v_ref, o_ref, ks, vs):
    chunks, _, chunk, _ = q_ref.shape
    lo = lax.broadcasted_iota(jnp.int32, (chunk, 128), 1) < 64
    for c in range(chunks):
        rows = slice(c * chunk, (c + 1) * chunk)
        keys = k_ref[c, 0].astype(F32).T.astype(BF16)
        values = v_ref[c, 0].astype(F32)
        swapped = pltpu.roll(values, 64, 1)
        for g in range(2):
            key = keys[64 * g:64 * g + 64, :]
            ks[g, :, rows] = jnp.concatenate([key, key], axis=0)
            first, second = (swapped, values) if g else (values, swapped)
            vs[g, 0, rows, :] = jnp.where(lo, first, 0.0).astype(BF16)
            vs[g, 1, rows, :] = jnp.where(lo, 0.0, second).astype(BF16)
    scale = 64 ** -0.5 * math.log2(math.e)
    row = lax.broadcasted_iota(jnp.int32, (4 * chunk, chunk), 0) % chunk
    col = lax.broadcasted_iota(jnp.int32, (4 * chunk, chunk), 1)
    causal = row >= col

    def group(g, carry):
        for b in range(chunks):
            n = (b + 1) * chunk
            heads = []
            for p in range(2):
                pair = q_ref[b, 0, :, pl.ds(pl.multiple_of(g * 256 + p * 128, 128), 128)].astype(F32)
                heads += [jnp.where(lo, pair, 0.0).astype(BF16), jnp.where(lo, 0.0, pair).astype(BF16)]
            q = jnp.concatenate(heads, axis=0)
            parts = [dot(q, ks[g, :, c * chunk:(c + 1) * chunk]) for c in range(b + 1)]
            parts[b] = jnp.where(causal, parts[b], -jnp.inf)
            top = jnp.max(functools.reduce(jnp.maximum, parts), axis=1, keepdims=True)
            parts = [jnp.exp2((part - top) * scale) for part in parts]
            inverse = 1.0 / jnp.sum(functools.reduce(jnp.add, parts), axis=1, keepdims=True)
            probs = [(part * inverse).astype(BF16) for part in parts]
            values = jnp.concatenate([vs[g, 0, :n, :], vs[g, 1, :n, :]], axis=0)
            for p in range(2):
                even, odd = 2 * p * chunk, (2 * p + 1) * chunk
                pair = jnp.concatenate([x[even:even + chunk] for x in probs] + [x[odd:odd + chunk] for x in probs], axis=1)
                o_ref[b, 0, :, pl.ds(pl.multiple_of(g * 256 + p * 128, 128), 128)] = dot(pair, values).astype(BF16)
        return carry

    lax.fori_loop(0, 2, group, 0)


def attend(q, k, v, chunks, seqs, only):
    tokens = q.shape[0]
    chunk = tokens // (chunks * seqs)
    q4, k4, v4 = (a.reshape(chunks, seqs, chunk, a.shape[1]) for a in (q, k, v))
    seq = chunks * chunk
    blocks = k.shape[1] // 128
    q_width = q.shape[1] // blocks
    heads = q.shape[1] // 64
    count = seqs if only is None else 1
    first = only or 0
    out = pl.pallas_call(
        attention_kernel,
        grid=(count * blocks,),
        in_specs=[
            pl.BlockSpec((chunks, 1, chunk, width), lambda i: (0, first + i // blocks, 0, i % blocks))
            for width in (q_width, 128, 128)
        ],
        out_specs=pl.BlockSpec((chunks, 1, chunk, q_width), lambda i: (0, i // blocks, 0, i % blocks)),
        out_shape=jax.ShapeDtypeStruct((chunks, count, chunk, q.shape[1]), BF16),
        scratch_shapes=[
            pltpu.VMEM((2, 128, seq), BF16),
            pltpu.VMEM((2, 2, seq, 128), BF16),
        ],
        compiler_params=params(),
        cost_estimate=pl.CostEstimate(flops=8 * count * heads * seq * seq * 64, bytes_accessed=5 * count * seq * q.shape[1], transcendentals=count * heads * seq * seq),
    )(q4, k4, v4)
    return out.reshape(count * seq, q.shape[1])


def out_proj_kernel(a_ref, w_ref, r_ref, o_ref, *, chunk):
    w = w_ref[0].reshape(a_ref.shape[1], w_ref.shape[3])
    resid = r_ref[...].reshape(o_ref.shape)
    for r in range(0, a_ref.shape[0], chunk):
        acc = dot(a_ref[r:r + chunk, :], w)
        o_ref[r:r + chunk, :] = (resid[r:r + chunk, :].astype(F32) + acc).astype(BF16)


def out_proj(a, w, row_block, resid, only):
    tokens, depth = a.shape
    ys, ms, _, cols = w.shape
    block = 512
    per = cols // block
    chunks, seqs, chunk, _ = resid.shape
    count = seqs if only is None else 1
    first = only or 0
    return pl.pallas_call(
        functools.partial(out_proj_kernel, chunk=512),
        grid=(ys * per,),
        in_specs=[
            pl.BlockSpec((tokens, depth), lambda i: (0, 0)),
            pl.BlockSpec((1, ms, depth // ms, block), lambda i: (i // per, 0, row_block, i % per)),
            pl.BlockSpec((chunks, count, chunk, block), lambda i: (0, first, 0, i)),
        ],
        out_specs=pl.BlockSpec((tokens, block), lambda i: (0, i)),
        out_shape=jax.ShapeDtypeStruct((tokens, ys * cols), BF16),
        compiler_params=params(),
        cost_estimate=pl.CostEstimate(flops=2 * tokens * depth * ys * cols, bytes_accessed=6 * a.size + 2 * depth * ys * cols, transcendentals=0),
    )(a, w, resid)


def gate_up_kernel(x_ref, gain_ref, wg_ref, wu_ref, *refs, chunk):
    z_ref, h_ref = refs[-2:]

    @pl.when(pl.program_id(0) == 0)
    def _():
        normalise(x_ref, gain_ref, h_ref, 128)

    depth = wg_ref.shape[0] * wg_ref.shape[2]
    wg = wg_ref[...].reshape(depth, wg_ref.shape[3])
    wu = wu_ref[...].reshape(depth, wu_ref.shape[3])
    for r in range(0, h_ref.shape[0], chunk):
        h = h_ref[r:r + chunk, :]
        gate = dot(h, wg)
        up = dot(h, wu)
        z_ref[r:r + chunk, :] = (gate * jax.nn.sigmoid(gate) * up).astype(BF16)


def gate_up(x, gain, w, hidden, parts=1, part=0, onto=None):
    tokens, width = x.shape
    ys, ms = w.shape[:2]
    rows = width // ys
    block = 512
    per = hidden // block
    in_specs = [
        pl.BlockSpec((tokens, width), lambda i: (0, 0)),
        pl.BlockSpec((1, width), lambda i: (0, 0)),
        pl.BlockSpec((ys, 1, rows, block), lambda i: (0, i // per, 0, i % per)),
        pl.BlockSpec((ys, 1, rows, block), lambda i: (0, i // per, 1, i % per)),
    ]
    operands = [x, gain, w, w]
    aliases = {}
    if onto is not None:
        in_specs.append(pl.BlockSpec(memory_space=pl.ANY))
        operands.append(onto)
        aliases = {4: 0}
    return pl.pallas_call(
        functools.partial(gate_up_kernel, chunk=512),
        grid=(ms * per,),
        in_specs=in_specs,
        out_specs=pl.BlockSpec((tokens, block), lambda i: (part, i)),
        out_shape=jax.ShapeDtypeStruct((parts * tokens, ms * hidden), BF16),
        scratch_shapes=[pltpu.VMEM((tokens, width), BF16)],
        input_output_aliases=aliases,
        compiler_params=params(),
        cost_estimate=pl.CostEstimate(flops=4 * tokens * width * ms * hidden, bytes_accessed=2 * x.size + 4 * width * ms * hidden, transcendentals=tokens * ms * hidden),
    )(*operands)


def down_kernel(place_ref, *refs, count, resids, steps, chunk):
    za, zb, ws = refs[:count], refs[count:2 * count], refs[2 * count:3 * count]
    r_refs, o_ref = refs[3 * count:3 * count + resids], refs[-1]
    half = za[0].shape[1]
    w = jnp.concatenate([w[h * half:(h + 1) * half, :] for h in range(2) for w in ws], axis=0)
    for r in range(0, za[0].shape[0], chunk):
        rows = slice(r, r + chunk)
        z = jnp.concatenate([z[rows, :] for z in za + zb], axis=1)
        resid = r_refs[0][rows, :].astype(F32)
        if resids == 2:
            resid = jnp.where(pl.program_id(0) < steps, resid, r_refs[1][rows, :].astype(F32))
        out = (resid + dot(z, w)).astype(BF16)
        if len(o_ref.shape) == 4:
            positions = o_ref.shape[2]
            o_ref[r // positions:(r + chunk) // positions, 0] = out.reshape(chunk // positions, positions, out.shape[1])
        else:
            o_ref[rows, :] = out


def down(place, za, zb, ws, resids, other, split, onto=None):
    tokens = za.shape[0]
    width = resids[0].shape[1]
    count = len(ws)
    half = za.shape[1] // count
    cols = ws[0].shape[1]
    block, rows = 256, 1024
    per = cols // block

    def column(i, place):
        return (place[1] ^ other) * per + i % per

    z_specs = [pl.BlockSpec((rows, half), lambda i, place, k=k: (i // per, place[0] ^ k)) for k in range(count)]
    in_specs = z_specs + z_specs
    in_specs += [pl.BlockSpec((2 * half, block), lambda i, place: (0, i % per))] * count
    if len(resids) == 1:
        in_specs += [pl.BlockSpec((rows, block), lambda i, place: (i // per, column(i, place)))]
    else:
        in_specs += [pl.BlockSpec((rows, block), lambda i, place: (0, column(i, place)))] * len(resids)
    operands = [za] * count + [zb] * count + list(ws) + list(resids)
    aliases = {}
    if onto is not None:
        in_specs.append(pl.BlockSpec(memory_space=pl.ANY))
        aliases = {1 + len(operands): 0}
        operands.append(onto)
    if split:
        out_spec = pl.BlockSpec((split, 1, rows // split, block), lambda i, place: (0, i // per, 0, column(i, place)))
        out_shape = (split, tokens // rows, rows // split, width)
    else:
        out_spec = pl.BlockSpec((rows, block), lambda i, place: (i // per, column(i, place)))
        out_shape = (tokens, width)
    return pl.pallas_call(
        functools.partial(down_kernel, count=count, resids=len(resids), steps=per, chunk=512),
        grid_spec=pltpu.PrefetchScalarGridSpec(
            num_scalar_prefetch=1,
            grid=(tokens // rows * per,),
            in_specs=in_specs,
            out_specs=out_spec,
        ),
        out_shape=jax.ShapeDtypeStruct(out_shape, BF16),
        input_output_aliases=aliases,
        compiler_params=params(),
        cost_estimate=pl.CostEstimate(flops=4 * tokens * za.shape[1] * cols, bytes_accessed=4 * za.size + 4 * za.shape[1] * cols, transcendentals=0),
        name="down_other" if other else "down_own",
    )(place, *operands)


def solution(mesh):
    act_spec = P('fsdp', 'model', None)
    col_spec = P(None, 'fsdp', 'model')
    row_spec = P(None, 'model', 'fsdp')
    ys, ms = mesh.shape['fsdp'], mesh.shape['model']

    def gather(block):
        full = lax.all_gather(block, ('fsdp', 'model'), axis=0, tiled=False)
        return full.reshape((ys, ms) + block.shape)

    def exchange(tokens):
        return lax.all_to_all(tokens, 'model', split_axis=0, concat_axis=0, tiled=True)

    def swap(block, axis, bit):
        return lax.ppermute(block, axis, [(i, i ^ bit) for i in range(mesh.shape[axis])])

    def spread(block):
        across = swap(block, 'model', 2)
        over, over_across = swap(block, 'fsdp', 1), swap(across, 'fsdp', 1)
        partners = [swap(b, 'model', 1) for b in (block, across, over, over_across)]
        return (block, partners[0], across, partners[1]), (over, partners[2], over_across, partners[3])

    def device_step(x_in, gain_attn, gain_mlp, rope_cos, rope_sin, w_q, w_k, w_v, w_o, w_gate, w_up, w_down):
        layers = w_q.shape[0]
        half = w_gate.shape[2] // 2
        place = jnp.stack([lax.axis_index('model'), lax.axis_index('fsdp')]).astype(jnp.int32)
        seqs = x_in.shape[0] // ms
        x = exchange(x_in)
        gathered = []
        for l in range(layers):
            block = jnp.concatenate([w_q[l], w_k[l], w_v[l]], axis=1)
            wqkv = gather(block)
            block = jnp.concatenate([w_gate[l, :, :half], w_up[l, :, :half], w_o[l]], axis=0)
            wgua = gather(block)
            block = jnp.concatenate([w_gate[l, :, half:], w_up[l, :, half:]], axis=0)
            wgub = gather(block)
            block = w_down[l]
            gathered.append((wqkv, wgua, wgub, spread(block)))

        x = x.reshape(-1, x.shape[2])
        cos = jnp.tile(rope_cos, (1, 4))
        sin = jnp.tile(jnp.concatenate([-rope_sin, rope_sin], axis=1), (1, 2))
        wo_block = 2 * w_gate.shape[1] // w_o.shape[1]
        for l in range(layers):
            wqkv, wgua, wgub, (own, other) = gathered[l]
            gain = gain_mlp[l][None]
            q, k, v = project_qkv(x, gain_attn[l][None], cos, sin, wqkv)
            x4 = x.reshape(ms, seqs, -1, x.shape[1])
            if l < layers - 1:
                o = attend(q, k, v, ms, seqs, None)
                resids = [out_proj(o, wgua, wo_block, x4, None)]
                split = None
            else:
                resids, split = [], ms
                for i in range(seqs):
                    o = attend(q, k, v, ms, seqs, i)
                    m = out_proj(o, wgua, wo_block, x4, i)
                    resids.append(exchange(m.reshape(ms, -1, m.shape[1])).reshape(m.shape))
            za = zb = None
            for i, m in enumerate(resids):
                za = gate_up(m, gain, wgua, half, len(resids), i, za)
            for i, m in enumerate(resids):
                zb = gate_up(m, gain, wgub, half, len(resids), i, zb)
            x = down(place, za, zb, own, resids, 0, split)
            x = down(place, za, zb, other, resids, 1, split, x)
        return x.reshape(x_in.shape)

    return jax.shard_map(device_step, mesh=mesh, in_specs=(act_spec, P(), P(), P(), P(), col_spec, col_spec, col_spec, row_spec, col_spec, col_spec, row_spec), out_specs=act_spec, check_vma=False)
```

time: 1570 us -> 1570 us (level)
  Pallas kernels: 968 us -> 833 us
  waiting for transfers between devices: 503 us -> 630 us
    all_gather x6, waiting for transfers between devices: 0.04 us -> 270 us  [gather(): full = lax.all_gather(block, ('fsdp', 'model'), axis=0, tiled=False)]
    ppermute x14, waiting for transfers between devices: 503 us -> 331 us  [swap(): lax.ppermute(block, axis, [(i, i ^ bit) for i in range(mesh.shape[axis])])]
    pallas_call x6 -> x7, Pallas kernels: 508 us -> 372 us  [the longest x4 197 us: down(): pl.pallas_call(functools.partial(down_kernel, count=count, resids=len(res...]
    all_to_all x2 -> x3, waiting for transfers between devices: 0.01 us -> 28 us  [exchange(): lax.all_to_all(tokens, 'model', split_axis=0, concat_axis=0, tiled=True)]
    pallas_call x4 -> x6, Pallas kernels: 325 us -> 334 us  [gate_up(): pl.pallas_call(functools.partial(gate_up_kernel, chunk=512), grid=(ms * p...]
    pallas_call x2 -> x3, Pallas kernels: 48.3 us -> 52.2 us  [out_proj(): pl.pallas_call(functools.partial(out_proj_kernel, chunk=512), grid=(ys *...]
  transfers between devices with their start and end apart: 22 -> 23, of which waited for: 4 -> 6; matrix products, arithmetic and copies ran while one was open for 3% -> 3% of each run, Pallas kernels for 59% -> 50%
where the time goes in v3:
time: 1570 us; the launch traced here: 1560 us
  Pallas kernels  833 us (53%)
  waiting for transfers between devices  630 us (40%)
  other arithmetic  30 us (2%)
  starting transfers between devices  26.7 us (2%)
  local copies, waits for them, and re-layouts  25.9 us (2%)
    pallas_call x6, Pallas kernels, gate_up(): pl.pallas_call(functools.partial(gate_up_kernel, chunk=512), grid=(ms * p...  334 us
    ppermute x14, waiting for transfers between devices, swap(): lax.ppermute(block, axis, [(i, i ^ bit) for i in range(mesh.shape[axis])])  331 us
    all_gather x6, waiting for transfers between devices, gather(): full = lax.all_gather(block, ('fsdp', 'model'), axis=0, tiled=False)  270 us
    pallas_call x4, Pallas kernels, down(): pl.pallas_call(functools.partial(down_kernel, count=count, resids=len(res...  197 us
    pallas_call x3, Pallas kernels, attend(): pl.pallas_call(attention_kernel, grid=(count * blocks,), in_specs=[pl.Blo...  175 us
    pallas_call x2, Pallas kernels, project_qkv(): pl.pallas_call(qkv_kernel, grid=(blocks,), in_specs=[pl.BlockSpec((tokens...  75.5 us
    pallas_call x3, Pallas kernels, out_proj(): pl.pallas_call(functools.partial(out_proj_kernel, chunk=512), grid=(ys *...  52.2 us
  transfers between devices with their start and end apart: 23, of which 6 were waited for; matrix products, arithmetic and copies ran while one was open for 3% of the time, Pallas kernels for 50%

profile of v3, /device:TPU:0, one launch (start us, length us, event | category | flops | bytes accessed | tf_op | source)
XLA Modules:
  0.0 1559.0 jit_solution(16357166579028017573)
XLA Ops:
  11.7 11.1 slice_bitcast_fusion.2
  22.8 11.2 pad_maximum_fusion
  34.0 4.8 pad_maximum_fusion.2
  41.2 5.7 pad_maximum_fusion.1
  52.7 6.2 slice_bitcast_fusion
  62.1 5.8 all-to-all-start
  69.4 154.6 %collective-permute-done.2.refs_10_ = bf16[2048,1024]{1,0:T(8,128)(2,1)} collective-permute-done((bf16[2048,1024]{1,0:T(8,128)(2,1)}, bf16[2048,1024]{1,0:T(8,128)(2,1)}, u32[]{:S(2)}, u32[]{:S(2)}) %collective-permute-start.2) | collective-permute-done | bytes 4194336 | tf_op jit(solution)/shard_map/ppermute | solution.py:328
  230.6 176.4 %collective-permute-done.3.refs_10_ = bf16[2048,1024]{1,0:T(8,128)(2,1)} collective-permute-done((bf16[2048,1024]{1,0:T(8,128)(2,1)}, bf16[2048,1024]{1,0:T(8,128)(2,1)}, u32[]{:S(2)}, u32[]{:S(2)}) %collective-permute-start.3) | collective-permute-done | bytes 4194336 | tf_op jit(solution)/shard_map/ppermute | solution.py:328
  407.0 37.8 %qkv.2 = (bf16[2048,2048]{1,0:T(8,128)(2,1)}, bf16[2048,512]{1,0:T(8,128)(2,1)}, bf16[2048,512]{1,0:T(8,128)(2,1)}) custom-call(bf16[2048,2048]{1,0:T(8,128)(2,1)} %bitcast.2.x_ref, f32[1,2048]{1,0:T(1,128)} %get-tuple-element.38.gain_ref, f32[1024,128]{1,0:T(8,128)} %copy.19.cos_ref, f32[1024,128]{1,0:T(8,128)} %copy.20.sin_ref, ...), custom_call_target="tpu_custom_call" | custom-call | flops 25769803776 | bytes 29360128 | tf_op jit(solution)/shard_map/qkv/pallas_call | solution.py:70
  444.8 86.2 %shard_map.118 = bf16[4,2,256,2048]{3,2,1,0:T(8,128)(2,1)} custom-call(bf16[4,2,256,2048]{3,2,1,0:T(8,128)(2,1)} %bitcast.91, bf16[4,2,256,512]{3,2,1,0:T(8,128)(2,1)} %bitcast.96, bf16[4,2,256,512]{3,2,1,0:T(8,128)(2,1)} %bitcast.97), custom_call_target="tpu_custom_call" | custom-call | flops 34359738368 | bytes 20971520 | tf_op jit(solution)/shard_map/pallas_call | solution.py:150
  531.0 24.4 %shard_map.119.x_ref.refs_12_ = bf16[2048,2048]{1,0:T(8,128)(2,1)} custom-call(bf16[2048,2048]{1,0:T(8,128)(2,1)} %bitcast.76, bf16[2,4,2560,1024]{3,2,1,0:T(8,128)(2,1)} %bitcast.71, bf16[4,2,256,2048]{3,2,1,0:T(8,128)(2,1)} %bitcast.17.r_ref), custom_call_target="tpu_custom_call" | custom-call | flops 17179869184 | bytes 33554432 | tf_op jit(solution)/shard_map/pallas_call | solution.py:185
  555.4 81.1 %shard_map.120.refs_0_.refs_1_.refs_2_.refs_3_ = bf16[2048,4096]{1,0:T(8,128)(2,1)} custom-call(bf16[2048,2048]{1,0:T(8,128)(2,1)} %shard_map.119.x_ref.refs_12_, f32[1,2048]{1,0:T(1,128)} %get-tuple-element.36.gain_ref, bf16[2,4,2560,1024]{3,2,1,0:T(8,128)(2,1)} %bitcast.72, bf16[2,4,2560,1024]{3,2,1,0:T(8,128)(2,1)} %bitcast.73), custom_call_target="tpu_custom_call" | custom-call | flops 68719476736 | bytes 41943040 | tf_op jit(solution)/shard_map/pallas_call | solution.py:235
  636.5 18.9 %all-gather.17.cloned.1.call-done = bf16[16384,1024]{1,0:T(8,128)(2,1)} async-done(((bf16[2048,1024]{1,0:T(8,128)(2,1)}), bf16[16384,1024]{1,0:T(8,128)(2,1)}) %all-gather.17.cloned.1.call-update) | async-done | bytes 33554448 | tf_op jit(solution)/shard_map/all_gather | solution.py:321
  655.3 81.2 %shard_map.121.refs_4_.refs_5_.refs_6_.refs_7_ = bf16[2048,4096]{1,0:T(8,128)(2,1)} custom-call(bf16[2048,2048]{1,0:T(8,128)(2,1)} %shard_map.119.x_ref.refs_12_, f32[1,2048]{1,0:T(1,128)} %get-tuple-element.36.gain_ref, bf16[2,4,2048,1024]{3,2,1,0:T(8,128)(2,1)} %bitcast.85, bf16[2,4,2048,1024]{3,2,1,0:T(8,128)(2,1)} %bitcast.86), custom_call_target="tpu_custom_call" | custom-call | flops 68719476736 | bytes 41943040 | tf_op jit(solution)/shard_map/pallas_call | solution.py:235
  738.6 49.0 %down_own.2.refs_13_ = bf16[2048,2048]{1,0:T(8,128)(2,1)} custom-call(s32[2]{0:T(128)} %pad_add_fusion.place_ref, bf16[2048,4096]{1,0:T(8,128)(2,1)} %shard_map.120.refs_0_.refs_1_.refs_2_.refs_3_, bf16[2048,4096]{1,0:T(8,128)(2,1)} %shard_map.120.refs_0_.refs_1_.refs_2_.refs_3_, bf16[2048,4096]{1,0:T(8,128)(2,1)} %shard_map.120.refs_0_.refs_1_.refs_2_.refs_3_, ...), custom_call_target="tpu_custom_call" | custom-call | flops 34359738368 | bytes 50331648 | tf_op jit(solution)/shard_map/down_own/pallas_call | solution.py:298
  787.6 49.0 %down_other.2.x_ref = bf16[2048,2048]{1,0:T(8,128)(2,1)} custom-call(s32[2]{0:T(128)} %pad_add_fusion.place_ref, bf16[2048,4096]{1,0:T(8,128)(2,1)} %shard_map.120.refs_0_.refs_1_.refs_2_.refs_3_, bf16[2048,4096]{1,0:T(8,128)(2,1)} %shard_map.120.refs_0_.refs_1_.refs_2_.refs_3_, ...), custom_call_target="tpu_custom_call", output_to_operand_aliasing={{}: (14, {})} | custom-call | flops 34359738368 | bytes 50331648 | tf_op jit(solution)/shard_map/down_other/pallas_call | solution.py:298
  836.6 37.7 %qkv.3 = (bf16[2048,2048]{1,0:T(8,128)(2,1)}, bf16[2048,512]{1,0:T(8,128)(2,1)}, bf16[2048,512]{1,0:T(8,128)(2,1)}) custom-call(bf16[2048,2048]{1,0:T(8,128)(2,1)} %down_other.2.x_ref, f32[1,2048]{1,0:T(1,128)} %get-tuple-element.37.gain_ref, f32[1024,128]{1,0:T(8,128)} %copy.19.cos_ref, f32[1024,128]{1,0:T(8,128)} %copy.20.sin_ref, ...), custom_call_target="tpu_custom_call" | custom-call | flops 25769803776 | bytes 29360128 | tf_op jit(solution)/shard_map/qkv/pallas_call | solution.py:70
  874.3 44.5 %shard_map.124 = bf16[4,1,256,2048]{3,2,1,0:T(8,128)(2,1)} custom-call(bf16[4,2,256,2048]{3,2,1,0:T(8,128)(2,1)} %bitcast.89, bf16[4,2,256,512]{3,2,1,0:T(8,128)(2,1)} %bitcast.92, bf16[4,2,256,512]{3,2,1,0:T(8,128)(2,1)} %bitcast.94), custom_call_target="tpu_custom_call" | custom-call | flops 17179869184 | bytes 10485760 | tf_op jit(solution)/shard_map/pallas_call | solution.py:150
  918.8 166.2 %all-gather.21.cloned.1.call-done = bf16[20480,1024]{1,0:T(8,128)(2,1)} async-done(((bf16[2560,1024]{1,0:T(8,128)(2,1)}), bf16[20480,1024]{1,0:T(8,128)(2,1)}) %all-gather.21.cloned.1.call-update) | async-done | bytes 41943056 | tf_op jit(solution)/shard_map/all_gather | solution.py:321
  1085.0 14.3 shard_map.125
  1099.3 5.1 all-to-all-start.2
  1105.4 44.3 %shard_map.122 = bf16[4,1,256,2048]{3,2,1,0:T(8,128)(2,1)} custom-call(bf16[4,2,256,2048]{3,2,1,0:T(8,128)(2,1)} %bitcast.90, bf16[4,2,256,512]{3,2,1,0:T(8,128)(2,1)} %bitcast.93, bf16[4,2,256,512]{3,2,1,0:T(8,128)(2,1)} %bitcast.95), custom_call_target="tpu_custom_call" | custom-call | flops 17179869184 | bytes 10485760 | tf_op jit(solution)/shard_map/pallas_call | solution.py:150
  1149.7 13.6 shard_map.123
  1163.3 28.0 %all-to-all-done.2 = bf16[4,256,2048]{2,1,0:T(8,128)(2,1)} async-done(((bf16[4,256,2048]{2,1,0:T(8,128)(2,1)}), bf16[4,256,2048]{2,1,0:T(8,128)(2,1)}, u32[]{:S(2)}, u32[]{:S(2)}) %all-to-all-start.2) | async-done | bytes 4194336 | tf_op jit(solution)/shard_map/all_to_all | solution.py:325
  1191.3 5.3 all-to-all-start.1
  1196.7 42.9 %shard_map.126.refs_0_ = bf16[2048,4096]{1,0:T(8,128)(2,1)} custom-call(bf16[1024,2048]{1,0:T(8,128)(2,1)} %bitcast.39.x_ref.refs_12_, f32[1,2048]{1,0:T(1,128)} %get-tuple-element.35.gain_ref, bf16[2,4,2560,1024]{3,2,1,0:T(8,128)(2,1)} %bitcast.65, bf16[2,4,2560,1024]{3,2,1,0:T(8,128)(2,1)} %bitcast.66), custom_call_target="tpu_custom_call" | custom-call | flops 34359738368 | bytes 37748736 | tf_op jit(solution)/shard_map/pallas_call | solution.py:235
  1239.6 85.4 %all-gather.23.cloned.1.call-done = bf16[16384,1024]{1,0:T(8,128)(2,1)} async-done(((bf16[2048,1024]{1,0:T(8,128)(2,1)}), bf16[16384,1024]{1,0:T(8,128)(2,1)}) %all-gather.23.cloned.1.call-update) | async-done | bytes 33554448 | tf_op jit(solution)/shard_map/all_gather | solution.py:321
  1325.0 42.7 %shard_map.128.refs_0_ = bf16[2048,4096]{1,0:T(8,128)(2,1)} custom-call(bf16[1024,2048]{1,0:T(8,128)(2,1)} %bitcast.39.x_ref.refs_12_, f32[1,2048]{1,0:T(1,128)} %get-tuple-element.35.gain_ref, bf16[2,4,2048,1024]{3,2,1,0:T(8,128)(2,1)} %bitcast.81, bf16[2,4,2048,1024]{3,2,1,0:T(8,128)(2,1)} %bitcast.82), custom_call_target="tpu_custom_call" | custom-call | flops 34359738368 | bytes 37748736 | tf_op jit(solution)/shard_map/pallas_call | solution.py:235
  1367.7 42.7 %shard_map.127.refs_0_.refs_1_.refs_2_.refs_3_ = bf16[2048,4096]{1,0:T(8,128)(2,1)} custom-call(bf16[1024,2048]{1,0:T(8,128)(2,1)} %bitcast.36.x_ref.refs_13_, f32[1,2048]{1,0:T(1,128)} %get-tuple-element.35.gain_ref, bf16[2,4,2560,1024]{3,2,1,0:T(8,128)(2,1)} %bitcast.67, bf16[2,4,2560,1024]{3,2,1,0:T(8,128)(2,1)} %bitcast.68, ...), custom_call_target="tpu_custom_call", output_to_operand_aliasing={{}: (4, {})} | custom-call | flops 34359738368 | bytes 37748736 | tf_op jit(solution)/shard_map/pallas_call | solution.py:235
  1410.4 42.9 %shard_map.129.refs_4_.refs_5_.refs_6_.refs_7_ = bf16[2048,4096]{1,0:T(8,128)(2,1)} custom-call(bf16[1024,2048]{1,0:T(8,128)(2,1)} %bitcast.36.x_ref.refs_13_, f32[1,2048]{1,0:T(1,128)} %get-tuple-element.35.gain_ref, bf16[2,4,2048,1024]{3,2,1,0:T(8,128)(2,1)} %bitcast.83, bf16[2,4,2048,1024]{3,2,1,0:T(8,128)(2,1)} %bitcast.84, ...), custom_call_target="tpu_custom_call", output_to_operand_aliasing={{}: (4, {})} | custom-call | flops 34359738368 | bytes 37748736 | tf_op jit(solution)/shard_map/pallas_call | solution.py:235
  1453.4 49.3 %down_own.3.refs_14_ = bf16[4,2,256,2048]{3,2,1,0:T(8,128)(2,1)} custom-call(s32[2]{0:T(128)} %pad_add_fusion.place_ref, bf16[2048,4096]{1,0:T(8,128)(2,1)} %shard_map.127.refs_0_.refs_1_.refs_2_.refs_3_, bf16[2048,4096]{1,0:T(8,128)(2,1)} %shard_map.127.refs_0_.refs_1_.refs_2_.refs_3_, bf16[2048,4096]{1,0:T(8,128)(2,1)} %shard_map.127.refs_0_.refs_1_.refs_2_.refs_3_, ...), custom_call_target="tpu_custom_call" | custom-call | flops 34359738368 | bytes 50331648 | tf_op jit(solution)/shard_map/down_own/pallas_call | solution.py:298
  1502.7 49.2 %down_other.3 = bf16[4,2,256,2048]{3,2,1,0:T(8,128)(2,1)} custom-call(s32[2]{0:T(128)} %pad_add_fusion.place_ref, bf16[2048,4096]{1,0:T(8,128)(2,1)} %shard_map.127.refs_0_.refs_1_.refs_2_.refs_3_, bf16[2048,4096]{1,0:T(8,128)(2,1)} %shard_map.127.refs_0_.refs_1_.refs_2_.refs_3_, ...), custom_call_target="tpu_custom_call", output_to_operand_aliasing={{}: (15, {})} | custom-call | flops 34359738368 | bytes 50331648 | tf_op jit(solution)/shard_map/down_other/pallas_call | solution.py:298
  (74 shorter events, 27.6 us)
Async XLA Ops:
  6.5 400.5 %all-gather.13.cloned.1.call-start = ((), (), s32[]{:S(2)}) async-start(), calls=%async_computation.3 | async-start | bytes 14155776 | tf_op jit(solution)/shard_map/all_gather | solution.py:321
  6.5 1.8 copy-start.3
  6.5 1.8 copy-start.4
  8.4 2.1 copy-start.1
  10.5 520.6 %all-gather.15.cloned.1.call-start = ((), (), s32[]{:S(2)}) async-start(), calls=%async_computation.4 | async-start | bytes 47185920 | tf_op jit(solution)/shard_map/all_gather | solution.py:321
  34.0 621.4 %all-gather.17.cloned.1.call-start = ((), (), s32[]{:S(2)}) async-start(), calls=%async_computation.5 | async-start | bytes 37748736 | tf_op jit(solution)/shard_map/all_gather | solution.py:321
  38.9 797.7 %all-gather.19.cloned.1.call-start = ((), (), s32[]{:S(2)}) async-start(), calls=%async_computation.6 | async-start | bytes 14155776 | tf_op jit(solution)/shard_map/all_gather | solution.py:321
  41.2 1043.8 %all-gather.21.cloned.1.call-start = ((), (), s32[]{:S(2)}) async-start(), calls=%async_computation.7 | async-start | bytes 47185920 | tf_op jit(solution)/shard_map/all_gather | solution.py:321
  46.9 1.6 copy-start
  47.0 1278.0 %all-gather.23.cloned.1.call-start = ((), (), s32[]{:S(2)}) async-start(), calls=%async_computation.8 | async-start | bytes 37748736 | tf_op jit(solution)/shard_map/all_gather | solution.py:321
  58.9 167.1 %copy-start.5 = (f32[1024,32]{0,1:T(8,128)S(1)}, f32[1024,32]{0,1:T(8,128)}, u32[]{:S(2)}) copy-start(f32[1024,32]{0,1:T(8,128)} %param.15) | copy-start | bytes 393220
  58.9 168.2 %copy-start.2 = (f32[1024,32]{0,1:T(8,128)S(1)}, f32[1024,32]{0,1:T(8,128)}, u32[]{:S(2)}) copy-start(f32[1024,32]{0,1:T(8,128)} %param.16) | copy-start | bytes 393220
  58.9 165.1 %collective-permute-start.2 = (bf16[2048,1024]{1,0:T(8,128)(2,1)}, bf16[2048,1024]{1,0:T(8,128)(2,1)}, u32[]{:S(2)}, u32[]{:S(2)}) collective-permute-start(bf16[2048,1024]{1,0:T(8,128)(2,1)} %get-tuple-element.18.refs_8_), channel_id=1, source_target_pairs={{0,2},{1,3},{2,0},{3,1},{4,6},{5,7},{6,4},{7,5}} | collective-permute-start | bytes 12582920 | tf_op jit(solution)/shard_map/ppermute | solution.py:328
  62.1 345.0 %all-to-all-start = ((bf16[8,256,2048]{2,1,0:T(8,128)(2,1)}), bf16[8,256,2048]{2,1,0:T(8,128)(2,1)}, u32[]{:S(2)}, u32[]{:S(2)}) async-start(bf16[8,256,2048]{2,1,0:T(8,128)(2,1)} %param.12), calls=%async_computation | async-start | bytes 16777216 | tf_op jit(solution)/shard_map/all_to_all | solution.py:325
  67.9 161.0 %copy-start.6 = (f32[2,2048]{1,0:T(2,128)S(1)}, f32[2,2048]{1,0:T(2,128)}, u32[]{:S(2)}) copy-start(f32[2,2048]{1,0:T(2,128)} %param.13) | copy-start | bytes 49156
  67.9 161.6 %copy-start.7 = (f32[2,2048]{1,0:T(2,128)S(1)}, f32[2,2048]{1,0:T(2,128)}, u32[]{:S(2)}) copy-start(f32[2,2048]{1,0:T(2,128)} %param.14) | copy-start | bytes 49156
  67.9 162.4 %collective-permute-start = (bf16[2048,1024]{1,0:T(8,128)(2,1)}, bf16[2048,1024]{1,0:T(8,128)(2,1)}, u32[]{:S(2)}, u32[]{:S(2)}) collective-permute-start(bf16[2048,1024]{1,0:T(8,128)(2,1)} %get-tuple-element.18.refs_8_), channel_id=1, source_target_pairs={{0,4},{4,0},{1,5},{5,1},{2,6},{6,2},{3,7},{7,3}} | collective-permute-start | bytes 12582920 | tf_op jit(solution)/shard_map/ppermute | solution.py:328
  224.0 183.0 %collective-permute-start.3 = (bf16[2048,1024]{1,0:T(8,128)(2,1)}, bf16[2048,1024]{1,0:T(8,128)(2,1)}, u32[]{:S(2)}, u32[]{:S(2)}) collective-permute-start(bf16[2048,1024]{1,0:T(8,128)(2,1)} %collective-permute-done.2.refs_10_), channel_id=1, source_target_pairs={{0,4},{4,0},{1,5},{5,1},{2,6},{6,2},{3,7},{7,3}} | collective-permute-start | bytes 12582920 | tf_op jit(solution)/shard_map/ppermute | solution.py:328
  225.5 511.0 %collective-permute-start.5 = (bf16[2048,1024]{1,0:T(8,128)(2,1)}, bf16[2048,1024]{1,0:T(8,128)(2,1)}, u32[]{:S(2)}, u32[]{:S(2)}) collective-permute-start(bf16[2048,1024]{1,0:T(8,128)(2,1)} %get-tuple-element.18.refs_8_), channel_id=1, source_target_pairs={{0,1},{1,0},{2,3},{3,2},{4,5},{5,4},{6,7},{7,6}} | collective-permute-start | bytes 12582920 | tf_op jit(solution)/shard_map/ppermute | solution.py:328
  225.5 511.4 %collective-permute-start.9 = (bf16[2048,1024]{1,0:T(8,128)(2,1)}, bf16[2048,1024]{1,0:T(8,128)(2,1)}, u32[]{:S(2)}, u32[]{:S(2)}) collective-permute-start(bf16[2048,1024]{1,0:T(8,128)(2,1)} %get-tuple-element.17.refs_8_), channel_id=1, source_target_pairs={{0,2},{1,3},{2,0},{3,1},{4,6},{5,7},{6,4},{7,5}} | collective-permute-start | bytes 12582920 | tf_op jit(solution)/shard_map/ppermute | solution.py:328
  230.1 508.5 %collective-permute-start.6 = (bf16[2048,1024]{1,0:T(8,128)(2,1)}, bf16[2048,1024]{1,0:T(8,128)(2,1)}, u32[]{:S(2)}, u32[]{:S(2)}) collective-permute-start(bf16[2048,1024]{1,0:T(8,128)(2,1)} %collective-permute-done.2.refs_10_), channel_id=1, source_target_pairs={{0,1},{1,0},{2,3},{3,2},{4,5},{5,4},{6,7},{7,6}} | collective-permute-start | bytes 12582920 | tf_op jit(solution)/shard_map/ppermute | solution.py:328
  230.3 557.3 %collective-permute-start.1 = (bf16[2048,1024]{1,0:T(8,128)(2,1)}, bf16[2048,1024]{1,0:T(8,128)(2,1)}, u32[]{:S(2)}, u32[]{:S(2)}) collective-permute-start(bf16[2048,1024]{1,0:T(8,128)(2,1)} %collective-permute-done.refs_8_), channel_id=1, source_target_pairs={{0,1},{1,0},{2,3},{3,2},{4,5},{5,4},{6,7},{7,6}} | collective-permute-start | bytes 12582920 | tf_op jit(solution)/shard_map/ppermute | solution.py:328
  407.0 380.6 %collective-permute-start.4 = (bf16[2048,1024]{1,0:T(8,128)(2,1)}, bf16[2048,1024]{1,0:T(8,128)(2,1)}, u32[]{:S(2)}, u32[]{:S(2)}) collective-permute-start(bf16[2048,1024]{1,0:T(8,128)(2,1)} %collective-permute-done.3.refs_10_), channel_id=1, source_target_pairs={{0,1},{1,0},{2,3},{3,2},{4,5},{5,4},{6,7},{7,6}} | collective-permute-start | bytes 12582920 | tf_op jit(solution)/shard_map/ppermute | solution.py:328
  736.6 368.3 %collective-permute-start.7 = (bf16[2048,1024]{1,0:T(8,128)(2,1)}, bf16[2048,1024]{1,0:T(8,128)(2,1)}, u32[]{:S(2)}, u32[]{:S(2)}) collective-permute-start(bf16[2048,1024]{1,0:T(8,128)(2,1)} %get-tuple-element.17.refs_8_), channel_id=1, source_target_pairs={{0,4},{4,0},{1,5},{5,1},{2,6},{6,2},{3,7},{7,3}} | collective-permute-start | bytes 12582920 | tf_op jit(solution)/shard_map/ppermute | solution.py:328
  736.9 368.4 %collective-permute-start.10 = (bf16[2048,1024]{1,0:T(8,128)(2,1)}, bf16[2048,1024]{1,0:T(8,128)(2,1)}, u32[]{:S(2)}, u32[]{:S(2)}) collective-permute-start(bf16[2048,1024]{1,0:T(8,128)(2,1)} %collective-permute-done.9.refs_10_), channel_id=1, source_target_pairs={{0,4},{4,0},{1,5},{5,1},{2,6},{6,2},{3,7},{7,3}} | collective-permute-start | bytes 12582920 | tf_op jit(solution)/shard_map/ppermute | solution.py:328
  1099.3 92.1 %all-to-all-start.2 = ((bf16[4,256,2048]{2,1,0:T(8,128)(2,1)}), bf16[4,256,2048]{2,1,0:T(8,128)(2,1)}, u32[]{:S(2)}, u32[]{:S(2)}) async-start(bf16[4,256,2048]{2,1,0:T(8,128)(2,1)} %bitcast.74), calls=%async_computation.2 | async-start | bytes 8388608 | tf_op jit(solution)/shard_map/all_to_all | solution.py:325
  1104.3 349.0 %collective-permute-start.12 = (bf16[2048,1024]{1,0:T(8,128)(2,1)}, bf16[2048,1024]{1,0:T(8,128)(2,1)}, u32[]{:S(2)}, u32[]{:S(2)}) collective-permute-start(bf16[2048,1024]{1,0:T(8,128)(2,1)} %get-tuple-element.17.refs_8_), channel_id=1, source_target_pairs={{0,1},{1,0},{2,3},{3,2},{4,5},{5,4},{6,7},{7,6}} | collective-permute-start | bytes 12582920 | tf_op jit(solution)/shard_map/ppermute | solution.py:328
  1104.8 348.5 %collective-permute-start.13 = (bf16[2048,1024]{1,0:T(8,128)(2,1)}, bf16[2048,1024]{1,0:T(8,128)(2,1)}, u32[]{:S(2)}, u32[]{:S(2)}) collective-permute-start(bf16[2048,1024]{1,0:T(8,128)(2,1)} %collective-permute-done.9.refs_10_), channel_id=1, source_target_pairs={{0,1},{1,0},{2,3},{3,2},{4,5},{5,4},{6,7},{7,6}} | collective-permute-start | bytes 12582920 | tf_op jit(solution)/shard_map/ppermute | solution.py:328
  1104.9 397.8 %collective-permute-start.8 = (bf16[2048,1024]{1,0:T(8,128)(2,1)}, bf16[2048,1024]{1,0:T(8,128)(2,1)}, u32[]{:S(2)}, u32[]{:S(2)}) collective-permute-start(bf16[2048,1024]{1,0:T(8,128)(2,1)} %collective-permute-done.7.refs_8_), channel_id=1, source_target_pairs={{0,1},{1,0},{2,3},{3,2},{4,5},{5,4},{6,7},{7,6}} | collective-permute-start | bytes 12582920 | tf_op jit(solution)/shard_map/ppermute | solution.py:328
  1105.4 397.3 %collective-permute-start.11 = (bf16[2048,1024]{1,0:T(8,128)(2,1)}, bf16[2048,1024]{1,0:T(8,128)(2,1)}, u32[]{:S(2)}, u32[]{:S(2)}) collective-permute-start(bf16[2048,1024]{1,0:T(8,128)(2,1)} %collective-permute-done.10.refs_10_), channel_id=1, source_target_pairs={{0,1},{1,0},{2,3},{3,2},{4,5},{5,4},{6,7},{7,6}} | collective-permute-start | bytes 12582920 | tf_op jit(solution)/shard_map/ppermute | solution.py:328
  1191.3 176.4 %all-to-all-start.1 = ((bf16[4,256,2048]{2,1,0:T(8,128)(2,1)}), bf16[4,256,2048]{2,1,0:T(8,128)(2,1)}, u32[]{:S(2)}, u32[]{:S(2)}) async-start(bf16[4,256,2048]{2,1,0:T(8,128)(2,1)} %bitcast.75), calls=%async_computation.1 | async-start | bytes 8388608 | tf_op jit(solution)/shard_map/all_to_all | solution.py:325
Sparse Core Ops, SparseCore 0:
  10.6 83.3 all-gather.12
  95.8 357.9 all-gather.14
  455.5 199.7 all-gather.16
  657.0 66.4 all-gather.18
  725.2 359.7 all-gather.20
  1086.6 238.2 all-gather.22

commit v4 on v3

--- a/solution.py
+++ b/solution.py
@@ -264,50 +264,60 @@
             o_ref[rows, :] = out
 
 
-def down(place, za, zb, ws, resids, other, split, onto=None):
+def down(place, za, zb, ws, resids, split, other=0, part=0, parts=1, onto=None):
     tokens = za.shape[0]
     width = resids[0].shape[1]
-    count = len(ws)
+    whole = not isinstance(ws, (list, tuple))
+    count = ws.shape[1] if whole else len(ws)
+    halves = ws.shape[0] if whole else 1
+    cols = ws.shape[3] if whole else ws[0].shape[1]
     half = za.shape[1] // count
-    cols = ws[0].shape[1]
     block, rows = 256, 1024
     per = cols // block
+    steps = halves * per
 
     def column(i, place):
-        return (place[1] ^ other) * per + i % per
-
-    z_specs = [pl.BlockSpec((rows, half), lambda i, place, k=k: (i // per, place[0] ^ k)) for k in range(count)]
+        y = i // per % halves if whole else place[1] ^ other
+        return (y * parts + part) * per + i % per
+
+    def source(k, place):
+        return k if whole else place[0] ^ k
+
+    z_specs = [pl.BlockSpec((rows, half), lambda i, place, k=k: (i // steps, source(k, place))) for k in range(count)]
     in_specs = z_specs + z_specs
-    in_specs += [pl.BlockSpec((2 * half, block), lambda i, place: (0, i % per))] * count
+    if whole:
+        in_specs += [pl.BlockSpec((None, None, 2 * half, block), lambda i, place, k=k: (i // per % halves, k, 0, i % per)) for k in range(count)]
+        operands = [za] * count + [zb] * count + [ws] * count + list(resids)
+    else:
+        in_specs += [pl.BlockSpec((2 * half, block), lambda i, place: (0, i % per))] * count
+        operands = [za] * count + [zb] * count + list(ws) + list(resids)
     if len(resids) == 1:
-        in_specs += [pl.BlockSpec((rows, block), lambda i, place: (i // per, column(i, place)))]
+        in_specs += [pl.BlockSpec((rows, block), lambda i, place: (i // steps, column(i, place)))]
     else:
         in_specs += [pl.BlockSpec((rows, block), lambda i, place: (0, column(i, place)))] * len(resids)
-    operands = [za] * count + [zb] * count + list(ws) + list(resids)
     aliases = {}
     if onto is not None:
         in_specs.append(pl.BlockSpec(memory_space=pl.ANY))
         aliases = {1 + len(operands): 0}
         operands.append(onto)
     if split:
-        out_spec = pl.BlockSpec((split, 1, rows // split, block), lambda i, place: (0, i // per, 0, column(i, place)))
+        out_spec = pl.BlockSpec((split, 1, rows // split, block), lambda i, place: (0, i // steps, 0, column(i, place)))
         out_shape = (split, tokens // rows, rows // split, width)
     else:
-        out_spec = pl.BlockSpec((rows, block), lambda i, place: (i // per, column(i, place)))
+        out_spec = pl.BlockSpec((rows, block), lambda i, place: (i // steps, column(i, place)))
         out_shape = (tokens, width)
     return pl.pallas_call(
-        functools.partial(down_kernel, count=count, resids=len(resids), steps=per, chunk=512),
+        functools.partial(down_kernel, count=count, resids=len(resids), steps=steps, chunk=512),
         grid_spec=pltpu.PrefetchScalarGridSpec(
             num_scalar_prefetch=1,
-            grid=(tokens // rows * per,),
+            grid=(tokens // rows * steps,),
             in_specs=in_specs,
             out_specs=out_spec,
         ),
         out_shape=jax.ShapeDtypeStruct(out_shape, BF16),
         input_output_aliases=aliases,
         compiler_params=params(),
-        cost_estimate=pl.CostEstimate(flops=4 * tokens * za.shape[1] * cols, bytes_accessed=4 * za.size + 4 * za.shape[1] * cols, transcendentals=0),
-        name="down_other" if other else "down_own",
+        cost_estimate=pl.CostEstimate(flops=4 * tokens * za.shape[1] * halves * cols, bytes_accessed=4 * za.size + 4 * za.shape[1] * halves * cols, transcendentals=0),
     )(place, *operands)
 
 
@@ -341,41 +351,52 @@
         x = exchange(x_in)
         gathered = []
         for l in range(layers):
+            last = l == layers - 1
             block = jnp.concatenate([w_q[l], w_k[l], w_v[l]], axis=1)
             wqkv = gather(block)
-            block = jnp.concatenate([w_gate[l, :, :half], w_up[l, :, :half], w_o[l]], axis=0)
+            if last:
+                wo = gather(w_o[l])
+            block = jnp.concatenate([w_gate[l, :, :half], w_up[l, :, :half]] + ([] if last else [w_o[l]]), axis=0)
             wgua = gather(block)
+            if not last:
+                wo = wgua
             block = jnp.concatenate([w_gate[l, :, half:], w_up[l, :, half:]], axis=0)
             wgub = gather(block)
-            block = w_down[l]
-            gathered.append((wqkv, wgua, wgub, spread(block)))
+            cols = w_down.shape[2] // (2 if last else 1)
+            block = w_down[l, :, :cols]
+            rest = w_down[l, :, cols:]
+            wd = spread(block)
+            gathered.append((wqkv, wo, wgua, wgub, wd, gather(rest) if last else None))
 
         x = x.reshape(-1, x.shape[2])
         cos = jnp.tile(rope_cos, (1, 4))
         sin = jnp.tile(jnp.concatenate([-rope_sin, rope_sin], axis=1), (1, 2))
-        wo_block = 2 * w_gate.shape[1] // w_o.shape[1]
         for l in range(layers):
-            wqkv, wgua, wgub, (own, other) = gathered[l]
+            wqkv, wo, wgua, wgub, (own, other), rest = gathered[l]
             gain = gain_mlp[l][None]
+            wo_block = wo.shape[2] // w_o.shape[1] - 1
+            parts = 1 if rest is None else 2
             q, k, v = project_qkv(x, gain_attn[l][None], cos, sin, wqkv)
             x4 = x.reshape(ms, seqs, -1, x.shape[1])
             if l < layers - 1:
                 o = attend(q, k, v, ms, seqs, None)
-                resids = [out_proj(o, wgua, wo_block, x4, None)]
+                resids = [out_proj(o, wo, wo_block, x4, None)]
                 split = None
             else:
                 resids, split = [], ms
                 for i in range(seqs):
                     o = attend(q, k, v, ms, seqs, i)
-                    m = out_proj(o, wgua, wo_block, x4, i)
+                    m = out_proj(o, wo, wo_block, x4, i)
                     resids.append(exchange(m.reshape(ms, -1, m.shape[1])).reshape(m.shape))
             za = zb = None
             for i, m in enumerate(resids):
                 za = gate_up(m, gain, wgua, half, len(resids), i, za)
             for i, m in enumerate(resids):
                 zb = gate_up(m, gain, wgub, half, len(resids), i, zb)
-            x = down(place, za, zb, own, resids, 0, split)
-            x = down(place, za, zb, other, resids, 1, split, x)
+            x = down(place, za, zb, own, resids, split, 0, 0, parts)
+            x = down(place, za, zb, other, resids, split, 1, 0, parts, x)
+            if rest is not None:
+                x = down(place, za, zb, rest, resids, split, 0, 1, parts, x)
         return x.reshape(x_in.shape)
 
     return jax.shard_map(device_step, mesh=mesh, in_specs=(act_spec, P(), P(), P(), P(), col_spec, col_spec, col_spec, row_spec, col_spec, col_spec, row_spec), out_specs=act_spec, check_vma=False)

time: 1570 us -> 1420 us (0.904)
  waiting for transfers between devices: 630 us -> 473 us
    all_gather x6 -> x8, waiting for transfers between devices: 270 us -> 128 us  [gather(): full = lax.all_gather(block, ('fsdp', 'model'), axis=0, tiled=False)]
    pallas_call x4 -> x5, Pallas kernels: 197 us -> 207 us  [down(): pl.pallas_call(functools.partial(down_kernel, count=count, resids=len(res...]
  transfers between devices with their start and end apart: 23 -> 25, of which waited for: 6 -> 4; matrix products, arithmetic and copies ran while one was open for 3% -> 4% of each run, Pallas kernels for 50% -> 56%
where the time goes in v4:
time: 1420 us
  Pallas kernels  844 us (59%)
  waiting for transfers between devices  473 us (33%)
  other arithmetic  30.2 us (2%)
  local copies, waits for them, and re-layouts  29.1 us (2%)
  starting transfers between devices  26.1 us (2%)
    pallas_call x6, Pallas kernels, gate_up(): pl.pallas_call(functools.partial(gate_up_kernel, chunk=512), grid=(ms * p...  333 us
    ppermute x14, waiting for transfers between devices, swap(): lax.ppermute(block, axis, [(i, i ^ bit) for i in range(mesh.shape[axis])])  326 us
    pallas_call x5, Pallas kernels, down(): pl.pallas_call(functools.partial(down_kernel, count=count, resids=len(res...  207 us
    pallas_call x3, Pallas kernels, attend(): pl.pallas_call(attention_kernel, grid=(count * blocks,), in_specs=[pl.Blo...  176 us
    all_gather x8, waiting for transfers between devices, gather(): full = lax.all_gather(block, ('fsdp', 'model'), axis=0, tiled=False)  128 us
    pallas_call x2, Pallas kernels, project_qkv(): pl.pallas_call(qkv_kernel, grid=(blocks,), in_specs=[pl.BlockSpec((tokens...  75.8 us
    pallas_call x3, Pallas kernels, out_proj(): pl.pallas_call(functools.partial(out_proj_kernel, chunk=512), grid=(ys *...  51.8 us
  transfers between devices with their start and end apart: 25, of which 4 were waited for; matrix products, arithmetic and copies ran while one was open for 4% of the time, Pallas kernels for 56%

profile of v4, /device:TPU:0, one launch (start us, length us, event | category | flops | bytes accessed | tf_op | source)
XLA Modules:
  0.0 1416.3 jit_solution(8560949030186180279)
XLA Ops:
  11.7 11.1 slice_bitcast_fusion.2
  22.7 11.2 pad_maximum_fusion
  34.0 4.7 pad_maximum_fusion.1
  41.7 6.1 pad_maximum_fusion.3
  51.9 4.8 slice_bitcast_fusion.refs_8_
  59.2 5.7 all-to-all-start
  66.4 157.5 %collective-permute-done.2.refs_10_ = bf16[2048,1024]{1,0:T(8,128)(2,1)} collective-permute-done((bf16[2048,1024]{1,0:T(8,128)(2,1)}, bf16[2048,1024]{1,0:T(8,128)(2,1)}, u32[]{:S(2)}, u32[]{:S(2)}) %collective-permute-start.2) | collective-permute-done | bytes 4194336 | tf_op jit(solution)/shard_map/ppermute | solution.py:338
  225.4 6.1 slice_bitcast_fusion.1
  236.2 168.5 %collective-permute-done.3.refs_10_ = bf16[2048,1024]{1,0:T(8,128)(2,1)} collective-permute-done((bf16[2048,1024]{1,0:T(8,128)(2,1)}, bf16[2048,1024]{1,0:T(8,128)(2,1)}, u32[]{:S(2)}, u32[]{:S(2)}) %collective-permute-start.3) | collective-permute-done | bytes 4194336 | tf_op jit(solution)/shard_map/ppermute | solution.py:338
  404.7 37.7 %qkv.2 = (bf16[2048,2048]{1,0:T(8,128)(2,1)}, bf16[2048,512]{1,0:T(8,128)(2,1)}, bf16[2048,512]{1,0:T(8,128)(2,1)}) custom-call(bf16[2048,2048]{1,0:T(8,128)(2,1)} %bitcast.2.x_ref, f32[1,2048]{1,0:T(1,128)} %get-tuple-element.38.gain_ref, f32[1024,128]{1,0:T(8,128)} %copy.24.cos_ref, f32[1024,128]{1,0:T(8,128)} %copy.25.sin_ref, ...), custom_call_target="tpu_custom_call" | custom-call | flops 25769803776 | bytes 29360128 | tf_op jit(solution)/shard_map/qkv/pallas_call | solution.py:70
  442.4 86.2 %shard_map.118 = bf16[4,2,256,2048]{3,2,1,0:T(8,128)(2,1)} custom-call(bf16[4,2,256,2048]{3,2,1,0:T(8,128)(2,1)} %bitcast.93, bf16[4,2,256,512]{3,2,1,0:T(8,128)(2,1)} %bitcast.100, bf16[4,2,256,512]{3,2,1,0:T(8,128)(2,1)} %bitcast.101), custom_call_target="tpu_custom_call" | custom-call | flops 34359738368 | bytes 20971520 | tf_op jit(solution)/shard_map/pallas_call | solution.py:150
  528.7 24.4 %shard_map.119.x_ref.refs_12_ = bf16[2048,2048]{1,0:T(8,128)(2,1)} custom-call(bf16[2048,2048]{1,0:T(8,128)(2,1)} %bitcast.72, bf16[2,4,2560,1024]{3,2,1,0:T(8,128)(2,1)} %bitcast.67, bf16[4,2,256,2048]{3,2,1,0:T(8,128)(2,1)} %bitcast.17.r_ref), custom_call_target="tpu_custom_call" | custom-call | flops 17179869184 | bytes 33554432 | tf_op jit(solution)/shard_map/pallas_call | solution.py:185
  553.0 81.0 %shard_map.120.refs_0_.refs_1_.refs_2_.refs_3_ = bf16[2048,4096]{1,0:T(8,128)(2,1)} custom-call(bf16[2048,2048]{1,0:T(8,128)(2,1)} %shard_map.119.x_ref.refs_12_, f32[1,2048]{1,0:T(1,128)} %get-tuple-element.36.gain_ref, bf16[2,4,2560,1024]{3,2,1,0:T(8,128)(2,1)} %bitcast.68, bf16[2,4,2560,1024]{3,2,1,0:T(8,128)(2,1)} %bitcast.69), custom_call_target="tpu_custom_call" | custom-call | flops 68719476736 | bytes 41943040 | tf_op jit(solution)/shard_map/pallas_call | solution.py:235
  634.0 81.2 %shard_map.121.refs_4_.refs_5_.refs_6_.refs_7_ = bf16[2048,4096]{1,0:T(8,128)(2,1)} custom-call(bf16[2048,2048]{1,0:T(8,128)(2,1)} %shard_map.119.x_ref.refs_12_, f32[1,2048]{1,0:T(1,128)} %get-tuple-element.36.gain_ref, bf16[2,4,2048,1024]{3,2,1,0:T(8,128)(2,1)} %bitcast.85, bf16[2,4,2048,1024]{3,2,1,0:T(8,128)(2,1)} %bitcast.86), custom_call_target="tpu_custom_call" | custom-call | flops 68719476736 | bytes 41943040 | tf_op jit(solution)/shard_map/pallas_call | solution.py:235
  717.8 49.0 %shard_map.122.refs_13_ = bf16[2048,2048]{1,0:T(8,128)(2,1)} custom-call(s32[2]{0:T(128)} %pad_add_fusion.place_ref, bf16[2048,4096]{1,0:T(8,128)(2,1)} %shard_map.120.refs_0_.refs_1_.refs_2_.refs_3_, bf16[2048,4096]{1,0:T(8,128)(2,1)} %shard_map.120.refs_0_.refs_1_.refs_2_.refs_3_, bf16[2048,4096]{1,0:T(8,128)(2,1)} %shard_map.120.refs_0_.refs_1_.refs_2_.refs_3_, ...), custom_call_target="tpu_custom_call" | custom-call | flops 34359738368 | bytes 50331648 | tf_op jit(solution)/shard_map/pallas_call | solution.py:309
  766.8 48.9 %shard_map.123.x_ref = bf16[2048,2048]{1,0:T(8,128)(2,1)} custom-call(s32[2]{0:T(128)} %pad_add_fusion.place_ref, bf16[2048,4096]{1,0:T(8,128)(2,1)} %shard_map.120.refs_0_.refs_1_.refs_2_.refs_3_, bf16[2048,4096]{1,0:T(8,128)(2,1)} %shard_map.120.refs_0_.refs_1_.refs_2_.refs_3_, ...), custom_call_target="tpu_custom_call", output_to_operand_aliasing={{}: (14, {})} | custom-call | flops 34359738368 | bytes 50331648 | tf_op jit(solution)/shard_map/pallas_call | solution.py:309
  815.7 38.1 %qkv.3 = (bf16[2048,2048]{1,0:T(8,128)(2,1)}, bf16[2048,512]{1,0:T(8,128)(2,1)}, bf16[2048,512]{1,0:T(8,128)(2,1)}) custom-call(bf16[2048,2048]{1,0:T(8,128)(2,1)} %shard_map.123.x_ref, f32[1,2048]{1,0:T(1,128)} %get-tuple-element.37.gain_ref, f32[1024,128]{1,0:T(8,128)} %copy.24.cos_ref, f32[1024,128]{1,0:T(8,128)} %copy.25.sin_ref, ...), custom_call_target="tpu_custom_call" | custom-call | flops 25769803776 | bytes 29360128 | tf_op jit(solution)/shard_map/qkv/pallas_call | solution.py:70
  853.8 45.0 %shard_map.126 = bf16[4,1,256,2048]{3,2,1,0:T(8,128)(2,1)} custom-call(bf16[4,2,256,2048]{3,2,1,0:T(8,128)(2,1)} %bitcast.91, bf16[4,2,256,512]{3,2,1,0:T(8,128)(2,1)} %bitcast.96, bf16[4,2,256,512]{3,2,1,0:T(8,128)(2,1)} %bitcast.98), custom_call_target="tpu_custom_call" | custom-call | flops 17179869184 | bytes 10485760 | tf_op jit(solution)/shard_map/pallas_call | solution.py:150
  898.8 13.9 shard_map.127
  912.7 5.1 all-to-all-start.2
  918.8 44.3 %shard_map.124 = bf16[4,1,256,2048]{3,2,1,0:T(8,128)(2,1)} custom-call(bf16[4,2,256,2048]{3,2,1,0:T(8,128)(2,1)} %bitcast.92, bf16[4,2,256,512]{3,2,1,0:T(8,128)(2,1)} %bitcast.97, bf16[4,2,256,512]{3,2,1,0:T(8,128)(2,1)} %bitcast.99), custom_call_target="tpu_custom_call" | custom-call | flops 17179869184 | bytes 10485760 | tf_op jit(solution)/shard_map/pallas_call | solution.py:150
  963.2 13.6 shard_map.125
  976.7 18.7 %all-to-all-done.2 = bf16[4,256,2048]{2,1,0:T(8,128)(2,1)} async-done(((bf16[4,256,2048]{2,1,0:T(8,128)(2,1)}), bf16[4,256,2048]{2,1,0:T(8,128)(2,1)}, u32[]{:S(2)}, u32[]{:S(2)}) %all-to-all-start.2) | async-done | bytes 4194336 | tf_op jit(solution)/shard_map/all_to_all | solution.py:335
  995.5 5.3 all-to-all-start.1
  1000.8 42.7 %shard_map.130.refs_0_ = bf16[2048,4096]{1,0:T(8,128)(2,1)} custom-call(bf16[1024,2048]{1,0:T(8,128)(2,1)} %bitcast.39.x_ref.refs_12_, f32[1,2048]{1,0:T(1,128)} %get-tuple-element.35.gain_ref, bf16[2,4,2048,1024]{3,2,1,0:T(8,128)(2,1)} %bitcast.77, bf16[2,4,2048,1024]{3,2,1,0:T(8,128)(2,1)} %bitcast.78), custom_call_target="tpu_custom_call" | custom-call | flops 34359738368 | bytes 37748736 | tf_op jit(solution)/shard_map/pallas_call | solution.py:235
  1043.6 127.7 %all-gather.27.cloned.1.call-done = bf16[16384,1024]{1,0:T(8,128)(2,1)} async-done(((bf16[2048,1024]{1,0:T(8,128)(2,1)}), bf16[16384,1024]{1,0:T(8,128)(2,1)}) %all-gather.27.cloned.1.call-update) | async-done | bytes 33554448 | tf_op jit(solution)/shard_map/all_gather | solution.py:331
  1171.3 42.7 %shard_map.128.refs_0_ = bf16[2048,4096]{1,0:T(8,128)(2,1)} custom-call(bf16[1024,2048]{1,0:T(8,128)(2,1)} %bitcast.39.x_ref.refs_12_, f32[1,2048]{1,0:T(1,128)} %get-tuple-element.35.gain_ref, bf16[2,4,2048,1024]{3,2,1,0:T(8,128)(2,1)} %bitcast.81, bf16[2,4,2048,1024]{3,2,1,0:T(8,128)(2,1)} %bitcast.82), custom_call_target="tpu_custom_call" | custom-call | flops 34359738368 | bytes 37748736 | tf_op jit(solution)/shard_map/pallas_call | solution.py:235
  1214.0 42.9 %shard_map.131.refs_4_.refs_5_.refs_6_.refs_7_ = bf16[2048,4096]{1,0:T(8,128)(2,1)} custom-call(bf16[1024,2048]{1,0:T(8,128)(2,1)} %bitcast.33.x_ref.refs_13_, f32[1,2048]{1,0:T(1,128)} %get-tuple-element.35.gain_ref, bf16[2,4,2048,1024]{3,2,1,0:T(8,128)(2,1)} %bitcast.79, bf16[2,4,2048,1024]{3,2,1,0:T(8,128)(2,1)} %bitcast.80, ...), custom_call_target="tpu_custom_call", output_to_operand_aliasing={{}: (4, {})} | custom-call | flops 34359738368 | bytes 37748736 | tf_op jit(solution)/shard_map/pallas_call | solution.py:235
  1256.9 42.9 %shard_map.129.refs_0_.refs_1_.refs_2_.refs_3_ = bf16[2048,4096]{1,0:T(8,128)(2,1)} custom-call(bf16[1024,2048]{1,0:T(8,128)(2,1)} %bitcast.33.x_ref.refs_13_, f32[1,2048]{1,0:T(1,128)} %get-tuple-element.35.gain_ref, bf16[2,4,2048,1024]{3,2,1,0:T(8,128)(2,1)} %bitcast.83, bf16[2,4,2048,1024]{3,2,1,0:T(8,128)(2,1)} %bitcast.84, ...), custom_call_target="tpu_custom_call", output_to_operand_aliasing={{}: (4, {})} | custom-call | flops 34359738368 | bytes 37748736 | tf_op jit(solution)/shard_map/pallas_call | solution.py:235
  1299.8 30.2 %shard_map.132.refs_14_ = bf16[4,2,256,2048]{3,2,1,0:T(8,128)(2,1)} custom-call(s32[2]{0:T(128)} %pad_add_fusion.place_ref, bf16[2048,4096]{1,0:T(8,128)(2,1)} %shard_map.129.refs_0_.refs_1_.refs_2_.refs_3_, bf16[2048,4096]{1,0:T(8,128)(2,1)} %shard_map.129.refs_0_.refs_1_.refs_2_.refs_3_, bf16[2048,4096]{1,0:T(8,128)(2,1)} %shard_map.129.refs_0_.refs_1_.refs_2_.refs_3_, ...), custom_call_target="tpu_custom_call" | custom-call | flops 17179869184 | bytes 41943040 | tf_op jit(solution)/shard_map/pallas_call | solution.py:309
  1330.1 30.2 %shard_map.133.refs_14_ = bf16[4,2,256,2048]{3,2,1,0:T(8,128)(2,1)} custom-call(s32[2]{0:T(128)} %pad_add_fusion.place_ref, bf16[2048,4096]{1,0:T(8,128)(2,1)} %shard_map.129.refs_0_.refs_1_.refs_2_.refs_3_, bf16[2048,4096]{1,0:T(8,128)(2,1)} %shard_map.129.refs_0_.refs_1_.refs_2_.refs_3_, ...), custom_call_target="tpu_custom_call", output_to_operand_aliasing={{}: (15, {})} | custom-call | flops 17179869184 | bytes 41943040 | tf_op jit(solution)/shard_map/pallas_call | solution.py:309
  1360.3 48.8 %shard_map.134 = bf16[4,2,256,2048]{3,2,1,0:T(8,128)(2,1)} custom-call(s32[2]{0:T(128)} %pad_add_fusion.place_ref, bf16[2048,4096]{1,0:T(8,128)(2,1)} %shard_map.129.refs_0_.refs_1_.refs_2_.refs_3_, bf16[2048,4096]{1,0:T(8,128)(2,1)} %shard_map.129.refs_0_.refs_1_.refs_2_.refs_3_, ...), custom_call_target="tpu_custom_call", output_to_operand_aliasing={{}: (15, {})} | custom-call | flops 34359738368 | bytes 50331648 | tf_op jit(solution)/shard_map/pallas_call | solution.py:309
  (80 shorter events, 25.9 us)
Async XLA Ops:
  6.5 398.2 %all-gather.19.cloned.1.call-start = ((), (), s32[]{:S(2)}) async-start(), calls=%async_computation.5 | async-start | bytes 14155776 | tf_op jit(solution)/shard_map/all_gather | solution.py:331
  6.5 1.8 copy-start.2
  6.5 1.8 copy-start.3
  8.4 2.1 copy-start
  10.4 518.2 %all-gather.21.cloned.1.call-start = ((), (), s32[]{:S(2)}) async-start(), calls=%async_computation.6 | async-start | bytes 47185920 | tf_op jit(solution)/shard_map/all_gather | solution.py:331
  34.0 600.0 %all-gather.23.cloned.1.call-start = ((), (), s32[]{:S(2)}) async-start(), calls=%async_computation.7 | async-start | bytes 37748736 | tf_op jit(solution)/shard_map/all_gather | solution.py:331
  38.8 776.9 %all-gather.25.cloned.1.call-start = ((), (), s32[]{:S(2)}) async-start(), calls=%async_computation.8 | async-start | bytes 14155776 | tf_op jit(solution)/shard_map/all_gather | solution.py:331
  41.1 857.7 %all-gather.15.cloned.1.call-start = ((), (), s32[]{:S(2)}) async-start(), calls=%async_computation.3 | async-start | bytes 9437184 | tf_op jit(solution)/shard_map/all_gather | solution.py:331
  41.7 959.1 %all-gather.29.cloned.1.call-start = ((), (), s32[]{:S(2)}) async-start(), calls=%async_computation.10 | async-start | bytes 37748736 | tf_op jit(solution)/shard_map/all_gather | solution.py:331
  47.8 1123.5 %all-gather.27.cloned.1.call-start = ((), (), s32[]{:S(2)}) async-start(), calls=%async_computation.9 | async-start | bytes 37748736 | tf_op jit(solution)/shard_map/all_gather | solution.py:331
  56.7 167.1 %collective-permute-start.2 = (bf16[2048,1024]{1,0:T(8,128)(2,1)}, bf16[2048,1024]{1,0:T(8,128)(2,1)}, u32[]{:S(2)}, u32[]{:S(2)}) collective-permute-start(bf16[2048,1024]{1,0:T(8,128)(2,1)} %slice_bitcast_fusion.refs_8_), channel_id=1, source_target_pairs={{0,2},{1,3},{2,0},{3,1},{4,6},{5,7},{6,4},{7,5}} | collective-permute-start | bytes 12582920 | tf_op jit(solution)/shard_map/ppermute | solution.py:338
  59.2 345.5 %all-to-all-start = ((bf16[8,256,2048]{2,1,0:T(8,128)(2,1)}), bf16[8,256,2048]{2,1,0:T(8,128)(2,1)}, u32[]{:S(2)}, u32[]{:S(2)}) async-start(bf16[8,256,2048]{2,1,0:T(8,128)(2,1)} %param.12), calls=%async_computation | async-start | bytes 16777216 | tf_op jit(solution)/shard_map/all_to_all | solution.py:335
  65.0 166.5 %copy-start.1 = (f32[1024,32]{0,1:T(8,128)S(1)}, f32[1024,32]{0,1:T(8,128)}, u32[]{:S(2)}) copy-start(f32[1024,32]{0,1:T(8,128)} %param.16) | copy-start | bytes 393220
  65.0 1295.3 %all-gather.17.cloned.1.call-start = ((), (), s32[]{:S(2)}) async-start(), calls=%async_computation.4 | async-start | bytes 18874368 | tf_op jit(solution)/shard_map/all_gather | solution.py:331
  65.2 170.9 %collective-permute-start = (bf16[2048,1024]{1,0:T(8,128)(2,1)}, bf16[2048,1024]{1,0:T(8,128)(2,1)}, u32[]{:S(2)}, u32[]{:S(2)}) collective-permute-start(bf16[2048,1024]{1,0:T(8,128)(2,1)} %slice_bitcast_fusion.refs_8_), channel_id=1, source_target_pairs={{0,4},{4,0},{1,5},{5,1},{2,6},{6,2},{3,7},{7,3}} | collective-permute-start | bytes 12582920 | tf_op jit(solution)/shard_map/ppermute | solution.py:338
  223.9 180.8 %collective-permute-start.3 = (bf16[2048,1024]{1,0:T(8,128)(2,1)}, bf16[2048,1024]{1,0:T(8,128)(2,1)}, u32[]{:S(2)}, u32[]{:S(2)}) collective-permute-start(bf16[2048,1024]{1,0:T(8,128)(2,1)} %collective-permute-done.2.refs_10_), channel_id=1, source_target_pairs={{0,4},{4,0},{1,5},{5,1},{2,6},{6,2},{3,7},{7,3}} | collective-permute-start | bytes 12582920 | tf_op jit(solution)/shard_map/ppermute | solution.py:338
  225.4 492.3 %collective-permute-start.5 = (bf16[2048,1024]{1,0:T(8,128)(2,1)}, bf16[2048,1024]{1,0:T(8,128)(2,1)}, u32[]{:S(2)}, u32[]{:S(2)}) collective-permute-start(bf16[2048,1024]{1,0:T(8,128)(2,1)} %slice_bitcast_fusion.refs_8_), channel_id=1, source_target_pairs={{0,1},{1,0},{2,3},{3,2},{4,5},{5,4},{6,7},{7,6}} | collective-permute-start | bytes 12582920 | tf_op jit(solution)/shard_map/ppermute | solution.py:338
  231.5 1.2 copy-start.4
  231.5 2.8 copy-start.5
  231.5 3.4 copy-start.6
  231.5 483.7 %collective-permute-start.9 = (bf16[2048,512]{1,0:T(8,128)(2,1)}, bf16[2048,512]{1,0:T(8,128)(2,1)}, u32[]{:S(2)}, u32[]{:S(2)}) collective-permute-start(bf16[2048,512]{1,0:T(8,128)(2,1)} %get-tuple-element.17.refs_8_), channel_id=1, source_target_pairs={{0,2},{1,3},{2,0},{3,1},{4,6},{5,7},{6,4},{7,5}} | collective-permute-start | bytes 6291464 | tf_op jit(solution)/shard_map/ppermute | solution.py:338
  235.5 482.2 %collective-permute-start.6 = (bf16[2048,1024]{1,0:T(8,128)(2,1)}, bf16[2048,1024]{1,0:T(8,128)(2,1)}, u32[]{:S(2)}, u32[]{:S(2)}) collective-permute-start(bf16[2048,1024]{1,0:T(8,128)(2,1)} %collective-permute-done.2.refs_10_), channel_id=1, source_target_pairs={{0,1},{1,0},{2,3},{3,2},{4,5},{5,4},{6,7},{7,6}} | collective-permute-start | bytes 12582920 | tf_op jit(solution)/shard_map/ppermute | solution.py:338
  236.2 530.6 %collective-permute-start.1 = (bf16[2048,1024]{1,0:T(8,128)(2,1)}, bf16[2048,1024]{1,0:T(8,128)(2,1)}, u32[]{:S(2)}, u32[]{:S(2)}) collective-permute-start(bf16[2048,1024]{1,0:T(8,128)(2,1)} %collective-permute-done.refs_8_), channel_id=1, source_target_pairs={{0,1},{1,0},{2,3},{3,2},{4,5},{5,4},{6,7},{7,6}} | collective-permute-start | bytes 12582920 | tf_op jit(solution)/shard_map/ppermute | solution.py:338
  404.7 362.0 %collective-permute-start.4 = (bf16[2048,1024]{1,0:T(8,128)(2,1)}, bf16[2048,1024]{1,0:T(8,128)(2,1)}, u32[]{:S(2)}, u32[]{:S(2)}) collective-permute-start(bf16[2048,1024]{1,0:T(8,128)(2,1)} %collective-permute-done.3.refs_10_), channel_id=1, source_target_pairs={{0,1},{1,0},{2,3},{3,2},{4,5},{5,4},{6,7},{7,6}} | collective-permute-start | bytes 12582920 | tf_op jit(solution)/shard_map/ppermute | solution.py:338
  715.2 203.1 %collective-permute-start.7 = (bf16[2048,512]{1,0:T(8,128)(2,1)}, bf16[2048,512]{1,0:T(8,128)(2,1)}, u32[]{:S(2)}, u32[]{:S(2)}) collective-permute-start(bf16[2048,512]{1,0:T(8,128)(2,1)} %get-tuple-element.17.refs_8_), channel_id=1, source_target_pairs={{0,4},{4,0},{1,5},{5,1},{2,6},{6,2},{3,7},{7,3}} | collective-permute-start | bytes 6291464 | tf_op jit(solution)/shard_map/ppermute | solution.py:338
  717.7 201.1 %collective-permute-start.10 = (bf16[2048,512]{1,0:T(8,128)(2,1)}, bf16[2048,512]{1,0:T(8,128)(2,1)}, u32[]{:S(2)}, u32[]{:S(2)}) collective-permute-start(bf16[2048,512]{1,0:T(8,128)(2,1)} %collective-permute-done.9.refs_10_), channel_id=1, source_target_pairs={{0,4},{4,0},{1,5},{5,1},{2,6},{6,2},{3,7},{7,3}} | collective-permute-start | bytes 6291464 | tf_op jit(solution)/shard_map/ppermute | solution.py:338
  912.7 82.8 %all-to-all-start.2 = ((bf16[4,256,2048]{2,1,0:T(8,128)(2,1)}), bf16[4,256,2048]{2,1,0:T(8,128)(2,1)}, u32[]{:S(2)}, u32[]{:S(2)}) async-start(bf16[4,256,2048]{2,1,0:T(8,128)(2,1)} %bitcast.73), calls=%async_computation.2 | async-start | bytes 8388608 | tf_op jit(solution)/shard_map/all_to_all | solution.py:335
  917.8 382.0 %collective-permute-start.12 = (bf16[2048,512]{1,0:T(8,128)(2,1)}, bf16[2048,512]{1,0:T(8,128)(2,1)}, u32[]{:S(2)}, u32[]{:S(2)}) collective-permute-start(bf16[2048,512]{1,0:T(8,128)(2,1)} %get-tuple-element.17.refs_8_), channel_id=1, source_target_pairs={{0,1},{1,0},{2,3},{3,2},{4,5},{5,4},{6,7},{7,6}} | collective-permute-start | bytes 6291464 | tf_op jit(solution)/shard_map/ppermute | solution.py:338
  918.3 381.5 %collective-permute-start.13 = (bf16[2048,512]{1,0:T(8,128)(2,1)}, bf16[2048,512]{1,0:T(8,128)(2,1)}, u32[]{:S(2)}, u32[]{:S(2)}) collective-permute-start(bf16[2048,512]{1,0:T(8,128)(2,1)} %collective-permute-done.9.refs_10_), channel_id=1, source_target_pairs={{0,1},{1,0},{2,3},{3,2},{4,5},{5,4},{6,7},{7,6}} | collective-permute-start | bytes 6291464 | tf_op jit(solution)/shard_map/ppermute | solution.py:338
  918.3 411.7 %collective-permute-start.8 = (bf16[2048,512]{1,0:T(8,128)(2,1)}, bf16[2048,512]{1,0:T(8,128)(2,1)}, u32[]{:S(2)}, u32[]{:S(2)}) collective-permute-start(bf16[2048,512]{1,0:T(8,128)(2,1)} %collective-permute-done.7.refs_8_), channel_id=1, source_target_pairs={{0,1},{1,0},{2,3},{3,2},{4,5},{5,4},{6,7},{7,6}} | collective-permute-start | bytes 6291464 | tf_op jit(solution)/shard_map/ppermute | solution.py:338
  918.8 411.3 %collective-permute-start.11 = (bf16[2048,512]{1,0:T(8,128)(2,1)}, bf16[2048,512]{1,0:T(8,128)(2,1)}, u32[]{:S(2)}, u32[]{:S(2)}) collective-permute-start(bf16[2048,512]{1,0:T(8,128)(2,1)} %collective-permute-done.10.refs_10_), channel_id=1, source_target_pairs={{0,1},{1,0},{2,3},{3,2},{4,5},{5,4},{6,7},{7,6}} | collective-permute-start | bytes 6291464 | tf_op jit(solution)/shard_map/ppermute | solution.py:338
  995.5 218.5 %all-to-all-start.1 = ((bf16[4,256,2048]{2,1,0:T(8,128)(2,1)}), bf16[4,256,2048]{2,1,0:T(8,128)(2,1)}, u32[]{:S(2)}, u32[]{:S(2)}) async-start(bf16[4,256,2048]{2,1,0:T(8,128)(2,1)} %bitcast.74), calls=%async_computation.1 | async-start | bytes 8388608 | tf_op jit(solution)/shard_map/all_to_all | solution.py:335
Sparse Core Ops, SparseCore 0:
  10.6 86.0 all-gather.18
  98.5 357.4 all-gather.20
  457.8 156.2 all-gather.22
  615.8 66.4 all-gather.24
  684.0 60.3 all-gather.14
  746.0 224.1 all-gather.28
  972.0 199.2 all-gather.26
  1173.1 84.1 all-gather.16

commit v5 on v4

--- a/solution.py
+++ b/solution.py
@@ -321,6 +321,72 @@
     )(place, *operands)
 
 
+def down_last_kernel(place_ref, *refs, count, steps):
+    za, zb = refs[:count], refs[count:2 * count]
+    groups = [refs[(2 + g) * count:(3 + g) * count] for g in range(3)]
+    r_refs, o_ref = refs[5 * count:5 * count + 2], refs[-1]
+    half = za[0].shape[1]
+    step = pl.program_id(0) % steps
+    first = pl.program_id(0) < 2 * steps
+
+    def run(ws):
+        w = jnp.concatenate([w[h * half:(h + 1) * half, :] for h in range(2) for w in ws], axis=0)
+        z = jnp.concatenate([z[...] for z in za + zb], axis=1)
+        resid = jnp.where(first, r_refs[0][...].astype(F32), r_refs[1][...].astype(F32))
+        out = (resid + dot(z, w)).astype(BF16)
+        o_ref[...] = out.reshape(o_ref.shape)
+
+    for g, here in enumerate((step < 2, jnp.logical_and(step >= 2, step < 4), step >= 4)):
+        pl.when(here)(functools.partial(run, groups[g]))
+
+
+def down_last(place, za, zb, own, other, rest, resids, sources):
+    tokens = za.shape[0]
+    width = resids[0].shape[1]
+    count = len(own)
+    half = za.shape[1] // count
+    block, rows = 256, 512
+    steps = width // block
+    positions = tokens // 2 // sources
+    assert rest.shape[3] == own[0].shape[1] == 2 * block and rest.shape[0] == 2 and rows * 4 == tokens
+
+    def rest_block(j):
+        t = jnp.maximum(j - 4, 0)
+        return t // 2, t % 2
+
+    def column(i, place):
+        j = i % steps
+        y, c = rest_block(j)
+        side = jnp.where(j < 2, place[1], place[1] ^ 1)
+        return jnp.where(j < 4, side * 4 + j % 2, y * 4 + 2 + c)
+
+    def rest_spec(k):
+        def index(i, place):
+            y, c = rest_block(i % steps)
+            return y, place[0] ^ k, 0, c
+
+        return pl.BlockSpec((None, None, 2 * half, block), index)
+
+    in_specs = [pl.BlockSpec((rows, half), lambda i, place, k=k: (i // steps, place[0] ^ k)) for k in range(count)] * 2
+    in_specs += [pl.BlockSpec((2 * half, block), lambda i, place: (0, jnp.minimum(i % steps, 1)))] * count
+    in_specs += [pl.BlockSpec((2 * half, block), lambda i, place: (0, jnp.clip(i % steps - 2, 0, 1)))] * count
+    in_specs += [rest_spec(k) for k in range(count)]
+    in_specs += [pl.BlockSpec((rows, block), lambda i, place: (i // steps % 2, column(i, place)))] * 2
+    return pl.pallas_call(
+        functools.partial(down_last_kernel, count=count, steps=steps),
+        grid_spec=pltpu.PrefetchScalarGridSpec(
+            num_scalar_prefetch=1,
+            grid=(tokens // rows * steps,),
+            in_specs=in_specs,
+            out_specs=pl.BlockSpec((rows // positions, 1, positions, block), lambda i, place: (i // steps % 2, i // steps // 2, 0, column(i, place))),
+        ),
+        out_shape=jax.ShapeDtypeStruct((sources, 2, positions, width), BF16),
+        compiler_params=params(),
+        cost_estimate=pl.CostEstimate(flops=4 * tokens * za.shape[1] * width, bytes_accessed=4 * za.size + 4 * za.shape[1] * width, transcendentals=0),
+        name="down_last",
+    )(place, *[za] * count, *[zb] * count, *own, *other, *[rest] * count, *resids)
+
+
 def solution(mesh):
     act_spec = P('fsdp', 'model', None)
     col_spec = P(None, 'fsdp', 'model')
@@ -375,7 +441,6 @@
             wqkv, wo, wgua, wgub, (own, other), rest = gathered[l]
             gain = gain_mlp[l][None]
             wo_block = wo.shape[2] // w_o.shape[1] - 1
-            parts = 1 if rest is None else 2
             q, k, v = project_qkv(x, gain_attn[l][None], cos, sin, wqkv)
             x4 = x.reshape(ms, seqs, -1, x.shape[1])
             if l < layers - 1:
@@ -393,10 +458,11 @@
                 za = gate_up(m, gain, wgua, half, len(resids), i, za)
             for i, m in enumerate(resids):
                 zb = gate_up(m, gain, wgub, half, len(resids), i, zb)
-            x = down(place, za, zb, own, resids, split, 0, 0, parts)
-            x = down(place, za, zb, other, resids, split, 1, 0, parts, x)
-            if rest is not None:
-                x = down(place, za, zb, rest, resids, split, 0, 1, parts, x)
+            if rest is None:
+                x = down(place, za, zb, own, resids, split)
+                x = down(place, za, zb, other, resids, split, 1, onto=x)
+            else:
+                x = down_last(place, za, zb, own, other, rest, resids, ms)
         return x.reshape(x_in.shape)
 
     return jax.shard_map(device_step, mesh=mesh, in_specs=(act_spec, P(), P(), P(), P(), col_spec, col_spec, col_spec, row_spec, col_spec, col_spec, row_spec), out_specs=act_spec, check_vma=False)

time: 1420 us -> 1420 us (level)
    pallas_call x5 -> x2, Pallas kernels: 207 us -> 97.9 us  [down(): pl.pallas_call(functools.partial(down_kernel, count=count, resids=len(res...]
    pallas_call x0 -> x1, Pallas kernels: none -> 108 us  [down_last(): pl.pallas_call(functools.partial(down_last_kernel, count=count, steps=ste...]
  transfers between devices with their start and end apart: 25 -> 25, of which waited for: 4 -> 4; matrix products, arithmetic and copies ran while one was open for 4% -> 4% of each run, Pallas kernels for 56% -> 52%
where the time goes in v5:
time: 1420 us; the launch traced here: 1410 us
  Pallas kernels  844 us (59%)
  waiting for transfers between devices  468 us (33%)
  local copies, waits for them, and re-layouts  31.8 us (2%)
  other arithmetic  28.9 us (2%)
  starting transfers between devices  27.8 us (2%)
    pallas_call x6, Pallas kernels, gate_up(): pl.pallas_call(functools.partial(gate_up_kernel, chunk=512), grid=(ms * p...  333 us
    ppermute x14, waiting for transfers between devices, swap(): lax.ppermute(block, axis, [(i, i ^ bit) for i in range(mesh.shape[axis])])  324 us
    pallas_call x3, Pallas kernels, attend(): pl.pallas_call(attention_kernel, grid=(count * blocks,), in_specs=[pl.Blo...  176 us
    all_gather x8, waiting for transfers between devices, gather(): full = lax.all_gather(block, ('fsdp', 'model'), axis=0, tiled=False)  125 us
    pallas_call x1, Pallas kernels, down_last(): pl.pallas_call(functools.partial(down_last_kernel, count=count, steps=ste...  108 us
    pallas_call x2, Pallas kernels, down(): pl.pallas_call(functools.partial(down_kernel, count=count, resids=len(res...  97.9 us
    pallas_call x2, Pallas kernels, project_qkv(): pl.pallas_call(qkv_kernel, grid=(blocks,), in_specs=[pl.BlockSpec((tokens...  75.8 us
    pallas_call x3, Pallas kernels, out_proj(): pl.pallas_call(functools.partial(out_proj_kernel, chunk=512), grid=(ys *...  52.6 us
  transfers between devices with their start and end apart: 25, of which 4 were waited for; matrix products, arithmetic and copies ran while one was open for 4% of the time, Pallas kernels for 52%

profile of v5, /device:TPU:0, one launch (start us, length us, event | category | flops | bytes accessed | tf_op | source)
XLA Modules:
  0.0 1413.6 jit_solution(7439028984639696250)
XLA Ops:
  13.2 11.8 slice_bitcast_fusion.2
  25.0 11.2 pad_maximum_fusion
  36.3 4.7 pad_maximum_fusion.1
  44.1 4.8 pad_maximum_fusion.3
  48.9 4.0 pad_maximum_fusion.2
  53.0 4.8 slice_bitcast_fusion.refs_8_
  57.8 3.5 collective-permute-start.2
  61.3 5.6 all-to-all-start
  69.0 155.2 %collective-permute-done.2.refs_10_ = bf16[2048,1024]{1,0:T(8,128)(2,1)} collective-permute-done((bf16[2048,1024]{1,0:T(8,128)(2,1)}, bf16[2048,1024]{1,0:T(8,128)(2,1)}, u32[]{:S(2)}, u32[]{:S(2)}) %collective-permute-start.2) | collective-permute-done | bytes 4194336 | tf_op jit(solution)/shard_map/ppermute | solution.py:404
  225.8 6.5 fusion
  237.3 168.9 %collective-permute-done.3.refs_10_ = bf16[2048,1024]{1,0:T(8,128)(2,1)} collective-permute-done((bf16[2048,1024]{1,0:T(8,128)(2,1)}, bf16[2048,1024]{1,0:T(8,128)(2,1)}, u32[]{:S(2)}, u32[]{:S(2)}) %collective-permute-start.3) | collective-permute-done | bytes 4194336 | tf_op jit(solution)/shard_map/ppermute | solution.py:404
  406.2 37.7 %qkv.2 = (bf16[2048,2048]{1,0:T(8,128)(2,1)}, bf16[2048,512]{1,0:T(8,128)(2,1)}, bf16[2048,512]{1,0:T(8,128)(2,1)}) custom-call(bf16[2048,2048]{1,0:T(8,128)(2,1)} %bitcast.2.x_ref, f32[1,2048]{1,0:T(1,128)} %get-tuple-element.38.gain_ref, f32[1024,128]{1,0:T(8,128)} %copy.22.cos_ref, f32[1024,128]{1,0:T(8,128)} %copy.23.sin_ref, ...), custom_call_target="tpu_custom_call" | custom-call | flops 25769803776 | bytes 29360128 | tf_op jit(solution)/shard_map/qkv/pallas_call | solution.py:70
  443.9 86.2 %shard_map.118 = bf16[4,2,256,2048]{3,2,1,0:T(8,128)(2,1)} custom-call(bf16[4,2,256,2048]{3,2,1,0:T(8,128)(2,1)} %bitcast.93, bf16[4,2,256,512]{3,2,1,0:T(8,128)(2,1)} %bitcast.100, bf16[4,2,256,512]{3,2,1,0:T(8,128)(2,1)} %bitcast.101), custom_call_target="tpu_custom_call" | custom-call | flops 34359738368 | bytes 20971520 | tf_op jit(solution)/shard_map/pallas_call | solution.py:150
  530.2 24.5 %shard_map.119.x_ref.refs_12_ = bf16[2048,2048]{1,0:T(8,128)(2,1)} custom-call(bf16[2048,2048]{1,0:T(8,128)(2,1)} %bitcast.68, bf16[2,4,2560,1024]{3,2,1,0:T(8,128)(2,1)} %bitcast.63, bf16[4,2,256,2048]{3,2,1,0:T(8,128)(2,1)} %bitcast.17.r_ref), custom_call_target="tpu_custom_call" | custom-call | flops 17179869184 | bytes 33554432 | tf_op jit(solution)/shard_map/pallas_call | solution.py:185
  554.7 80.9 %shard_map.120.refs_0_.refs_1_.refs_2_.refs_3_ = bf16[2048,4096]{1,0:T(8,128)(2,1)} custom-call(bf16[2048,2048]{1,0:T(8,128)(2,1)} %shard_map.119.x_ref.refs_12_, f32[1,2048]{1,0:T(1,128)} %get-tuple-element.36.gain_ref, bf16[2,4,2560,1024]{3,2,1,0:T(8,128)(2,1)} %bitcast.64, bf16[2,4,2560,1024]{3,2,1,0:T(8,128)(2,1)} %bitcast.65), custom_call_target="tpu_custom_call" | custom-call | flops 68719476736 | bytes 41943040 | tf_op jit(solution)/shard_map/pallas_call | solution.py:235
  635.6 81.2 %shard_map.121.refs_4_.refs_5_.refs_6_.refs_7_ = bf16[2048,4096]{1,0:T(8,128)(2,1)} custom-call(bf16[2048,2048]{1,0:T(8,128)(2,1)} %shard_map.119.x_ref.refs_12_, f32[1,2048]{1,0:T(1,128)} %get-tuple-element.36.gain_ref, bf16[2,4,2048,1024]{3,2,1,0:T(8,128)(2,1)} %bitcast.81, bf16[2,4,2048,1024]{3,2,1,0:T(8,128)(2,1)} %bitcast.82), custom_call_target="tpu_custom_call" | custom-call | flops 68719476736 | bytes 41943040 | tf_op jit(solution)/shard_map/pallas_call | solution.py:235
  719.1 49.0 %shard_map.122.refs_13_ = bf16[2048,2048]{1,0:T(8,128)(2,1)} custom-call(s32[2]{0:T(128)} %pad_add_fusion.place_ref, bf16[2048,4096]{1,0:T(8,128)(2,1)} %shard_map.120.refs_0_.refs_1_.refs_2_.refs_3_, bf16[2048,4096]{1,0:T(8,128)(2,1)} %shard_map.120.refs_0_.refs_1_.refs_2_.refs_3_, bf16[2048,4096]{1,0:T(8,128)(2,1)} %shard_map.120.refs_0_.refs_1_.refs_2_.refs_3_, ...), custom_call_target="tpu_custom_call" | custom-call | flops 34359738368 | bytes 50331648 | tf_op jit(solution)/shard_map/pallas_call | solution.py:309
  768.1 48.9 %shard_map.123.x_ref = bf16[2048,2048]{1,0:T(8,128)(2,1)} custom-call(s32[2]{0:T(128)} %pad_add_fusion.place_ref, bf16[2048,4096]{1,0:T(8,128)(2,1)} %shard_map.120.refs_0_.refs_1_.refs_2_.refs_3_, bf16[2048,4096]{1,0:T(8,128)(2,1)} %shard_map.120.refs_0_.refs_1_.refs_2_.refs_3_, ...), custom_call_target="tpu_custom_call", output_to_operand_aliasing={{}: (14, {})} | custom-call | flops 34359738368 | bytes 50331648 | tf_op jit(solution)/shard_map/pallas_call | solution.py:309
  817.1 38.1 %qkv.3 = (bf16[2048,2048]{1,0:T(8,128)(2,1)}, bf16[2048,512]{1,0:T(8,128)(2,1)}, bf16[2048,512]{1,0:T(8,128)(2,1)}) custom-call(bf16[2048,2048]{1,0:T(8,128)(2,1)} %shard_map.123.x_ref, f32[1,2048]{1,0:T(1,128)} %get-tuple-element.37.gain_ref, f32[1024,128]{1,0:T(8,128)} %copy.22.cos_ref, f32[1024,128]{1,0:T(8,128)} %copy.23.sin_ref, ...), custom_call_target="tpu_custom_call" | custom-call | flops 25769803776 | bytes 29360128 | tf_op jit(solution)/shard_map/qkv/pallas_call | solution.py:70
  855.2 45.0 %shard_map.126 = bf16[4,1,256,2048]{3,2,1,0:T(8,128)(2,1)} custom-call(bf16[4,2,256,2048]{3,2,1,0:T(8,128)(2,1)} %bitcast.91, bf16[4,2,256,512]{3,2,1,0:T(8,128)(2,1)} %bitcast.96, bf16[4,2,256,512]{3,2,1,0:T(8,128)(2,1)} %bitcast.98), custom_call_target="tpu_custom_call" | custom-call | flops 17179869184 | bytes 10485760 | tf_op jit(solution)/shard_map/pallas_call | solution.py:150
  900.2 13.7 shard_map.127
  913.9 5.1 all-to-all-start.2
  920.0 44.3 %shard_map.124 = bf16[4,1,256,2048]{3,2,1,0:T(8,128)(2,1)} custom-call(bf16[4,2,256,2048]{3,2,1,0:T(8,128)(2,1)} %bitcast.92, bf16[4,2,256,512]{3,2,1,0:T(8,128)(2,1)} %bitcast.97, bf16[4,2,256,512]{3,2,1,0:T(8,128)(2,1)} %bitcast.99), custom_call_target="tpu_custom_call" | custom-call | flops 17179869184 | bytes 10485760 | tf_op jit(solution)/shard_map/pallas_call | solution.py:150
  964.3 14.4 %shard_map.125 = bf16[1024,2048]{1,0:T(8,128)(2,1)} custom-call(bf16[1024,2048]{1,0:T(8,128)(2,1)} %bitcast.94, bf16[2,4,512,1024]{3,2,1,0:T(8,128)(2,1)} %bitcast.90, bf16[4,2,256,2048]{3,2,1,0:T(8,128)(2,1)} %bitcast.67), custom_call_target="tpu_custom_call" | custom-call | flops 8589934592 | bytes 20971520 | tf_op jit(solution)/shard_map/pallas_call | solution.py:185
  978.7 18.0 %all-to-all-done.2 = bf16[4,256,2048]{2,1,0:T(8,128)(2,1)} async-done(((bf16[4,256,2048]{2,1,0:T(8,128)(2,1)}), bf16[4,256,2048]{2,1,0:T(8,128)(2,1)}, u32[]{:S(2)}, u32[]{:S(2)}) %all-to-all-start.2) | async-done | bytes 4194336 | tf_op jit(solution)/shard_map/all_to_all | solution.py:401
  996.7 5.3 all-to-all-start.1
  1002.1 42.7 %shard_map.130.refs_0_ = bf16[2048,4096]{1,0:T(8,128)(2,1)} custom-call(bf16[1024,2048]{1,0:T(8,128)(2,1)} %bitcast.39.x_ref.refs_20_, f32[1,2048]{1,0:T(1,128)} %get-tuple-element.35.gain_ref, bf16[2,4,2048,1024]{3,2,1,0:T(8,128)(2,1)} %bitcast.73, bf16[2,4,2048,1024]{3,2,1,0:T(8,128)(2,1)} %bitcast.74), custom_call_target="tpu_custom_call" | custom-call | flops 34359738368 | bytes 37748736 | tf_op jit(solution)/shard_map/pallas_call | solution.py:235
  1044.8 124.9 %all-gather.27.cloned.1.call-done = bf16[16384,1024]{1,0:T(8,128)(2,1)} async-done(((bf16[2048,1024]{1,0:T(8,128)(2,1)}), bf16[16384,1024]{1,0:T(8,128)(2,1)}) %all-gather.27.cloned.1.call-update) | async-done | bytes 33554448 | tf_op jit(solution)/shard_map/all_gather | solution.py:397
  1169.7 42.7 %shard_map.128.refs_0_ = bf16[2048,4096]{1,0:T(8,128)(2,1)} custom-call(bf16[1024,2048]{1,0:T(8,128)(2,1)} %bitcast.39.x_ref.refs_20_, f32[1,2048]{1,0:T(1,128)} %get-tuple-element.35.gain_ref, bf16[2,4,2048,1024]{3,2,1,0:T(8,128)(2,1)} %bitcast.77, bf16[2,4,2048,1024]{3,2,1,0:T(8,128)(2,1)} %bitcast.78), custom_call_target="tpu_custom_call" | custom-call | flops 34359738368 | bytes 37748736 | tf_op jit(solution)/shard_map/pallas_call | solution.py:235
  1212.4 42.8 %shard_map.131.refs_4_.refs_5_.refs_6_.refs_7_ = bf16[2048,4096]{1,0:T(8,128)(2,1)} custom-call(bf16[1024,2048]{1,0:T(8,128)(2,1)} %bitcast.33.x_ref.refs_21_, f32[1,2048]{1,0:T(1,128)} %get-tuple-element.35.gain_ref, bf16[2,4,2048,1024]{3,2,1,0:T(8,128)(2,1)} %bitcast.75, bf16[2,4,2048,1024]{3,2,1,0:T(8,128)(2,1)} %bitcast.76, ...), custom_call_target="tpu_custom_call", output_to_operand_aliasing={{}: (4, {})} | custom-call | flops 34359738368 | bytes 37748736 | tf_op jit(solution)/shard_map/pallas_call | solution.py:235
  1255.3 42.9 %shard_map.129.refs_0_.refs_1_.refs_2_.refs_3_ = bf16[2048,4096]{1,0:T(8,128)(2,1)} custom-call(bf16[1024,2048]{1,0:T(8,128)(2,1)} %bitcast.33.x_ref.refs_21_, f32[1,2048]{1,0:T(1,128)} %get-tuple-element.35.gain_ref, bf16[2,4,2048,1024]{3,2,1,0:T(8,128)(2,1)} %bitcast.79, bf16[2,4,2048,1024]{3,2,1,0:T(8,128)(2,1)} %bitcast.80, ...), custom_call_target="tpu_custom_call", output_to_operand_aliasing={{}: (4, {})} | custom-call | flops 34359738368 | bytes 37748736 | tf_op jit(solution)/shard_map/pallas_call | solution.py:235
  1298.2 108.3 %down_last.1 = bf16[4,2,256,2048]{3,2,1,0:T(8,128)(2,1)} custom-call(s32[2]{0:T(128)} %pad_add_fusion.place_ref, bf16[2048,4096]{1,0:T(8,128)(2,1)} %shard_map.129.refs_0_.refs_1_.refs_2_.refs_3_, bf16[2048,4096]{1,0:T(8,128)(2,1)} %shard_map.129.refs_0_.refs_1_.refs_2_.refs_3_, bf16[2048,4096]{1,0:T(8,128)(2,1)} %shard_map.129.refs_0_.refs_1_.refs_2_.refs_3_, ...), custom_call_target="tpu_custom_call" | custom-call | flops 68719476736 | bytes 67108864 | tf_op jit(solution)/shard_map/down_last/pallas_call | solution.py:375
  (76 shorter events, 21.7 us)
Async XLA Ops:
  6.5 1.8 copy-start.1
  6.5 399.7 %all-gather.19.cloned.1.call-start = ((), (), s32[]{:S(2)}) async-start(), calls=%async_computation.5 | async-start | bytes 14155776 | tf_op jit(solution)/shard_map/all_gather | solution.py:397
  6.5 1.8 copy-start.2
  10.4 519.8 %all-gather.21.cloned.1.call-start = ((), (), s32[]{:S(2)}) async-start(), calls=%async_computation.6 | async-start | bytes 47185920 | tf_op jit(solution)/shard_map/all_gather | solution.py:397
  36.3 599.4 %all-gather.23.cloned.1.call-start = ((), (), s32[]{:S(2)}) async-start(), calls=%async_computation.7 | async-start | bytes 37748736 | tf_op jit(solution)/shard_map/all_gather | solution.py:397
  41.0 776.0 %all-gather.25.cloned.1.call-start = ((), (), s32[]{:S(2)}) async-start(), calls=%async_computation.8 | async-start | bytes 14155776 | tf_op jit(solution)/shard_map/all_gather | solution.py:397
  43.4 856.7 %all-gather.15.cloned.1.call-start = ((), (), s32[]{:S(2)}) async-start(), calls=%async_computation.3 | async-start | bytes 9437184 | tf_op jit(solution)/shard_map/all_gather | solution.py:397
  44.0 958.1 %all-gather.29.cloned.1.call-start = ((), (), s32[]{:S(2)}) async-start(), calls=%async_computation.10 | async-start | bytes 37748736 | tf_op jit(solution)/shard_map/all_gather | solution.py:397
  48.9 1120.8 %all-gather.27.cloned.1.call-start = ((), (), s32[]{:S(2)}) async-start(), calls=%async_computation.9 | async-start | bytes 37748736 | tf_op jit(solution)/shard_map/all_gather | solution.py:397
  57.8 166.3 %collective-permute-start.2 = (bf16[2048,1024]{1,0:T(8,128)(2,1)}, bf16[2048,1024]{1,0:T(8,128)(2,1)}, u32[]{:S(2)}, u32[]{:S(2)}) collective-permute-start(bf16[2048,1024]{1,0:T(8,128)(2,1)} %slice_bitcast_fusion.refs_8_), channel_id=1, source_target_pairs={{0,2},{1,3},{2,0},{3,1},{4,6},{5,7},{6,4},{7,5}} | collective-permute-start | bytes 12582920 | tf_op jit(solution)/shard_map/ppermute | solution.py:404
  61.3 344.9 %all-to-all-start = ((bf16[8,256,2048]{2,1,0:T(8,128)(2,1)}), bf16[8,256,2048]{2,1,0:T(8,128)(2,1)}, u32[]{:S(2)}, u32[]{:S(2)}) async-start(bf16[8,256,2048]{2,1,0:T(8,128)(2,1)} %param.12), calls=%async_computation | async-start | bytes 16777216 | tf_op jit(solution)/shard_map/all_to_all | solution.py:401
  67.0 165.9 %copy-start = (f32[1024,32]{0,1:T(8,128)S(1)}, f32[1024,32]{0,1:T(8,128)}, u32[]{:S(2)}) copy-start(f32[1024,32]{0,1:T(8,128)} %param.16) | copy-start | bytes 393220
  67.0 1231.2 %all-gather.17.cloned.1.call-start = ((), (), s32[]{:S(2)}) async-start(), calls=%async_computation.4 | async-start | bytes 18874368 | tf_op jit(solution)/shard_map/all_gather | solution.py:397
  67.2 169.9 %collective-permute-start = (bf16[2048,1024]{1,0:T(8,128)(2,1)}, bf16[2048,1024]{1,0:T(8,128)(2,1)}, u32[]{:S(2)}, u32[]{:S(2)}) collective-permute-start(bf16[2048,1024]{1,0:T(8,128)(2,1)} %slice_bitcast_fusion.refs_8_), channel_id=1, source_target_pairs={{0,4},{4,0},{1,5},{5,1},{2,6},{6,2},{3,7},{7,3}} | collective-permute-start | bytes 12582920 | tf_op jit(solution)/shard_map/ppermute | solution.py:404
  224.1 182.1 %collective-permute-start.3 = (bf16[2048,1024]{1,0:T(8,128)(2,1)}, bf16[2048,1024]{1,0:T(8,128)(2,1)}, u32[]{:S(2)}, u32[]{:S(2)}) collective-permute-start(bf16[2048,1024]{1,0:T(8,128)(2,1)} %collective-permute-done.2.refs_10_), channel_id=1, source_target_pairs={{0,4},{4,0},{1,5},{5,1},{2,6},{6,2},{3,7},{7,3}} | collective-permute-start | bytes 12582920 | tf_op jit(solution)/shard_map/ppermute | solution.py:404
  225.8 493.3 %collective-permute-start.5 = (bf16[2048,1024]{1,0:T(8,128)(2,1)}, bf16[2048,1024]{1,0:T(8,128)(2,1)}, u32[]{:S(2)}, u32[]{:S(2)}) collective-permute-start(bf16[2048,1024]{1,0:T(8,128)(2,1)} %slice_bitcast_fusion.refs_8_), channel_id=1, source_target_pairs={{0,1},{1,0},{2,3},{3,2},{4,5},{5,4},{6,7},{7,6}} | collective-permute-start | bytes 12582920 | tf_op jit(solution)/shard_map/ppermute | solution.py:404
  232.3 1.7 copy-start.3
  232.3 3.3 copy-start.4
  232.3 3.9 copy-start.5
  232.3 484.6 %collective-permute-start.8 = (bf16[2048,512]{1,0:T(8,128)(2,1)}, bf16[2048,512]{1,0:T(8,128)(2,1)}, u32[]{:S(2)}, u32[]{:S(2)}) collective-permute-start(bf16[2048,512]{1,0:T(8,128)(2,1)} %get-tuple-element.18.refs_8_), channel_id=1, source_target_pairs={{0,2},{1,3},{2,0},{3,1},{4,6},{5,7},{6,4},{7,5}} | collective-permute-start | bytes 6291464 | tf_op jit(solution)/shard_map/ppermute | solution.py:404
  236.8 482.3 %collective-permute-start.6 = (bf16[2048,1024]{1,0:T(8,128)(2,1)}, bf16[2048,1024]{1,0:T(8,128)(2,1)}, u32[]{:S(2)}, u32[]{:S(2)}) collective-permute-start(bf16[2048,1024]{1,0:T(8,128)(2,1)} %collective-permute-done.2.refs_10_), channel_id=1, source_target_pairs={{0,1},{1,0},{2,3},{3,2},{4,5},{5,4},{6,7},{7,6}} | collective-permute-start | bytes 12582920 | tf_op jit(solution)/shard_map/ppermute | solution.py:404
  237.1 531.0 %collective-permute-start.1 = (bf16[2048,1024]{1,0:T(8,128)(2,1)}, bf16[2048,1024]{1,0:T(8,128)(2,1)}, u32[]{:S(2)}, u32[]{:S(2)}) collective-permute-start(bf16[2048,1024]{1,0:T(8,128)(2,1)} %collective-permute-done.refs_8_), channel_id=1, source_target_pairs={{0,1},{1,0},{2,3},{3,2},{4,5},{5,4},{6,7},{7,6}} | collective-permute-start | bytes 12582920 | tf_op jit(solution)/shard_map/ppermute | solution.py:404
  406.2 361.9 %collective-permute-start.4 = (bf16[2048,1024]{1,0:T(8,128)(2,1)}, bf16[2048,1024]{1,0:T(8,128)(2,1)}, u32[]{:S(2)}, u32[]{:S(2)}) collective-permute-start(bf16[2048,1024]{1,0:T(8,128)(2,1)} %collective-permute-done.3.refs_10_), channel_id=1, source_target_pairs={{0,1},{1,0},{2,3},{3,2},{4,5},{5,4},{6,7},{7,6}} | collective-permute-start | bytes 12582920 | tf_op jit(solution)/shard_map/ppermute | solution.py:404
  716.9 202.7 %collective-permute-start.10 = (bf16[2048,512]{1,0:T(8,128)(2,1)}, bf16[2048,512]{1,0:T(8,128)(2,1)}, u32[]{:S(2)}, u32[]{:S(2)}) collective-permute-start(bf16[2048,512]{1,0:T(8,128)(2,1)} %get-tuple-element.18.refs_8_), channel_id=1, source_target_pairs={{0,4},{4,0},{1,5},{5,1},{2,6},{6,2},{3,7},{7,3}} | collective-permute-start | bytes 6291464 | tf_op jit(solution)/shard_map/ppermute | solution.py:404
  719.1 201.0 %collective-permute-start.12 = (bf16[2048,512]{1,0:T(8,128)(2,1)}, bf16[2048,512]{1,0:T(8,128)(2,1)}, u32[]{:S(2)}, u32[]{:S(2)}) collective-permute-start(bf16[2048,512]{1,0:T(8,128)(2,1)} %collective-permute-done.8.refs_10_), channel_id=1, source_target_pairs={{0,4},{4,0},{1,5},{5,1},{2,6},{6,2},{3,7},{7,3}} | collective-permute-start | bytes 6291464 | tf_op jit(solution)/shard_map/ppermute | solution.py:404
  913.9 82.9 %all-to-all-start.2 = ((bf16[4,256,2048]{2,1,0:T(8,128)(2,1)}), bf16[4,256,2048]{2,1,0:T(8,128)(2,1)}, u32[]{:S(2)}, u32[]{:S(2)}) async-start(bf16[4,256,2048]{2,1,0:T(8,128)(2,1)} %bitcast.69), calls=%async_computation.2 | async-start | bytes 8388608 | tf_op jit(solution)/shard_map/all_to_all | solution.py:401
  919.0 379.2 %collective-permute-start.7 = (bf16[2048,512]{1,0:T(8,128)(2,1)}, bf16[2048,512]{1,0:T(8,128)(2,1)}, u32[]{:S(2)}, u32[]{:S(2)}) collective-permute-start(bf16[2048,512]{1,0:T(8,128)(2,1)} %get-tuple-element.18.refs_8_), channel_id=1, source_target_pairs={{0,1},{1,0},{2,3},{3,2},{4,5},{5,4},{6,7},{7,6}} | collective-permute-start | bytes 6291464 | tf_op jit(solution)/shard_map/ppermute | solution.py:404
  919.5 378.7 %collective-permute-start.9 = (bf16[2048,512]{1,0:T(8,128)(2,1)}, bf16[2048,512]{1,0:T(8,128)(2,1)}, u32[]{:S(2)}, u32[]{:S(2)}) collective-permute-start(bf16[2048,512]{1,0:T(8,128)(2,1)} %collective-permute-done.8.refs_10_), channel_id=1, source_target_pairs={{0,1},{1,0},{2,3},{3,2},{4,5},{5,4},{6,7},{7,6}} | collective-permute-start | bytes 6291464 | tf_op jit(solution)/shard_map/ppermute | solution.py:404
  919.5 378.6 %collective-permute-start.11 = (bf16[2048,512]{1,0:T(8,128)(2,1)}, bf16[2048,512]{1,0:T(8,128)(2,1)}, u32[]{:S(2)}, u32[]{:S(2)}) collective-permute-start(bf16[2048,512]{1,0:T(8,128)(2,1)} %collective-permute-done.10.refs_12_), channel_id=1, source_target_pairs={{0,1},{1,0},{2,3},{3,2},{4,5},{5,4},{6,7},{7,6}} | collective-permute-start | bytes 6291464 | tf_op jit(solution)/shard_map/ppermute | solution.py:404
  920.0 378.2 %collective-permute-start.13 = (bf16[2048,512]{1,0:T(8,128)(2,1)}, bf16[2048,512]{1,0:T(8,128)(2,1)}, u32[]{:S(2)}, u32[]{:S(2)}) collective-permute-start(bf16[2048,512]{1,0:T(8,128)(2,1)} %collective-permute-done.12.refs_14_), channel_id=1, source_target_pairs={{0,1},{1,0},{2,3},{3,2},{4,5},{5,4},{6,7},{7,6}} | collective-permute-start | bytes 6291464 | tf_op jit(solution)/shard_map/ppermute | solution.py:404
  996.7 215.7 %all-to-all-start.1 = ((bf16[4,256,2048]{2,1,0:T(8,128)(2,1)}), bf16[4,256,2048]{2,1,0:T(8,128)(2,1)}, u32[]{:S(2)}, u32[]{:S(2)}) async-start(bf16[4,256,2048]{2,1,0:T(8,128)(2,1)} %bitcast.70), calls=%async_computation.1 | async-start | bytes 8388608 | tf_op jit(solution)/shard_map/all_to_all | solution.py:401
Sparse Core Ops, SparseCore 0:
  10.5 84.2 all-gather.18
  96.7 357.7 all-gather.20
  456.3 157.7 all-gather.22
  615.8 66.4 all-gather.24
  683.9 59.0 all-gather.14
  744.7 221.0 all-gather.28
  967.6 202.0 all-gather.26
  1171.5 84.1 all-gather.16

commit v6 on v5

--- a/solution.py
+++ b/solution.py
@@ -204,13 +204,14 @@
     def _():
         normalise(x_ref, gain_ref, h_ref, 128)
 
-    depth = wg_ref.shape[0] * wg_ref.shape[2]
-    wg = wg_ref[...].reshape(depth, wg_ref.shape[3])
-    wu = wu_ref[...].reshape(depth, wu_ref.shape[3])
+    depth = wg_ref.shape[2]
+
+    def project(rows, w_ref):
+        return functools.reduce(jnp.add, [dot(h_ref[rows, y * depth:(y + 1) * depth], w_ref[y, 0]) for y in range(w_ref.shape[0])])
+
     for r in range(0, h_ref.shape[0], chunk):
-        h = h_ref[r:r + chunk, :]
-        gate = dot(h, wg)
-        up = dot(h, wu)
+        gate = project(slice(r, r + chunk), wg_ref)
+        up = project(slice(r, r + chunk), wu_ref)
         z_ref[r:r + chunk, :] = (gate * jax.nn.sigmoid(gate) * up).astype(BF16)
 
 
@@ -245,18 +246,21 @@
     )(*operands)
 
 
+def down_dot(za, zb, ws, rows):
+    half = za[0].shape[1]
+    terms = [dot(z[rows, :], w[h * half:(h + 1) * half, :]) for h, zs in enumerate((za, zb)) for z, w in zip(zs, ws)]
+    return functools.reduce(jnp.add, terms)
+
+
 def down_kernel(place_ref, *refs, count, resids, steps, chunk):
     za, zb, ws = refs[:count], refs[count:2 * count], refs[2 * count:3 * count]
     r_refs, o_ref = refs[3 * count:3 * count + resids], refs[-1]
-    half = za[0].shape[1]
-    w = jnp.concatenate([w[h * half:(h + 1) * half, :] for h in range(2) for w in ws], axis=0)
     for r in range(0, za[0].shape[0], chunk):
         rows = slice(r, r + chunk)
-        z = jnp.concatenate([z[rows, :] for z in za + zb], axis=1)
         resid = r_refs[0][rows, :].astype(F32)
         if resids == 2:
             resid = jnp.where(pl.program_id(0) < steps, resid, r_refs[1][rows, :].astype(F32))
-        out = (resid + dot(z, w)).astype(BF16)
+        out = (resid + down_dot(za, zb, ws, rows)).astype(BF16)
         if len(o_ref.shape) == 4:
             positions = o_ref.shape[2]
             o_ref[r // positions:(r + chunk) // positions, 0] = out.reshape(chunk // positions, positions, out.shape[1])
@@ -325,15 +329,12 @@
     za, zb = refs[:count], refs[count:2 * count]
     groups = [refs[(2 + g) * count:(3 + g) * count] for g in range(3)]
     r_refs, o_ref = refs[5 * count:5 * count + 2], refs[-1]
-    half = za[0].shape[1]
     step = pl.program_id(0) % steps
     first = pl.program_id(0) < 2 * steps
 
     def run(ws):
-        w = jnp.concatenate([w[h * half:(h + 1) * half, :] for h in range(2) for w in ws], axis=0)
-        z = jnp.concatenate([z[...] for z in za + zb], axis=1)
         resid = jnp.where(first, r_refs[0][...].astype(F32), r_refs[1][...].astype(F32))
-        out = (resid + dot(z, w)).astype(BF16)
+        out = (resid + down_dot(za, zb, ws, slice(None))).astype(BF16)
         o_ref[...] = out.reshape(o_ref.shape)
 
     for g, here in enumerate((step < 2, jnp.logical_and(step >= 2, step < 4), step >= 4)):

time: 1420 us -> 1420 us (level)
  no operation moved by 1% of the time
where the time goes in v6:
time: 1420 us; the launch traced here: 1410 us
  Pallas kernels  844 us (59%)
  waiting for transfers between devices  468 us (33%)
  local copies, waits for them, and re-layouts  31.8 us (2%)
  other arithmetic  28.9 us (2%)
  starting transfers between devices  27.8 us (2%)
    pallas_call x6, Pallas kernels, gate_up(): pl.pallas_call(functools.partial(gate_up_kernel, chunk=512), grid=(ms * p...  333 us
    ppermute x14, waiting for transfers between devices, swap(): lax.ppermute(block, axis, [(i, i ^ bit) for i in range(mesh.shape[axis])])  324 us
    pallas_call x3, Pallas kernels, attend(): pl.pallas_call(attention_kernel, grid=(count * blocks,), in_specs=[pl.Blo...  176 us
    all_gather x8, waiting for transfers between devices, gather(): full = lax.all_gather(block, ('fsdp', 'model'), axis=0, tiled=False)  125 us
    pallas_call x1, Pallas kernels, down_last(): pl.pallas_call(functools.partial(down_last_kernel, count=count, steps=ste...  108 us
    pallas_call x2, Pallas kernels, down(): pl.pallas_call(functools.partial(down_kernel, count=count, resids=len(res...  97.9 us
    pallas_call x2, Pallas kernels, project_qkv(): pl.pallas_call(qkv_kernel, grid=(blocks,), in_specs=[pl.BlockSpec((tokens...  75.8 us
    pallas_call x3, Pallas kernels, out_proj(): pl.pallas_call(functools.partial(out_proj_kernel, chunk=512), grid=(ys *...  52.7 us
  transfers between devices with their start and end apart: 25, of which 4 were waited for; matrix products, arithmetic and copies ran while one was open for 4% of the time, Pallas kernels for 52%

profile of v6, /device:TPU:0, one launch (start us, length us, event | category | flops | bytes accessed | tf_op | source)
XLA Modules:
  0.0 1413.6 jit_solution(14656162833893952197)
XLA Ops:
  13.2 11.8 slice_bitcast_fusion.2
  25.0 11.2 pad_maximum_fusion
  36.3 4.7 pad_maximum_fusion.1
  44.1 4.8 pad_maximum_fusion.3
  48.9 4.0 pad_maximum_fusion.2
  53.0 4.8 slice_bitcast_fusion.refs_8_
  57.8 3.5 collective-permute-start.2
  61.3 5.6 all-to-all-start
  69.0 155.2 %collective-permute-done.2.refs_10_ = bf16[2048,1024]{1,0:T(8,128)(2,1)} collective-permute-done((bf16[2048,1024]{1,0:T(8,128)(2,1)}, bf16[2048,1024]{1,0:T(8,128)(2,1)}, u32[]{:S(2)}, u32[]{:S(2)}) %collective-permute-start.2) | collective-permute-done | bytes 4194336 | tf_op jit(solution)/shard_map/ppermute | solution.py:405
  225.8 6.5 fusion
  237.3 168.9 %collective-permute-done.3.refs_10_ = bf16[2048,1024]{1,0:T(8,128)(2,1)} collective-permute-done((bf16[2048,1024]{1,0:T(8,128)(2,1)}, bf16[2048,1024]{1,0:T(8,128)(2,1)}, u32[]{:S(2)}, u32[]{:S(2)}) %collective-permute-start.3) | collective-permute-done | bytes 4194336 | tf_op jit(solution)/shard_map/ppermute | solution.py:405
  406.2 37.7 %qkv.2 = (bf16[2048,2048]{1,0:T(8,128)(2,1)}, bf16[2048,512]{1,0:T(8,128)(2,1)}, bf16[2048,512]{1,0:T(8,128)(2,1)}) custom-call(bf16[2048,2048]{1,0:T(8,128)(2,1)} %bitcast.2.x_ref, f32[1,2048]{1,0:T(1,128)} %get-tuple-element.38.gain_ref, f32[1024,128]{1,0:T(8,128)} %copy.22.cos_ref, f32[1024,128]{1,0:T(8,128)} %copy.23.sin_ref, ...), custom_call_target="tpu_custom_call" | custom-call | flops 25769803776 | bytes 29360128 | tf_op jit(solution)/shard_map/qkv/pallas_call | solution.py:70
  443.9 86.2 %shard_map.118 = bf16[4,2,256,2048]{3,2,1,0:T(8,128)(2,1)} custom-call(bf16[4,2,256,2048]{3,2,1,0:T(8,128)(2,1)} %bitcast.93, bf16[4,2,256,512]{3,2,1,0:T(8,128)(2,1)} %bitcast.100, bf16[4,2,256,512]{3,2,1,0:T(8,128)(2,1)} %bitcast.101), custom_call_target="tpu_custom_call" | custom-call | flops 34359738368 | bytes 20971520 | tf_op jit(solution)/shard_map/pallas_call | solution.py:150
  530.2 24.5 %shard_map.119.x_ref.refs_12_ = bf16[2048,2048]{1,0:T(8,128)(2,1)} custom-call(bf16[2048,2048]{1,0:T(8,128)(2,1)} %bitcast.68, bf16[2,4,2560,1024]{3,2,1,0:T(8,128)(2,1)} %bitcast.63, bf16[4,2,256,2048]{3,2,1,0:T(8,128)(2,1)} %bitcast.17.r_ref), custom_call_target="tpu_custom_call" | custom-call | flops 17179869184 | bytes 33554432 | tf_op jit(solution)/shard_map/pallas_call | solution.py:185
  554.7 80.9 %shard_map.120.refs_0_.refs_1_.refs_2_.refs_3_ = bf16[2048,4096]{1,0:T(8,128)(2,1)} custom-call(bf16[2048,2048]{1,0:T(8,128)(2,1)} %shard_map.119.x_ref.refs_12_, f32[1,2048]{1,0:T(1,128)} %get-tuple-element.36.gain_ref, bf16[2,4,2560,1024]{3,2,1,0:T(8,128)(2,1)} %bitcast.64, bf16[2,4,2560,1024]{3,2,1,0:T(8,128)(2,1)} %bitcast.65), custom_call_target="tpu_custom_call" | custom-call | flops 68719476736 | bytes 41943040 | tf_op jit(solution)/shard_map/pallas_call | solution.py:236
  635.6 81.2 %shard_map.121.refs_4_.refs_5_.refs_6_.refs_7_ = bf16[2048,4096]{1,0:T(8,128)(2,1)} custom-call(bf16[2048,2048]{1,0:T(8,128)(2,1)} %shard_map.119.x_ref.refs_12_, f32[1,2048]{1,0:T(1,128)} %get-tuple-element.36.gain_ref, bf16[2,4,2048,1024]{3,2,1,0:T(8,128)(2,1)} %bitcast.81, bf16[2,4,2048,1024]{3,2,1,0:T(8,128)(2,1)} %bitcast.82), custom_call_target="tpu_custom_call" | custom-call | flops 68719476736 | bytes 41943040 | tf_op jit(solution)/shard_map/pallas_call | solution.py:236
  719.1 49.0 %shard_map.122.refs_13_ = bf16[2048,2048]{1,0:T(8,128)(2,1)} custom-call(s32[2]{0:T(128)} %pad_add_fusion.place_ref, bf16[2048,4096]{1,0:T(8,128)(2,1)} %shard_map.120.refs_0_.refs_1_.refs_2_.refs_3_, bf16[2048,4096]{1,0:T(8,128)(2,1)} %shard_map.120.refs_0_.refs_1_.refs_2_.refs_3_, bf16[2048,4096]{1,0:T(8,128)(2,1)} %shard_map.120.refs_0_.refs_1_.refs_2_.refs_3_, ...), custom_call_target="tpu_custom_call" | custom-call | flops 34359738368 | bytes 50331648 | tf_op jit(solution)/shard_map/pallas_call | solution.py:313
  768.1 48.9 %shard_map.123.x_ref = bf16[2048,2048]{1,0:T(8,128)(2,1)} custom-call(s32[2]{0:T(128)} %pad_add_fusion.place_ref, bf16[2048,4096]{1,0:T(8,128)(2,1)} %shard_map.120.refs_0_.refs_1_.refs_2_.refs_3_, bf16[2048,4096]{1,0:T(8,128)(2,1)} %shard_map.120.refs_0_.refs_1_.refs_2_.refs_3_, ...), custom_call_target="tpu_custom_call", output_to_operand_aliasing={{}: (14, {})} | custom-call | flops 34359738368 | bytes 50331648 | tf_op jit(solution)/shard_map/pallas_call | solution.py:313
  817.0 38.1 %qkv.3 = (bf16[2048,2048]{1,0:T(8,128)(2,1)}, bf16[2048,512]{1,0:T(8,128)(2,1)}, bf16[2048,512]{1,0:T(8,128)(2,1)}) custom-call(bf16[2048,2048]{1,0:T(8,128)(2,1)} %shard_map.123.x_ref, f32[1,2048]{1,0:T(1,128)} %get-tuple-element.37.gain_ref, f32[1024,128]{1,0:T(8,128)} %copy.22.cos_ref, f32[1024,128]{1,0:T(8,128)} %copy.23.sin_ref, ...), custom_call_target="tpu_custom_call" | custom-call | flops 25769803776 | bytes 29360128 | tf_op jit(solution)/shard_map/qkv/pallas_call | solution.py:70
  855.1 45.0 %shard_map.126 = bf16[4,1,256,2048]{3,2,1,0:T(8,128)(2,1)} custom-call(bf16[4,2,256,2048]{3,2,1,0:T(8,128)(2,1)} %bitcast.91, bf16[4,2,256,512]{3,2,1,0:T(8,128)(2,1)} %bitcast.96, bf16[4,2,256,512]{3,2,1,0:T(8,128)(2,1)} %bitcast.98), custom_call_target="tpu_custom_call" | custom-call | flops 17179869184 | bytes 10485760 | tf_op jit(solution)/shard_map/pallas_call | solution.py:150
  900.1 13.7 shard_map.127
  913.8 5.1 all-to-all-start.2
  920.0 44.3 %shard_map.124 = bf16[4,1,256,2048]{3,2,1,0:T(8,128)(2,1)} custom-call(bf16[4,2,256,2048]{3,2,1,0:T(8,128)(2,1)} %bitcast.92, bf16[4,2,256,512]{3,2,1,0:T(8,128)(2,1)} %bitcast.97, bf16[4,2,256,512]{3,2,1,0:T(8,128)(2,1)} %bitcast.99), custom_call_target="tpu_custom_call" | custom-call | flops 17179869184 | bytes 10485760 | tf_op jit(solution)/shard_map/pallas_call | solution.py:150
  964.3 14.4 %shard_map.125 = bf16[1024,2048]{1,0:T(8,128)(2,1)} custom-call(bf16[1024,2048]{1,0:T(8,128)(2,1)} %bitcast.94, bf16[2,4,512,1024]{3,2,1,0:T(8,128)(2,1)} %bitcast.90, bf16[4,2,256,2048]{3,2,1,0:T(8,128)(2,1)} %bitcast.67), custom_call_target="tpu_custom_call" | custom-call | flops 8589934592 | bytes 20971520 | tf_op jit(solution)/shard_map/pallas_call | solution.py:185
  978.7 17.9 %all-to-all-done.2 = bf16[4,256,2048]{2,1,0:T(8,128)(2,1)} async-done(((bf16[4,256,2048]{2,1,0:T(8,128)(2,1)}), bf16[4,256,2048]{2,1,0:T(8,128)(2,1)}, u32[]{:S(2)}, u32[]{:S(2)}) %all-to-all-start.2) | async-done | bytes 4194336 | tf_op jit(solution)/shard_map/all_to_all | solution.py:402
  996.7 5.3 all-to-all-start.1
  1002.1 42.7 %shard_map.130.refs_0_ = bf16[2048,4096]{1,0:T(8,128)(2,1)} custom-call(bf16[1024,2048]{1,0:T(8,128)(2,1)} %bitcast.39.x_ref.refs_20_, f32[1,2048]{1,0:T(1,128)} %get-tuple-element.35.gain_ref, bf16[2,4,2048,1024]{3,2,1,0:T(8,128)(2,1)} %bitcast.73, bf16[2,4,2048,1024]{3,2,1,0:T(8,128)(2,1)} %bitcast.74), custom_call_target="tpu_custom_call" | custom-call | flops 34359738368 | bytes 37748736 | tf_op jit(solution)/shard_map/pallas_call | solution.py:236
  1044.8 125.0 %all-gather.27.cloned.1.call-done = bf16[16384,1024]{1,0:T(8,128)(2,1)} async-done(((bf16[2048,1024]{1,0:T(8,128)(2,1)}), bf16[16384,1024]{1,0:T(8,128)(2,1)}) %all-gather.27.cloned.1.call-update) | async-done | bytes 33554448 | tf_op jit(solution)/shard_map/all_gather | solution.py:398
  1169.8 42.7 %shard_map.128.refs_0_ = bf16[2048,4096]{1,0:T(8,128)(2,1)} custom-call(bf16[1024,2048]{1,0:T(8,128)(2,1)} %bitcast.39.x_ref.refs_20_, f32[1,2048]{1,0:T(1,128)} %get-tuple-element.35.gain_ref, bf16[2,4,2048,1024]{3,2,1,0:T(8,128)(2,1)} %bitcast.77, bf16[2,4,2048,1024]{3,2,1,0:T(8,128)(2,1)} %bitcast.78), custom_call_target="tpu_custom_call" | custom-call | flops 34359738368 | bytes 37748736 | tf_op jit(solution)/shard_map/pallas_call | solution.py:236
  1212.5 42.8 %shard_map.131.refs_4_.refs_5_.refs_6_.refs_7_ = bf16[2048,4096]{1,0:T(8,128)(2,1)} custom-call(bf16[1024,2048]{1,0:T(8,128)(2,1)} %bitcast.33.x_ref.refs_21_, f32[1,2048]{1,0:T(1,128)} %get-tuple-element.35.gain_ref, bf16[2,4,2048,1024]{3,2,1,0:T(8,128)(2,1)} %bitcast.75, bf16[2,4,2048,1024]{3,2,1,0:T(8,128)(2,1)} %bitcast.76, ...), custom_call_target="tpu_custom_call", output_to_operand_aliasing={{}: (4, {})} | custom-call | flops 34359738368 | bytes 37748736 | tf_op jit(solution)/shard_map/pallas_call | solution.py:236
  1255.3 42.9 %shard_map.129.refs_0_.refs_1_.refs_2_.refs_3_ = bf16[2048,4096]{1,0:T(8,128)(2,1)} custom-call(bf16[1024,2048]{1,0:T(8,128)(2,1)} %bitcast.33.x_ref.refs_21_, f32[1,2048]{1,0:T(1,128)} %get-tuple-element.35.gain_ref, bf16[2,4,2048,1024]{3,2,1,0:T(8,128)(2,1)} %bitcast.79, bf16[2,4,2048,1024]{3,2,1,0:T(8,128)(2,1)} %bitcast.80, ...), custom_call_target="tpu_custom_call", output_to_operand_aliasing={{}: (4, {})} | custom-call | flops 34359738368 | bytes 37748736 | tf_op jit(solution)/shard_map/pallas_call | solution.py:236
  1298.3 108.3 %down_last.1 = bf16[4,2,256,2048]{3,2,1,0:T(8,128)(2,1)} custom-call(s32[2]{0:T(128)} %pad_add_fusion.place_ref, bf16[2048,4096]{1,0:T(8,128)(2,1)} %shard_map.129.refs_0_.refs_1_.refs_2_.refs_3_, bf16[2048,4096]{1,0:T(8,128)(2,1)} %shard_map.129.refs_0_.refs_1_.refs_2_.refs_3_, bf16[2048,4096]{1,0:T(8,128)(2,1)} %shard_map.129.refs_0_.refs_1_.refs_2_.refs_3_, ...), custom_call_target="tpu_custom_call" | custom-call | flops 68719476736 | bytes 67108864 | tf_op jit(solution)/shard_map/down_last/pallas_call | solution.py:376
  (76 shorter events, 21.7 us)
Async XLA Ops:
  6.5 1.8 copy-start.1
  6.5 399.7 %all-gather.19.cloned.1.call-start = ((), (), s32[]{:S(2)}) async-start(), calls=%async_computation.5 | async-start | bytes 14155776 | tf_op jit(solution)/shard_map/all_gather | solution.py:398
  6.5 1.8 copy-start.2
  10.4 519.8 %all-gather.21.cloned.1.call-start = ((), (), s32[]{:S(2)}) async-start(), calls=%async_computation.6 | async-start | bytes 47185920 | tf_op jit(solution)/shard_map/all_gather | solution.py:398
  36.3 599.4 %all-gather.23.cloned.1.call-start = ((), (), s32[]{:S(2)}) async-start(), calls=%async_computation.7 | async-start | bytes 37748736 | tf_op jit(solution)/shard_map/all_gather | solution.py:398
  41.0 776.0 %all-gather.25.cloned.1.call-start = ((), (), s32[]{:S(2)}) async-start(), calls=%async_computation.8 | async-start | bytes 14155776 | tf_op jit(solution)/shard_map/all_gather | solution.py:398
  43.4 856.7 %all-gather.15.cloned.1.call-start = ((), (), s32[]{:S(2)}) async-start(), calls=%async_computation.3 | async-start | bytes 9437184 | tf_op jit(solution)/shard_map/all_gather | solution.py:398
  44.0 958.0 %all-gather.29.cloned.1.call-start = ((), (), s32[]{:S(2)}) async-start(), calls=%async_computation.10 | async-start | bytes 37748736 | tf_op jit(solution)/shard_map/all_gather | solution.py:398
  48.9 1120.9 %all-gather.27.cloned.1.call-start = ((), (), s32[]{:S(2)}) async-start(), calls=%async_computation.9 | async-start | bytes 37748736 | tf_op jit(solution)/shard_map/all_gather | solution.py:398
  57.8 166.3 %collective-permute-start.2 = (bf16[2048,1024]{1,0:T(8,128)(2,1)}, bf16[2048,1024]{1,0:T(8,128)(2,1)}, u32[]{:S(2)}, u32[]{:S(2)}) collective-permute-start(bf16[2048,1024]{1,0:T(8,128)(2,1)} %slice_bitcast_fusion.refs_8_), channel_id=1, source_target_pairs={{0,2},{1,3},{2,0},{3,1},{4,6},{5,7},{6,4},{7,5}} | collective-permute-start | bytes 12582920 | tf_op jit(solution)/shard_map/ppermute | solution.py:405
  61.3 344.9 %all-to-all-start = ((bf16[8,256,2048]{2,1,0:T(8,128)(2,1)}), bf16[8,256,2048]{2,1,0:T(8,128)(2,1)}, u32[]{:S(2)}, u32[]{:S(2)}) async-start(bf16[8,256,2048]{2,1,0:T(8,128)(2,1)} %param.12), calls=%async_computation | async-start | bytes 16777216 | tf_op jit(solution)/shard_map/all_to_all | solution.py:402
  67.0 165.9 %copy-start = (f32[1024,32]{0,1:T(8,128)S(1)}, f32[1024,32]{0,1:T(8,128)}, u32[]{:S(2)}) copy-start(f32[1024,32]{0,1:T(8,128)} %param.16) | copy-start | bytes 393220
  67.0 1231.3 %all-gather.17.cloned.1.call-start = ((), (), s32[]{:S(2)}) async-start(), calls=%async_computation.4 | async-start | bytes 18874368 | tf_op jit(solution)/shard_map/all_gather | solution.py:398
  67.2 169.9 %collective-permute-start = (bf16[2048,1024]{1,0:T(8,128)(2,1)}, bf16[2048,1024]{1,0:T(8,128)(2,1)}, u32[]{:S(2)}, u32[]{:S(2)}) collective-permute-start(bf16[2048,1024]{1,0:T(8,128)(2,1)} %slice_bitcast_fusion.refs_8_), channel_id=1, source_target_pairs={{0,4},{4,0},{1,5},{5,1},{2,6},{6,2},{3,7},{7,3}} | collective-permute-start | bytes 12582920 | tf_op jit(solution)/shard_map/ppermute | solution.py:405
  224.1 182.1 %collective-permute-start.3 = (bf16[2048,1024]{1,0:T(8,128)(2,1)}, bf16[2048,1024]{1,0:T(8,128)(2,1)}, u32[]{:S(2)}, u32[]{:S(2)}) collective-permute-start(bf16[2048,1024]{1,0:T(8,128)(2,1)} %collective-permute-done.2.refs_10_), channel_id=1, source_target_pairs={{0,4},{4,0},{1,5},{5,1},{2,6},{6,2},{3,7},{7,3}} | collective-permute-start | bytes 12582920 | tf_op jit(solution)/shard_map/ppermute | solution.py:405
  225.8 493.2 %collective-permute-start.5 = (bf16[2048,1024]{1,0:T(8,128)(2,1)}, bf16[2048,1024]{1,0:T(8,128)(2,1)}, u32[]{:S(2)}, u32[]{:S(2)}) collective-permute-start(bf16[2048,1024]{1,0:T(8,128)(2,1)} %slice_bitcast_fusion.refs_8_), channel_id=1, source_target_pairs={{0,1},{1,0},{2,3},{3,2},{4,5},{5,4},{6,7},{7,6}} | collective-permute-start | bytes 12582920 | tf_op jit(solution)/shard_map/ppermute | solution.py:405
  232.3 1.7 copy-start.3
  232.3 3.3 copy-start.4
  232.3 3.9 copy-start.5
  232.3 484.5 %collective-permute-start.8 = (bf16[2048,512]{1,0:T(8,128)(2,1)}, bf16[2048,512]{1,0:T(8,128)(2,1)}, u32[]{:S(2)}, u32[]{:S(2)}) collective-permute-start(bf16[2048,512]{1,0:T(8,128)(2,1)} %get-tuple-element.18.refs_8_), channel_id=1, source_target_pairs={{0,2},{1,3},{2,0},{3,1},{4,6},{5,7},{6,4},{7,5}} | collective-permute-start | bytes 6291464 | tf_op jit(solution)/shard_map/ppermute | solution.py:405
  236.8 482.3 %collective-permute-start.6 = (bf16[2048,1024]{1,0:T(8,128)(2,1)}, bf16[2048,1024]{1,0:T(8,128)(2,1)}, u32[]{:S(2)}, u32[]{:S(2)}) collective-permute-start(bf16[2048,1024]{1,0:T(8,128)(2,1)} %collective-permute-done.2.refs_10_), channel_id=1, source_target_pairs={{0,1},{1,0},{2,3},{3,2},{4,5},{5,4},{6,7},{7,6}} | collective-permute-start | bytes 12582920 | tf_op jit(solution)/shard_map/ppermute | solution.py:405
  237.1 531.0 %collective-permute-start.1 = (bf16[2048,1024]{1,0:T(8,128)(2,1)}, bf16[2048,1024]{1,0:T(8,128)(2,1)}, u32[]{:S(2)}, u32[]{:S(2)}) collective-permute-start(bf16[2048,1024]{1,0:T(8,128)(2,1)} %collective-permute-done.refs_8_), channel_id=1, source_target_pairs={{0,1},{1,0},{2,3},{3,2},{4,5},{5,4},{6,7},{7,6}} | collective-permute-start | bytes 12582920 | tf_op jit(solution)/shard_map/ppermute | solution.py:405
  406.2 361.9 %collective-permute-start.4 = (bf16[2048,1024]{1,0:T(8,128)(2,1)}, bf16[2048,1024]{1,0:T(8,128)(2,1)}, u32[]{:S(2)}, u32[]{:S(2)}) collective-permute-start(bf16[2048,1024]{1,0:T(8,128)(2,1)} %collective-permute-done.3.refs_10_), channel_id=1, source_target_pairs={{0,1},{1,0},{2,3},{3,2},{4,5},{5,4},{6,7},{7,6}} | collective-permute-start | bytes 12582920 | tf_op jit(solution)/shard_map/ppermute | solution.py:405
  716.8 202.6 %collective-permute-start.10 = (bf16[2048,512]{1,0:T(8,128)(2,1)}, bf16[2048,512]{1,0:T(8,128)(2,1)}, u32[]{:S(2)}, u32[]{:S(2)}) collective-permute-start(bf16[2048,512]{1,0:T(8,128)(2,1)} %get-tuple-element.18.refs_8_), channel_id=1, source_target_pairs={{0,4},{4,0},{1,5},{5,1},{2,6},{6,2},{3,7},{7,3}} | collective-permute-start | bytes 6291464 | tf_op jit(solution)/shard_map/ppermute | solution.py:405
  719.0 200.9 %collective-permute-start.12 = (bf16[2048,512]{1,0:T(8,128)(2,1)}, bf16[2048,512]{1,0:T(8,128)(2,1)}, u32[]{:S(2)}, u32[]{:S(2)}) collective-permute-start(bf16[2048,512]{1,0:T(8,128)(2,1)} %collective-permute-done.8.refs_10_), channel_id=1, source_target_pairs={{0,4},{4,0},{1,5},{5,1},{2,6},{6,2},{3,7},{7,3}} | collective-permute-start | bytes 6291464 | tf_op jit(solution)/shard_map/ppermute | solution.py:405
  913.8 82.9 %all-to-all-start.2 = ((bf16[4,256,2048]{2,1,0:T(8,128)(2,1)}), bf16[4,256,2048]{2,1,0:T(8,128)(2,1)}, u32[]{:S(2)}, u32[]{:S(2)}) async-start(bf16[4,256,2048]{2,1,0:T(8,128)(2,1)} %bitcast.69), calls=%async_computation.2 | async-start | bytes 8388608 | tf_op jit(solution)/shard_map/all_to_all | solution.py:402
  919.0 379.3 %collective-permute-start.7 = (bf16[2048,512]{1,0:T(8,128)(2,1)}, bf16[2048,512]{1,0:T(8,128)(2,1)}, u32[]{:S(2)}, u32[]{:S(2)}) collective-permute-start(bf16[2048,512]{1,0:T(8,128)(2,1)} %get-tuple-element.18.refs_8_), channel_id=1, source_target_pairs={{0,1},{1,0},{2,3},{3,2},{4,5},{5,4},{6,7},{7,6}} | collective-permute-start | bytes 6291464 | tf_op jit(solution)/shard_map/ppermute | solution.py:405
  919.4 378.8 %collective-permute-start.9 = (bf16[2048,512]{1,0:T(8,128)(2,1)}, bf16[2048,512]{1,0:T(8,128)(2,1)}, u32[]{:S(2)}, u32[]{:S(2)}) collective-permute-start(bf16[2048,512]{1,0:T(8,128)(2,1)} %collective-permute-done.8.refs_10_), channel_id=1, source_target_pairs={{0,1},{1,0},{2,3},{3,2},{4,5},{5,4},{6,7},{7,6}} | collective-permute-start | bytes 6291464 | tf_op jit(solution)/shard_map/ppermute | solution.py:405
  919.5 378.7 %collective-permute-start.11 = (bf16[2048,512]{1,0:T(8,128)(2,1)}, bf16[2048,512]{1,0:T(8,128)(2,1)}, u32[]{:S(2)}, u32[]{:S(2)}) collective-permute-start(bf16[2048,512]{1,0:T(8,128)(2,1)} %collective-permute-done.10.refs_12_), channel_id=1, source_target_pairs={{0,1},{1,0},{2,3},{3,2},{4,5},{5,4},{6,7},{7,6}} | collective-permute-start | bytes 6291464 | tf_op jit(solution)/shard_map/ppermute | solution.py:405
  920.0 378.3 %collective-permute-start.13 = (bf16[2048,512]{1,0:T(8,128)(2,1)}, bf16[2048,512]{1,0:T(8,128)(2,1)}, u32[]{:S(2)}, u32[]{:S(2)}) collective-permute-start(bf16[2048,512]{1,0:T(8,128)(2,1)} %collective-permute-done.12.refs_14_), channel_id=1, source_target_pairs={{0,1},{1,0},{2,3},{3,2},{4,5},{5,4},{6,7},{7,6}} | collective-permute-start | bytes 6291464 | tf_op jit(solution)/shard_map/ppermute | solution.py:405
  996.7 215.8 %all-to-all-start.1 = ((bf16[4,256,2048]{2,1,0:T(8,128)(2,1)}), bf16[4,256,2048]{2,1,0:T(8,128)(2,1)}, u32[]{:S(2)}, u32[]{:S(2)}) async-start(bf16[4,256,2048]{2,1,0:T(8,128)(2,1)} %bitcast.70), calls=%async_computation.1 | async-start | bytes 8388608 | tf_op jit(solution)/shard_map/all_to_all | solution.py:402
Sparse Core Ops, SparseCore 0:
  10.5 84.2 all-gather.18
  96.7 357.7 all-gather.20
  456.3 157.7 all-gather.22
  615.8 66.4 all-gather.24
  683.9 59.0 all-gather.14
  744.7 221.1 all-gather.28
  967.7 201.9 all-gather.26
  1171.6 84.1 all-gather.16
